TPU v7x, 32 devices: a whole 2x2x4 slice. The times are simulated.
32 devices in a mesh: rows: 4 (over y, x), heads: 8 (over z, core).
Axes of the slice: x: 2, y: 2, z: 4, core: 2. Of those that a mesh axis runs over, the one named last changes fastest.
Arguments:
- hidden_in: bfloat16 [16384, 2048], P('rows', 'heads'), may hold values from -6 to 6
- lengths: int32 [4, 4], P('rows'), may hold values from 0 to 4096, as said below
- norm_gain: float32 [2048], P('heads'), may hold values from 0.5 to 1.5
- in_gate_inner: bfloat16 [2048, 2, 4096], P(None, None, 'heads'), may hold values from -0.125 to 0.125
- in_step: bfloat16 [2048, 64], P(None, 'heads'), may hold values from -0.25 to 0.25
- in_shared: bfloat16 [128, 2048], P(None, 'heads'), may hold values from -0.125 to 0.125
- conv_inner: float32 [4, 4096], P(None, 'heads'), may hold values from -3 to 3
- conv_inner_bias: float32 [4096], P('heads'), may hold values from -3 to 3
- conv_shared: float32 [4, 128], replicated, may hold values from -3 to 3
- conv_shared_bias: float32 [128], replicated, may hold values from -3 to 3
- step_bias: float32 [64], P('heads'), may hold values from -4 to -2
- log_decay: float32 [64], P('heads'), may hold values from -6 to 1
- skip_gain: float32 [64], P('heads'), may hold values from 0.5 to 1.5
- gate_gain: float32 [4096], P('heads'), may hold values from 0.5 to 1.5
- out_weight: bfloat16 [4096, 2048], P('heads'), may hold values from -0.09375 to 0.09375
- cotangent: bfloat16 [16384, 2048], P('rows', 'heads'), may hold values from -6 to 6
Outputs:
- output: bfloat16 [16384, 2048], P('rows', 'heads')
- grad_input: float32 [16384, 2048], P('rows', 'heads')
- grad_norm_gain: float32 [2048], P('heads')
- grad_in_gate_inner: float32 [2048, 2, 4096], P(None, None, 'heads')
- grad_in_step: float32 [2048, 64], P(None, 'heads')
- grad_in_shared: float32 [128, 2048], P(None, 'heads')
- grad_conv_inner: float32 [4, 4096], P(None, 'heads')
- grad_conv_inner_bias: float32 [4096], P('heads')
- grad_conv_shared: float32 [4, 128], replicated
- grad_conv_shared_bias: float32 [128], replicated
- grad_step_bias: float32 [64], P('heads')
- grad_log_decay: float32 [64], P('heads')
- grad_skip_gain: float32 [64], P('heads')
- grad_gate_gain: float32 [4096], P('heads')
- grad_out_weight: float32 [4096, 2048], P('heads')
Inputs may be any that keep to these rules, and one draw needn't show every extreme that they name: `lengths`: row g lists the sequences packed at the start of group g: its nonzero entries come first, each from 512 to 4096, then zeros; their sum is at most 4096 and the rest of the group is padding. In every draw one row holds a single sequence of exactly 4096 tokens.
All inputs are finite; a program needn't handle non-finite values.
Results may differ from a plain program's by a relative error of at most 0.00155.
The roundings to bfloat16 on the way count: a program that leaves them out, or rounds other values in their place, can miss the bound.
Values may be sent and summed in bfloat16 or wider, within the bound.
A program may use at most 320 MiB of HBM per device.

v0:
```python
import jax
import jax.numpy as jnp
from jax import lax
from jax.sharding import PartitionSpec as P

D = 2048
CH = 256
DI = 4096


exact_mode = lax.Precision.HIGHEST
EPSILON = 1e-05


def segment_ids(length_row, count_tokens):
    bounds = jnp.cumsum(length_row, dtype=jnp.int32)
    places = jnp.arange(count_tokens, dtype=jnp.int32)
    return jnp.sum((places[:, None] >= bounds[None, :]).astype(jnp.int32), axis=1, dtype=jnp.int32)


def conv_silu(values, kernel, biases, segment):
    kernel_width = kernel.shape[0]
    length = values.shape[0]
    padded = jnp.concatenate(
        [jnp.zeros((kernel_width - 1, values.shape[1]), jnp.float32), values], axis=0
    )
    seg_padded = jnp.concatenate([jnp.full((kernel_width - 1,), -1, jnp.int32), segment], axis=0)
    summed = jnp.zeros_like(values) + biases[None, :]
    for offset in range(kernel_width):
        same_seg = (seg_padded[offset : offset + length] == segment).astype(jnp.float32)
        summed = (
            summed + kernel[offset][None, :] * padded[offset : offset + length] * same_seg[:, None]
        )
    return jax.nn.silu(summed)


def block_step(carried_in, block):
    carry_state, last_seg = carried_in
    inner_blk, write_blk, read_blk, step_blk, decay_blk, seg_blk = block
    block_len = seg_blk.shape[0]
    cumulative = jnp.cumsum(decay_blk, axis=0).T
    places = jnp.arange(block_len)
    causal = (places[:, None] >= places[None, :]) & (seg_blk[:, None] == seg_blk[None, :])
    spread = cumulative[:, :, None] - cumulative[:, None, :]
    factor = jnp.exp(jnp.where(causal[None], spread, -10000.0))
    scores = jnp.einsum("in,jn->ij", read_blk, write_blk, precision=exact_mode)
    mixing = factor * scores[None] * step_blk.T[:, None, :]
    within = jnp.einsum("hij,jhp->ihp", mixing, inner_blk, precision=exact_mode)
    carried = (seg_blk == last_seg).astype(jnp.float32)
    entry_gain = (jnp.exp(cumulative) * carried[None, :]).T
    from_state = (
        jnp.einsum("in,hpn->ihp", read_blk, carry_state, precision=exact_mode)
        * entry_gain[:, :, None]
    )
    tail_same = (seg_blk == seg_blk[-1]).astype(jnp.float32)
    to_end = jnp.exp(cumulative[:, -1:] - cumulative).T * tail_same[:, None] * step_blk
    weighted = inner_blk * to_end[:, :, None]
    new_state = jnp.einsum("jhp,jn->hpn", weighted, write_blk, precision=exact_mode)
    new_state = new_state + carry_state * (jnp.exp(cumulative[:, -1]) * carried[-1])[:, None, None]
    return ((new_state, seg_blk[-1]), within + from_state)


def mixer(
    gate_in,
    inner_raw,
    shared,
    step_raw,
    conv_inner,
    conv_inner_bias,
    conv_shared,
    conv_shared_bias,
    step_bias,
    log_decay,
    skip_gain,
    segment,
):
    tokens = inner_raw.shape[0]
    head_count = step_bias.shape[0]
    head_size = inner_raw.shape[1] // head_count
    state_size = shared.shape[1] // 2
    inner_act = conv_silu(inner_raw, conv_inner, conv_inner_bias, segment)
    shared_act = conv_silu(shared, conv_shared, conv_shared_bias, segment)
    write_all = shared_act[:, :state_size]
    read_all = shared_act[:, state_size:]
    step_size = jax.nn.softplus(step_raw + step_bias[None, :])
    decay_log = -jnp.exp(log_decay)[None, :] * step_size
    blocks = tokens // CH
    stacked = (
        inner_act.reshape(blocks, CH, head_count, head_size),
        write_all.reshape(blocks, CH, state_size),
        read_all.reshape(blocks, CH, state_size),
        step_size.reshape(blocks, CH, head_count),
        decay_log.reshape(blocks, CH, head_count),
        segment.reshape(blocks, CH),
    )
    start_state = (
        jnp.zeros((head_count, head_size, state_size), jnp.float32),
        jnp.array(-1, jnp.int32),
    )
    last_carry, outputs = lax.scan(jax.checkpoint(block_step), start_state, stacked)
    heads_out = outputs.reshape(tokens, head_count, head_size) + skip_gain[
        None, :, None
    ] * inner_act.reshape(tokens, head_count, head_size)
    return heads_out.reshape(tokens, head_count * head_size) * jax.nn.silu(gate_in)


def per_device(
    hidden_in,
    lengths,
    norm_gain,
    in_gate_inner,
    in_step,
    in_shared,
    conv_inner,
    conv_inner_bias,
    conv_shared,
    conv_shared_bias,
    step_bias,
    log_decay,
    skip_gain,
    gate_gain,
    out_weight,
    cotangent,
):
    source = hidden_in.astype(jnp.float32)
    tokens = source.shape[0]
    segment = segment_ids(lengths[0], tokens)
    live_mask = (segment < lengths.shape[1]).astype(jnp.float32)
    square_sum = lax.psum(jnp.sum(source * source, axis=1), "heads")
    inv_rms = lax.rsqrt(square_sum / D + EPSILON)
    normed_local = (source * inv_rms[:, None] * norm_gain[None, :]).astype(jnp.bfloat16)
    full_width = in_gate_inner.shape[0]
    inner_width = in_gate_inner.shape[2]
    flat_gate_inner = in_gate_inner.reshape(full_width, 2 * inner_width)
    piece_rows = lax.all_gather(normed_local, "heads", axis=1, tiled=True)
    piece_shared = lax.all_gather(in_shared, "heads", axis=1, tiled=True)
    rows_gate_inner = flat_gate_inner
    rows_step = in_step
    acc_gate_inner = jnp.dot(piece_rows, rows_gate_inner, preferred_element_type=jnp.float32)
    acc_step = jnp.dot(piece_rows, rows_step, preferred_element_type=jnp.float32)
    acc_shared = lax.dot_general(
        piece_rows, piece_shared, (((1,), (1,)), ((), ())), preferred_element_type=jnp.float32
    )
    normed_all = piece_rows
    acc_gate_inner, step_raw, shared, normed_all = (
        acc_gate_inner,
        acc_step,
        acc_shared,
        normed_all,
    )

    def local_mixer(
        gate_in,
        inner_raw,
        shared_in,
        step_in,
        kernel_inner,
        bias_inner,
        kernel_shared,
        bias_shared,
        bias_step,
        decay_rate,
        skip_part,
    ):
        return mixer(
            gate_in,
            inner_raw,
            shared_in,
            step_in,
            kernel_inner,
            bias_inner,
            kernel_shared,
            bias_shared,
            bias_step,
            decay_rate,
            skip_part,
            segment,
        )

    gated_out, mixer_back = jax.vjp(
        local_mixer,
        acc_gate_inner[:, :inner_width],
        acc_gate_inner[:, inner_width:],
        shared,
        step_raw,
        conv_inner,
        conv_inner_bias,
        conv_shared,
        conv_shared_bias,
        step_bias,
        log_decay,
        skip_gain,
    )
    gate_sum = lax.psum(jnp.sum(gated_out * gated_out, axis=1), "heads")
    gate_rms = lax.rsqrt(gate_sum / DI + EPSILON)
    scaled = (gated_out * gate_rms[:, None] * gate_gain[None, :]).astype(jnp.bfloat16)
    w_block = out_weight
    mixed_out = lax.psum_scatter(
        lax.dot_general(
            w_block, scaled, (((0,), (1,)), ((), ())), preferred_element_type=jnp.float32
        ),
        "heads",
        scatter_dimension=0,
        tiled=True,
    ).T
    output = (source + live_mask[:, None] * mixed_out).astype(jnp.bfloat16)
    live_low = live_mask.astype(jnp.bfloat16)
    masked = lax.all_gather(cotangent, "heads", axis=1, tiled=True) * live_low[:, None]
    w_block = out_weight
    grad_scaled = lax.dot_general(
        masked, w_block, (((1,), (1,)), ((), ())), preferred_element_type=jnp.float32
    )
    fresh = lax.dot_general(
        scaled, masked, (((0,), (0,)), ((), ())), preferred_element_type=jnp.float32
    )
    grad_wout = fresh
    grad_scaled, grad_wout = (grad_scaled, grad_wout)
    grad_gain_gate = jnp.sum(grad_scaled * gated_out * gate_rms[:, None], axis=0)
    gate_dot = lax.psum(jnp.sum(grad_scaled * gate_gain[None, :] * gated_out, axis=1), "heads")
    gate_cube = gate_rms * gate_rms * gate_rms
    grad_gated = (
        gate_rms[:, None] * gate_gain[None, :] * grad_scaled
        - gated_out * (gate_cube * gate_dot / DI)[:, None]
    )
    (
        grad_gate_in,
        grad_inner,
        grad_shared_part,
        grad_step_raw,
        grad_kernel_inner,
        grad_bias_inner,
        grad_kernel_part,
        grad_bias_part,
        grad_bias_step,
        grad_decay_rate,
        grad_skip,
    ) = mixer_back(grad_gated)
    grad_shared, grad_kernel_shared, grad_bias_shared = lax.psum(
        (grad_shared_part, grad_kernel_part, grad_bias_part), "heads"
    )
    low_gate_inner = jnp.concatenate([grad_gate_in, grad_inner], axis=1).astype(jnp.bfloat16)
    low_step = grad_step_raw.astype(jnp.bfloat16)
    low_shared = grad_shared.astype(jnp.bfloat16)
    rows_gate_inner = flat_gate_inner
    rows_step = in_step
    main_part = lax.dot_general(
        rows_gate_inner,
        low_gate_inner,
        (((1,), (1,)), ((), ())),
        preferred_element_type=jnp.float32,
    )
    grad_normed = lax.psum_scatter(
        main_part
        + lax.dot_general(
            rows_step, low_step, (((1,), (1,)), ((), ())), preferred_element_type=jnp.float32
        ),
        "heads",
        scatter_dimension=0,
        tiled=True,
    ).T
    grad_normed = grad_normed + lax.dot_general(
        low_shared, in_shared, (((1,), (0,)), ((), ())), preferred_element_type=jnp.float32
    )
    grad_gain_norm = jnp.sum(grad_normed * source * inv_rms[:, None], axis=0)
    norm_dot = lax.psum(jnp.sum(grad_normed * norm_gain[None, :] * source, axis=1), "heads")
    norm_cube = inv_rms * inv_rms * inv_rms
    grad_source = (
        inv_rms[:, None] * norm_gain[None, :] * grad_normed
        - source * (norm_cube * norm_dot / D)[:, None]
    )
    grad_input = cotangent.astype(jnp.float32) + grad_source
    grad_proj = lax.dot_general(
        normed_all, low_gate_inner, (((0,), (0,)), ((), ())), preferred_element_type=jnp.float32
    )
    grad_proj = grad_proj.reshape(full_width, 2, inner_width)
    grad_step_w = lax.dot_general(
        normed_all, low_step, (((0,), (0,)), ((), ())), preferred_element_type=jnp.float32
    )
    grad_shared_w = lax.dot_general(
        low_shared, normed_local, (((0,), (0,)), ((), ())), preferred_element_type=jnp.float32
    )
    summed = lax.psum(
        (
            grad_gain_norm,
            grad_proj,
            grad_step_w,
            grad_shared_w,
            grad_kernel_inner,
            grad_bias_inner,
            grad_kernel_shared,
            grad_bias_shared,
            grad_bias_step,
            grad_decay_rate,
            grad_skip,
            grad_gain_gate,
            grad_wout,
        ),
        "rows",
    )
    return (
        output,
        grad_input,
        summed[0],
        summed[1],
        summed[2],
        summed[3],
        summed[4],
        summed[5],
        summed[6],
        summed[7],
        summed[8],
        summed[9],
        summed[10],
        summed[11],
        summed[12],
    )


def solution(mesh):
    return jax.shard_map(
        per_device,
        mesh=mesh,
        in_specs=(
            P("rows", "heads"),
            P("rows", None),
            P("heads"),
            P(None, None, "heads"),
            P(None, "heads"),
            P(None, "heads"),
            P(None, "heads"),
            P("heads"),
            P(),
            P(),
            P("heads"),
            P("heads"),
            P("heads"),
            P("heads"),
            P("heads", None),
            P("rows", "heads"),
        ),
        out_specs=(
            P("rows", "heads"),
            P("rows", "heads"),
            P("heads"),
            P(None, None, "heads"),
            P(None, "heads"),
            P(None, "heads"),
            P(None, "heads"),
            P("heads"),
            P(),
            P(),
            P("heads"),
            P("heads"),
            P("heads"),
            P("heads"),
            P("heads", None),
        ),
        check_vma=False,
    )
```

profile of v0, /device:TPU:0, one launch (start us, length us, event | category | flops | bytes accessed | tf_op | source)
XLA Modules:
  0.0 2659.2 jit_solution(12310870349688964473)
XLA Ops:
  9.7 30.3 %psum.140 = f32[4096]{0:T(1024)S(1)} all-reduce(f32[4096]{0:T(1024)S(1)} %fusion.111), channel_id=1, replica_groups=mesh['rows'=4,'heads'=8] {'heads'}, use_global_device_ids=true, to_apply=%region_3.4 | all-reduce | flops 4096 | bytes 32768 | tf_op jit(solution)/shard_map/psum | solution.py:129
  46.2 17.1 all_gather.10
  68.7 128.5 %all-gather.3.cloned.1.call-done = bf16[4096,2048]{1,0:T(8,128)(2,1)} async-done(((bf16[4096,256]{1,0:T(8,128)(2,1)}), bf16[4096,2048]{1,0:T(8,128)(2,1)}) %all-gather.3.cloned.1.call-update) | async-done | bytes 16777232 | tf_op jit(solution)/shard_map/all_gather | solution.py:135
  219.2 23.4 fusion.159
  297.8 297.6 %while.45 = (s32[]{:T(128)}, f32[8,64,64]{2,1,0:T(8,128)S(1)}, s32[]{:T(128)}, f32[16,256,8,64]{1,3,2,0:T(8,128)}, f32[16,8,64,64]{3,2,1,0:T(8,128)}, /*index=5*...) while((s32[]{:T(128)}, f32[8,64,64]{2,1,0:T(8,128)S(1)}, ...), condition=%wide.region_7.8_spmd.clone, body=%wide.region_4.7_spmd.clone.sunk | while | flops 657433856 | bytes 4478122 | solution.py:100
  607.8 14.2 reshape.549
  622.0 13.6 multiply_reduce_fusion.11
  635.6 26.1 psum.141
  661.8 17.6 multiply_reduce_fusion.4
  679.4 25.9 psum.142
  705.3 19.6 multiply_reduce_fusion.5
  758.6 829.5 %while.46 = (s32[]{:T(128)}, f32[8,64,64]{2,1,0:T(8,128)}, f32[16,256,8,64]{1,3,2,0:T(8,128)}, f32[16,256,64]{1,2,0:T(8,128)}, f32[16,256,64]{1,2,0:T(8,128)}, /...) while((s32[]{:T(128)}, f32[8,64,64]{2,1,0:T(8,128)}, ...), condition=%wide.region_26.27_spmd.clone, body=%wide.region_13.26_spmd.clone.sunk | while | flops 1470606336 | bytes 14248691 | solution.py:100
  1600.4 14.2 reshape.551
  1614.7 22.9 multiply_reduce_fusion.8
  1672.7 32.1 %add_bitcast_fusion.2 = f32[2048,4096]{0,1:T(8,128)} fusion(f32[4096,2048]{1,0:T(8,128)} %fusion.133, bf16[2048,1024]{1,0:T(8,128)(2,1)} %bitcast.374, bf16[4096,512]{1,0:T(8,128)(2,1)} %fusion.105, bf16[4096,512]{1,0:T(8,128)(2,1)} %get-tuple-element.798), kind=kOutput, calls=%fused_computation.138 | convolution fusion | flops 17205035008 | bytes 79691776 | tf_op jit(solution)/shard_map/dot_general | solution.py:246
  1705.5 19.1 convolution_bitcast_fusion.2
  1742.6 21.7 fusion.110
  1777.5 91.1 %all-reduce.30 = bf16[4096,128]{1,0:T(8,128)(2,1)S(1)} all-reduce(f32[4096,128]{1,0:T(8,128)} %pad_add_fusion.3), channel_id=1, replica_groups=mesh['rows'=4,'heads'=8] {'heads'}, use_global_device_ids=true, to_apply=%region_28.29 | all-reduce | flops 524288 | bytes 3145728 | tf_op jit(solution)/shard_map/psum | solution.py:238
  1880.2 19.5 fusion.96
  1900.7 167.2 %reduce-scatter.5.cloned.1.call-done = f32[256,4096]{0,1:T(8,128)} async-done(((f32[2048,4096]{0,1:T(8,128)}), f32[256,4096]{0,1:T(8,128)}) %reduce-scatter.5.cloned.1.call-update) | async-done | bytes 4194320 | tf_op jit(solution)/shard_map/reduce_scatter | solution.py:252
  2073.4 27.6 %all-reduce.23 = (f32[4096]{0:T(1024)S(1)}, f32[4,128]{1,0:T(4,128)S(1)}, f32[128]{0:T(128)S(1)}) all-reduce(f32[4096]{0:T(1024)S(1)} %get-tuple-element.688, f32[4,128]{1,0:T(4,128)S(1)} %pad_add_fusion.7, f32[128]{0:T(128)S(1)} %get-tuple-element.693), channel_id=1, replica_groups=mesh['rows'=4,'heads'=8] {'heads'}, use_global_device_ids=true, to_apply=%region_30.31 | all-reduce | flops 4736 | bytes 37888 | tf_op jit(solution)/shard_map/psum | solution.py:265
  2101.0 16.8 all-reduce.24
  2117.8 276.8 %reduce-scatter.3.cloned.1.call-done = f32[256,4096]{0,1:T(8,128)} async-done(((f32[2048,4096]{0,1:T(8,128)}), f32[256,4096]{0,1:T(8,128)}) %reduce-scatter.3.cloned.1.call-update) | async-done | bytes 4194320 | tf_op jit(solution)/shard_map/reduce_scatter | solution.py:198
  2403.6 236.4 %all-reduce.29.cloned.1.call-done = (f32[2048,2,512]{2,1,0:T(2,128)}, f32[2048,8]{0,1:T(8,128)}, f32[128,256]{1,0:T(8,128)}, f32[512,2048]{1,0:T(8,128)}) async-done(((f32[2048,2,512]{2,1,0:T(2,128)}, f32[2048,8]{0,1:T(8,128)}, f32[128,256]{1,0:T(8,128)}, f32[512,2048]{1,0:T(8,128)}), (f32[2048,2,512]{2,1,0:T(2,128)}, f32[2048,8]{0,1:T(8,128)}, f32[128,256]{1,0:T(8,128)}, ...) | async-done | bytes 12779536 | tf_op jit(solution)/shard_map/psum | solution.py:282
  (1502 shorter events, 1359.2 us)
Async XLA Ops:
  7.2 654.6 %copy-start = (bf16[512,2048]{1,0:T(8,128)(2,1)S(1)}, bf16[512,2048]{1,0:T(8,128)(2,1)}, u32[]{:S(2)}) copy-start(bf16[512,2048]{1,0:T(8,128)(2,1)} %param.34) | copy-start | bytes 6291460
  7.3 189.9 %all-gather.3.cloned.1.call-start = ((), (), s32[]{:S(2)}) async-start(), calls=%async_computation.2 | async-start | bytes 18874368 | tf_op jit(solution)/shard_map/all_gather | solution.py:135
  43.5 618.3 %all-gather.5.cloned.1.call-start = ((), (), s32[]{:S(2)}) async-start(), calls=%async_computation.4 | async-start | bytes 18874368 | tf_op jit(solution)/shard_map/all_gather | solution.py:208
  44.2 2023.7 %reduce-scatter.5.cloned.1.call-start = ((), (), s32[]{:S(2)}) async-start(), calls=%async_computation.5 | async-start | bytes 37748736 | tf_op jit(solution)/shard_map/reduce_scatter | solution.py:252
  45.8 201.2 %copy-start.12 = (f32[4096]{0:T(1024)}, f32[4096]{0:T(1024)S(1)}, u32[]{:S(2)}) copy-start(f32[4096]{0:T(1024)S(1)} %get-tuple-element.815) | copy-start | bytes 49156
  45.8 201.2 %copy-start.14 = (f32[4096]{0:T(1024)}, f32[4096]{0:T(1024)S(1)}, u32[]{:S(2)}) copy-start(f32[4096]{0:T(1024)S(1)} %get-tuple-element.816) | copy-start | bytes 49156
  45.8 201.2 %copy-start.16 = (f32[4096]{0:T(1024)}, f32[4096]{0:T(1024)S(1)}, u32[]{:S(2)}) copy-start(f32[4096]{0:T(1024)S(1)} %get-tuple-element.817) | copy-start | bytes 49156
  45.8 615.9 %copy-start.60 = (bf16[4096]{0:T(1024)(128)(2,1)}, bf16[4096]{0:T(1024)(128)(2,1)S(1)}, u32[]{:S(2)}) copy-start(bf16[4096]{0:T(1024)(128)(2,1)S(1)} %get-tuple-element.814) | copy-start | bytes 24580
  45.9 236.1 %copy-start.51 = (f32[8]{0:T(128)}, f32[8]{0:T(128)S(1)}, u32[]{:S(2)}) copy-start(f32[8]{0:T(128)S(1)} %exponential_negate_fusion) | copy-start | bytes 100
  46.1 659.2 %copy-start.40 = (f32[512]{0:T(512)}, f32[512]{0:T(512)S(1)}, u32[]{:S(2)}) copy-start(f32[512]{0:T(512)S(1)} %mul.1018) | copy-start | bytes 6148
  46.1 200.9 %copy-start.42 = (f32[1,512]{1,0:T(1,128)}, f32[1,512]{1,0:T(1,128)S(1)}, u32[]{:S(2)}) copy-start(f32[1,512]{1,0:T(1,128)S(1)} %get-tuple-element.819) | copy-start | bytes 6148
  46.1 200.9 %copy-start.44 = (f32[1,512]{1,0:T(1,128)}, f32[1,512]{1,0:T(1,128)S(1)}, u32[]{:S(2)}) copy-start(f32[1,512]{1,0:T(1,128)S(1)} %get-tuple-element.820) | copy-start | bytes 6148
  46.2 200.9 %copy-start.46 = (f32[1,512]{1,0:T(1,128)}, f32[1,512]{1,0:T(1,128)S(1)}, u32[]{:S(2)}) copy-start(f32[1,512]{1,0:T(1,128)S(1)} %get-tuple-element.821) | copy-start | bytes 6148
  46.2 200.9 %copy-start.48 = (f32[1,512]{1,0:T(1,128)}, f32[1,512]{1,0:T(1,128)S(1)}, u32[]{:S(2)}) copy-start(f32[1,512]{1,0:T(1,128)S(1)} %get-tuple-element.822) | copy-start | bytes 6148
  1704.8 689.8 %reduce-scatter.3.cloned.1.call-start = ((), (), s32[]{:S(2)}) async-start(), calls=%async_computation.3 | async-start | bytes 37748736 | tf_op jit(solution)/shard_map/reduce_scatter | solution.py:198
  1724.6 915.4 %all-reduce.29.cloned.1.call-start = ((), (), s32[]{:S(2)}) async-start(), calls=%async_computation.6 | async-start | bytes 25559040 | tf_op jit(solution)/shard_map/psum | solution.py:282
  1899.8 168.1 %copy-start.27 = (bf16[128,256]{1,0:T(8,128)(2,1)S(1)}, bf16[128,256]{1,0:T(8,128)(2,1)}, u32[]{:S(2)}) copy-start(bf16[128,256]{1,0:T(8,128)(2,1)} %param.25) | copy-start | bytes 196612
  1899.8 168.1 %copy-start.29 = (f32[4096]{0:T(1024)S(1)}, f32[4096]{0:T(1024)}, u32[]{:S(2)}) copy-start(f32[4096]{0:T(1024)} %copy-done.28) | copy-start | bytes 49156
  1899.8 168.1 %copy-start.50 = (f32[256]{0:T(256)S(1)}, f32[256]{0:T(256)}, u32[]{:S(2)}) copy-start(f32[256]{0:T(256)} %param.22) | copy-start | bytes 3076
  1899.8 201.2 %copy-start.54 = (f32[512]{0:T(512)S(1)}, f32[512]{0:T(512)}, u32[]{:S(2)}) copy-start(f32[512]{0:T(512)} %get-tuple-element.685) | copy-start | bytes 6148
  1899.8 201.2 %copy-start.73 = (f32[512]{0:T(512)S(1)}, f32[512]{0:T(512)}, u32[]{:S(2)}) copy-start(f32[512]{0:T(512)} %get-tuple-element.680) | copy-start | bytes 6148
  1899.9 201.2 %copy-start.75 = (f32[8]{0:T(128)S(1)}, f32[8]{0:T(128)}, u32[]{:S(2)}) copy-start(f32[8]{0:T(128)} %get-tuple-element.774) | copy-start | bytes 100
  1899.9 218.0 %copy-start.32 = (f32[4096]{0:T(1024)S(1)}, f32[4096]{0:T(1024)}, u32[]{:S(2)}) copy-start(f32[4096]{0:T(1024)} %copy-done.31) | copy-start | bytes 49156
  1899.9 494.8 %copy-start.39 = (f32[4096]{0:T(1024)S(1)}, f32[4096]{0:T(1024)}, u32[]{:S(2)}) copy-start(f32[4096]{0:T(1024)} %get-tuple-element.818) | copy-start | bytes 49156
  (199 other events, 3246.7 us)
Sparse Core Ops, SparseCore 0:
  43.6 153.5 all-gather.2
  198.8 150.0 all-gather.4
  1705.0 362.8 reduce-scatter.4
  2070.1 324.4 reduce-scatter.2
  2399.0 240.9 all-reduce.28
where the time goes:
time: 2680 us; the launch traced here: 2660 us
  waiting for transfers between devices  810 us (30%)
  matrix products  620 us (23%)
  other arithmetic  510 us (19%)
  local copies, waits for them, and re-layouts  446 us (17%)
  blocking collectives  235 us (9%)
    reduce_scatter x1, waiting for transfers between devices, per_device(): lax.psum_scatter(lax.dot_general(w_block, scaled, (((0,), (1,)), ((), ())...  277 us
    psum x1, waiting for transfers between devices, per_device(): lax.psum((grad_gain_norm, grad_proj, grad_step_w, grad_shared_w, grad_ker...  236 us
    dot_general x48, matrix products, block_step(): within = jnp.einsum('hij,jhp->ihp', mixing, inner_blk, precision=exact_mode)  183 us
    reduce_scatter x1, waiting for transfers between devices, per_device(): lax.psum_scatter(main_part + lax.dot_general(rows_step, low_step, (((1,),...  167 us
    all_gather x1, waiting for transfers between devices, per_device(): piece_rows = lax.all_gather(normed_local, 'heads', axis=1, tiled=True)  129 us
    dot_general x64, matrix products, block_step(): jnp.einsum('in,hpn->ihp', read_blk, carry_state, precision=exact_mode)  124 us
    another operation x115, other arithmetic  116 us
    psum x1, blocking collectives, per_device(): lax.psum((grad_shared_part, grad_kernel_part, grad_bias_part), 'heads')  91.1 us
  transfers between devices with their start and end apart: 5, of which 4 were waited for; matrix products, arithmetic and copies ran while one was open for 20% of the time, Pallas kernels for 0%

commit v1 on v0

v1 whole, which is shorter than its diff:
```python
import functools

import jax
import jax.numpy as jnp
from jax import lax
from jax.experimental import pallas as pl
from jax.experimental.pallas import tpu as pltpu
from jax.sharding import PartitionSpec as P


EPSILON = 1e-05
L = 128
LB = 512
NSUB = LB // L
HEAD = 64
STATE = 64
f32 = jnp.float32
bf16 = jnp.bfloat16


def mm(a, b, ca=1, cb=0):
    return lax.dot_general(a, b, (((ca,), (cb,)), ((), ())), preferred_element_type=f32)


def split(x):
    hi = x.astype(bf16)
    return hi, (x - hi.astype(f32)).astype(bf16)


def mm3(a, b, ca=1, cb=0):
    ah, al = split(a)
    bh, bl = split(b)
    return mm(ah, bh, ca, cb) + mm(ah, bl, ca, cb) + mm(al, bh, ca, cb)


def mm_exact_left(mask, x):
    hi = x.astype(bf16)
    rest = x - hi.astype(f32)
    mid = rest.astype(bf16)
    low = (rest - mid.astype(f32)).astype(bf16)
    return mm(mask, hi) + mm(mask, mid) + mm(mask, low)


def block_diag(x, first):
    zero = jnp.zeros_like(x)
    return jnp.concatenate([jnp.where(first, x, zero), jnp.where(first, zero, x)], axis=0)


def bounds_of(len_ref):
    b0 = len_ref[0, 0]
    b1 = b0 + len_ref[0, 1]
    b2 = b1 + len_ref[0, 2]
    b3 = b2 + len_ref[0, 3]
    return b0, b1, b2, b3


def start_of(bounds, t):
    start = jnp.zeros_like(t)
    for b in bounds:
        start = jnp.where(t >= b, b, start)
    return start


def to_row(col):
    return jnp.transpose(jnp.broadcast_to(col, (L, L)))[0:1, :]


def to_col(row):
    return jnp.transpose(jnp.broadcast_to(row, (L, L)))


def pair_cols(a, q, first):
    return jnp.where(first, a[:, 2 * q : 2 * q + 1], a[:, 2 * q + 1 : 2 * q + 2])


def softplus(v):
    return jnp.maximum(v, 0.0) + jnp.log1p(jnp.exp(-jnp.abs(v)))


def shifted(win, m):
    if m == 0:
        return win[8:, :]
    return pltpu.roll(win, m, 0)[8:, :]


def chunk_columns(hp_ref, step, bounds, base):
    tcol = lax.broadcasted_iota(jnp.int32, (L, L), 0) + base
    trow = lax.broadcasted_iota(jnp.int32, (L, L), 1) + base
    start_col = start_of(bounds, tcol)
    start_end = start_of(bounds, base + (L - 1))
    raw = step + hp_ref[0:1, :]
    dt = softplus(raw)
    decay = hp_ref[1:2, :] * dt
    lower = jnp.where(trow <= tcol, 1.0, 0.0).astype(bf16)
    cum = mm_exact_left(lower, decay)
    cum_end = cum[L - 1 : L, :]
    ecum = jnp.where(start_col < base, jnp.exp(cum), 0.0)
    wend = jnp.where(tcol >= start_end, jnp.exp(cum_end - cum), 0.0)
    carried_end = (start_end < base).astype(f32)
    cdec = jnp.exp(cum_end) * carried_end
    return tcol, trow, start_col, start_end, raw, dt, decay, cum, ecum, wend, cdec


def fwd_kernel(
    len_ref, h_ref, gain_ref, wgi_ref, wss_ref, cp_ref, sp_ref, hp_ref,
    normed_ref, inv_ref, gate_ref, rest_ref, gated_ref, y_ref, st_ref, gsum_ref,
    vbuf, state,
):
    blk = pl.program_id(0)
    width = gate_ref.shape[1]
    full = h_ref.shape[1]
    pairs = width // L

    @pl.when(blk == 0)
    def _():
        vbuf[0:8, :] = jnp.zeros((8, vbuf.shape[1]), f32)
        state[...] = jnp.zeros(state.shape, f32)

    piece = 256

    def norm_rows(s, carry):
        rows = pl.ds(pl.multiple_of(s * L, L), L)
        acc = jnp.zeros((L, piece), f32)
        for k in range(full // piece):
            x = h_ref[rows, k * piece : (k + 1) * piece].astype(f32)
            acc = acc + x * x
        inv = lax.rsqrt(jnp.sum(acc, axis=1, keepdims=True) / full + EPSILON)
        for k in range(full // piece):
            cols = slice(k * piece, (k + 1) * piece)
            x = h_ref[rows, cols].astype(f32)
            normed_ref[rows, cols] = (x * inv * gain_ref[0:1, cols]).astype(bf16)
        inv_ref[s] = to_row(inv)
        return carry

    lax.fori_loop(0, NSUB, norm_rows, 0)
    normed = normed_ref[...]
    gate_ref[...] = mm(normed, wgi_ref[:, :width])
    inner = mm(normed, wgi_ref[:, width:])
    vbuf[8:, :width] = inner
    rest_ref[:, :width] = inner
    tail = mm(normed, wss_ref[...])
    vbuf[8:, width:] = tail[:, :L]
    rest_ref[:, width:] = tail

    bounds = bounds_of(len_ref)
    first = lax.broadcasted_iota(jnp.int32, (L, L), 1) < HEAD

    def chunk(s, carry):
        r0 = pl.multiple_of(s * L, L)
        rows = pl.ds(r0, L)
        base = blk * LB + s * L
        step = rest_ref[rows, width + L :]
        tcol, trow, start_col, _, _, dt, _, cum, ecum, wend, cdec = chunk_columns(
            hp_ref, step, bounds, base
        )
        cum_t = jnp.transpose(cum)
        mask = (trow <= tcol) & (trow >= start_col)
        valid = [tcol - m >= start_col for m in range(4)]

        def conv(cols, taps):
            win = vbuf[pl.ds(r0, L + 8), cols]
            pre = taps[4:5, :] + taps[3:4, :] * win[8:, :]
            for m in range(1, 4):
                pre = pre + taps[3 - m : 4 - m, :] * jnp.where(valid[m], shifted(win, m), 0.0)
            return pre

        pre_s = conv(slice(width, width + L), sp_ref)
        act = pre_s * lax.logistic(pre_s)
        b_map = act[:, :STATE]
        c_map = act[:, STATE:]
        scores = jnp.where(mask, mm3(c_map, b_map, 1, 1), 0.0)
        square = jnp.zeros((L, L), f32)
        for q in range(pairs):
            cols = slice(q * L, (q + 1) * L)
            pre = conv(cols, cp_ref.at[:, cols])
            xin = pre * lax.logistic(pre)
            xp = xin * pair_cols(dt, q, first)
            xh, xl = split(xp)
            bdh, bdl = block_diag(xh, first), block_diag(xl, first)
            mix = []
            for h in (2 * q, 2 * q + 1):
                spread = jnp.minimum(cum[:, h : h + 1] - cum_t[h : h + 1, :], 0.0)
                mix.append(jnp.exp(spread) * scores)
            mh, ml = split(jnp.concatenate(mix, axis=1))
            both = mm(mh, jnp.concatenate([bdh, bdl], axis=1))
            y = both[:, :L] + both[:, L:] + mm(ml, bdh)
            st = state[:, cols]
            st_ref[s, :, cols] = st
            y = y + mm3(c_map, st) * pair_cols(ecum, q, first)
            xw = xp * pair_cols(wend, q, first)
            state[:, cols] = mm3(b_map, xw, 0, 0) + st * pair_cols(cdec, q, first[0:1, :])
            y_ref[rows, cols] = y
            gate = gate_ref[rows, cols]
            gated = (y + cp_ref[5:6, cols] * xin) * (gate * lax.logistic(gate))
            gated_ref[rows, cols] = gated
            square = square + gated * gated
        gsum_ref[s] = to_row(jnp.sum(square, axis=1, keepdims=True))
        return carry

    lax.fori_loop(0, NSUB, chunk, 0)
    vbuf[0:8, :] = vbuf[LB : LB + 8, :]


def mid_kernel(len_ref, cot_ref, w_ref, gated_ref, cp_ref, gs_ref, gdot_ref):
    blk = pl.program_id(0)
    live = bounds_of(len_ref)[3]
    t = lax.broadcasted_iota(jnp.int32, gs_ref.shape, 0) + blk * LB
    gs = jnp.where(t < live, mm(cot_ref[...], w_ref[...], 1, 1), 0.0)
    gs_ref[...] = gs
    dots = jnp.sum(gs * cp_ref[6:7, :] * gated_ref[...], axis=1, keepdims=True)
    for s in range(NSUB):
        gdot_ref[s] = to_row(dots[s * L : (s + 1) * L, :])


def bwd_kernel(
    inner_total,
    len_ref, gate_ref, rest_ref, halo_ref, gs_ref, y_ref, st_ref, gsum_ref, gdot_ref,
    cp_ref, sp_ref, hp_ref,
    low_ref, gsh_ref, nd_ref, size_ref, pg_ref, sg_ref, hg_ref,
    vbuf, qnext, adj, send,
):
    step_id = pl.program_id(0)
    blk = pl.num_programs(0) - 1 - step_id
    width = gate_ref.shape[1]
    pairs = width // L

    @pl.when(step_id == 0)
    def _():
        qnext[...] = jnp.zeros(qnext.shape, f32)
        adj[...] = jnp.zeros(adj.shape, f32)
        send[...] = jnp.zeros(send.shape, f32)
        pg_ref[...] = jnp.zeros(pg_ref.shape, f32)
        sg_ref[...] = jnp.zeros(sg_ref.shape, f32)
        hg_ref[...] = jnp.zeros(hg_ref.shape, f32)

    vbuf[0:8, :] = halo_ref[:, : width + L]
    vbuf[8:, :] = rest_ref[:, : width + L]
    bounds = bounds_of(len_ref)
    first = lax.broadcasted_iota(jnp.int32, (L, L), 1) < HEAD
    lane = lax.broadcasted_iota(jnp.int32, (L, L), 1)
    half = lax.broadcasted_iota(jnp.int32, (L, L), 0) // HEAD

    def chunk(i, carry):
        s = NSUB - 1 - i
        r0 = pl.multiple_of(s * L, L)
        rows = pl.ds(r0, L)
        base = blk * LB + s * L
        step = rest_ref[rows, width + L :]
        tcol, trow, start_col, start_end, raw, dt, decay, cum, ecum, wend, cdec = chunk_columns(
            hp_ref, step, bounds, base
        )
        cum_t = jnp.transpose(cum)
        mask_t = (trow >= tcol) & (start_of(bounds, trow) <= tcol)
        valid = [tcol - m >= start_col for m in range(4)]
        valid_up = [start_of(bounds, tcol + m) <= tcol for m in range(4)]
        gate_rms_row = lax.rsqrt(gsum_ref[s] / inner_total + EPSILON)
        pull_row = gate_rms_row * gate_rms_row * gate_rms_row * gdot_ref[s] / inner_total
        gate_rms = to_col(gate_rms_row)
        pull = to_col(pull_row)

        def conv(cols, taps):
            win = vbuf[pl.ds(r0, L + 8), cols]
            seen = [win[8:, :]]
            pre = taps[4:5, :] + taps[3:4, :] * seen[0]
            for m in range(1, 4):
                seen.append(jnp.where(valid[m], shifted(win, m), 0.0))
                pre = pre + taps[3 - m : 4 - m, :] * seen[m]
            return seen, pre

        def conv_back(q, seen, cols, taps, grad_ref, grad_cols):
            win = jnp.concatenate([q, qnext[:, cols]], axis=0)
            qnext[:, cols] = q[0:8, :]
            grad = taps[3:4, :] * q
            for m in range(1, 4):
                up = pltpu.roll(win, L + 8 - m, 0)[:L, :]
                grad = grad + taps[3 - m : 4 - m, :] * jnp.where(valid_up[m], up, 0.0)
            for m in range(4):
                k = 3 - m
                grad_ref[k : k + 1, grad_cols] += jnp.sum(q * seen[m], axis=0, keepdims=True)
            grad_ref[4:5, grad_cols] += jnp.sum(q, axis=0, keepdims=True)
            return grad

        seen_s, pre_s = conv(slice(width, width + L), sp_ref)
        sig_s = lax.logistic(pre_s)
        act = pre_s * sig_s
        b_map = act[:, :STATE]
        c_map = act[:, STATE:]
        scores_t = jnp.where(mask_t, mm3(b_map, c_map, 1, 1), 0.0)
        d_scores = jnp.zeros((L, L), f32)
        d_b = jnp.zeros((L, STATE), f32)
        d_c = jnp.zeros((L, STATE), f32)
        reduced = jnp.zeros((2 * L, L), f32)
        ends = jnp.zeros((8, L), f32)
        norm_dot = jnp.zeros((L, L), f32)
        size = jnp.zeros((L, L), f32)
        for q in range(pairs):
            cols = slice(q * L, (q + 1) * L)
            taps = cp_ref.at[:, cols]
            skip = cp_ref[5:6, cols]
            seen, pre = conv(cols, taps)
            sig = lax.logistic(pre)
            xin = pre * sig
            dtx = pair_cols(dt, q, first)
            xp = xin * dtx
            y = y_ref[rows, cols]
            ho = y + skip * xin
            gate = gate_ref[rows, cols]
            gsig = lax.logistic(gate)
            sl = gate * gsig
            gated = ho * sl
            gs = gs_ref[rows, cols]
            pg_ref[6:7, cols] += jnp.sum(gs * gated * gate_rms, axis=0, keepdims=True)
            gg = gate_rms * cp_ref[6:7, cols] * gs - gated * pull
            gy = gg * sl
            low_gate = (gg * ho * (gsig * (1.0 + gate * (1.0 - gsig)))).astype(bf16)
            low_ref[rows, cols] = low_gate
            pg_ref[5:6, cols] += jnp.sum(gy * xin, axis=0, keepdims=True)

            yh, yl = split(gy)
            bdh, bdl = block_diag(yh, first), block_diag(yl, first)
            xh, xl = split(xp)
            d_mix = mm(
                jnp.concatenate([xh, xl], axis=1), jnp.concatenate([bdh, bdh], axis=1), 1, 1
            ) + mm(xh, bdl, 1, 1)
            mix = []
            for k in range(2):
                h = 2 * q + k
                spread = jnp.minimum(cum_t[h : h + 1, :] - cum[:, h : h + 1], 0.0)
                factor = jnp.exp(spread)
                d_scores = d_scores + d_mix[:, k * L : (k + 1) * L] * factor
                mix.append(factor * scores_t)
            mh, ml = split(jnp.concatenate(mix, axis=1))
            both = mm(mh, jnp.concatenate([bdh, bdl], axis=1))
            dxp = both[:, :L] + both[:, L:] + mm(ml, bdh)
            wendx = pair_cols(wend, q, first)
            a_in = adj[:, cols]
            dxp = dxp + mm3(b_map, a_in) * wendx
            xw = xp * wendx
            gyw = gy * pair_cols(ecum, q, first)
            s_in = st_ref[s, :, cols]
            d_b = d_b + mm3(xw, a_in, 1, 1)
            d_c = d_c + mm3(gyw, s_in, 1, 1)
            adj[:, cols] = mm3(c_map, gyw, 0, 0) + a_in * pair_cols(cdec, q, first[0:1, :])
            heads = jnp.where(lane == 2 * q + half, 1.0, 0.0).astype(bf16)
            zh, zl = split(jnp.concatenate([gy * y - dxp * xp, dxp * xin], axis=0))
            reduced = reduced + mm(zh, heads) + mm(zl, heads)
            end = jnp.broadcast_to(
                jnp.sum(a_in * send[:, cols], axis=0, keepdims=True), (8, L)
            )
            eh, el = split(end)
            ends = ends + mm(eh, heads) + mm(el, heads)
            send[:, cols] = s_in

            dxin = dxp * dtx + skip * gy
            qv = dxin * (sig * (1.0 + pre * (1.0 - sig)))
            grad = conv_back(qv, seen, cols, taps, pg_ref, cols)
            low_inner = grad.astype(bf16)
            low_ref[rows, width + q * L : width + (q + 1) * L] = low_inner
            wide_gate, wide_inner = low_gate.astype(f32), low_inner.astype(f32)
            norm_dot = norm_dot + wide_gate * gate + wide_inner * seen[0]
            size = size + wide_gate * wide_gate + wide_inner * wide_inner

        d_scores = jnp.where(mask_t, d_scores, 0.0)
        d_b = d_b + mm3(d_scores, c_map)
        d_c = d_c + mm3(d_scores, b_map, 0, 0)
        d_act = jnp.concatenate([d_b, d_c], axis=1)
        q_s = d_act * (sig_s * (1.0 + pre_s * (1.0 - sig_s)))
        shared_cols = slice(width, width + L)
        gsh_ref[rows, :] = conv_back(q_s, seen_s, shared_cols, sp_ref, sg_ref, slice(0, L))

        tail = jnp.where(tcol >= start_end, ends[0:1, :], 0.0)
        keep = jnp.where(mask_t, 1.0, 0.0).astype(bf16)
        d_decay = mm_exact_left(keep, reduced[:L, :]) + tail
        d_dt = reduced[L:, :] + d_decay * hp_ref[1:2, :]
        d_raw = d_dt * lax.logistic(raw)
        hg_ref[0:1, :] += jnp.sum(d_raw, axis=0, keepdims=True)
        hg_ref[1:2, :] += jnp.sum(d_decay * decay, axis=0, keepdims=True)
        low_step = d_raw.astype(bf16)
        low_ref[rows, 2 * width :] = low_step
        wide_step = low_step.astype(f32)
        norm_dot = norm_dot + wide_step * step
        size = size + wide_step * wide_step
        nd_ref[s] = to_row(jnp.sum(norm_dot, axis=1, keepdims=True))
        size_ref[s] = to_row(jnp.sum(size, axis=1, keepdims=True))
        return carry

    lax.fori_loop(0, NSUB, chunk, 0)


def unpack_kernel(x_ref, gate_inner_ref, step_ref):
    width = gate_inner_ref.shape[2]
    gate_inner_ref[:, 0, :] = x_ref[:, :width]
    gate_inner_ref[:, 1, :] = x_ref[:, width : 2 * width]
    step_ref[...] = x_ref[:, 2 * width : 2 * width + step_ref.shape[1]]


def unpack(x, width, heads):
    rows = x.shape[0]
    return pl.pallas_call(
        unpack_kernel,
        grid=(rows // 256,),
        in_specs=[pl.BlockSpec((256, x.shape[1]), lambda i: (i, 0))],
        out_specs=[
            pl.BlockSpec((256, 2, width), lambda i: (i, 0, 0)),
            pl.BlockSpec((256, heads), lambda i: (i, 0)),
        ],
        out_shape=[
            jax.ShapeDtypeStruct((rows, 2, width), f32),
            jax.ShapeDtypeStruct((rows, heads), f32),
        ],
        name="unpack",
    )(x)


def rows_spec(cols, order):
    return pl.BlockSpec((LB, cols), lambda i: (order(i), 0))


def line_spec(order):
    return pl.BlockSpec((NSUB, 1, L), lambda i: (order(i), 0, 0))


def whole_spec(shape):
    return pl.BlockSpec(shape, lambda i: (0,) * len(shape), pipeline_mode=pl.Buffered(1))


def smem_spec():
    return pl.BlockSpec(memory_space=pltpu.SMEM)


VMEM_LIMIT = 60 * 1024 * 1024


def run_fwd(lengths, hidden, gain, wgi, wss, cp, sp, hp):
    tokens, full = hidden.shape
    width = wgi.shape[1] // 2
    lines = tokens // L

    def same(i):
        return i

    return pl.pallas_call(
        fwd_kernel,
        grid=(tokens // LB,),
        in_specs=[
            smem_spec(),
            rows_spec(full, same),
            whole_spec(gain.shape),
            whole_spec(wgi.shape),
            whole_spec(wss.shape),
            whole_spec(cp.shape),
            whole_spec(sp.shape),
            whole_spec(hp.shape),
        ],
        out_specs=[
            rows_spec(full, same),
            line_spec(same),
            rows_spec(width, same),
            rows_spec(width + 2 * L, same),
            rows_spec(width, same),
            rows_spec(width, same),
            pl.BlockSpec((NSUB, STATE, width), lambda i: (i, 0, 0)),
            line_spec(same),
        ],
        out_shape=[
            jax.ShapeDtypeStruct((tokens, full), bf16),
            jax.ShapeDtypeStruct((lines, 1, L), f32),
            jax.ShapeDtypeStruct((tokens, width), f32),
            jax.ShapeDtypeStruct((tokens, width + 2 * L), f32),
            jax.ShapeDtypeStruct((tokens, width), f32),
            jax.ShapeDtypeStruct((tokens, width), f32),
            jax.ShapeDtypeStruct((lines, STATE, width), f32),
            jax.ShapeDtypeStruct((lines, 1, L), f32),
        ],
        scratch_shapes=[
            pltpu.VMEM((LB + 8, width + L), f32),
            pltpu.VMEM((STATE, width), f32),
        ],
        compiler_params=pltpu.CompilerParams(
            dimension_semantics=("arbitrary",), vmem_limit_bytes=VMEM_LIMIT
        ),
        name="mixer_fwd",
    )(lengths, hidden, gain, wgi, wss, cp, sp, hp)


def run_mid(lengths, cot, w_out, gated, cp):
    tokens, full = cot.shape
    width = gated.shape[1]
    lines = tokens // L

    def same(i):
        return i

    return pl.pallas_call(
        mid_kernel,
        grid=(tokens // LB,),
        in_specs=[
            smem_spec(),
            rows_spec(full, same),
            whole_spec(w_out.shape),
            rows_spec(width, same),
            whole_spec(cp.shape),
        ],
        out_specs=[rows_spec(width, same), line_spec(same)],
        out_shape=[
            jax.ShapeDtypeStruct((tokens, width), f32),
            jax.ShapeDtypeStruct((lines, 1, L), f32),
        ],
        compiler_params=pltpu.CompilerParams(
            dimension_semantics=("arbitrary",), vmem_limit_bytes=VMEM_LIMIT
        ),
        name="mixer_mid",
    )(lengths, cot, w_out, gated, cp)


def run_bwd(inner_total, lengths, gate, rest, gs, y, st, gsum, gdot, cp, sp, hp):
    tokens, width = gate.shape
    lines = tokens // L
    blocks = tokens // LB

    def back(i):
        return blocks - 1 - i

    def halo(i):
        return (jnp.maximum(back(i) * (LB // 8) - 1, 0), 0)

    return pl.pallas_call(
        functools.partial(bwd_kernel, float(inner_total)),
        grid=(blocks,),
        in_specs=[
            smem_spec(),
            rows_spec(width, back),
            rows_spec(width + 2 * L, back),
            pl.BlockSpec((8, width + 2 * L), halo),
            rows_spec(width, back),
            rows_spec(width, back),
            pl.BlockSpec((NSUB, STATE, width), lambda i: (back(i), 0, 0)),
            line_spec(back),
            line_spec(back),
            whole_spec(cp.shape),
            whole_spec(sp.shape),
            whole_spec(hp.shape),
        ],
        out_specs=[
            rows_spec(2 * width + L, back),
            rows_spec(L, back),
            line_spec(back),
            line_spec(back),
            pl.BlockSpec((8, width), lambda i: (0, 0)),
            pl.BlockSpec((8, L), lambda i: (0, 0)),
            pl.BlockSpec((8, L), lambda i: (0, 0)),
        ],
        out_shape=[
            jax.ShapeDtypeStruct((tokens, 2 * width + L), bf16),
            jax.ShapeDtypeStruct((tokens, L), f32),
            jax.ShapeDtypeStruct((lines, 1, L), f32),
            jax.ShapeDtypeStruct((lines, 1, L), f32),
            jax.ShapeDtypeStruct((8, width), f32),
            jax.ShapeDtypeStruct((8, L), f32),
            jax.ShapeDtypeStruct((8, L), f32),
        ],
        scratch_shapes=[
            pltpu.VMEM((LB + 8, width + L), f32),
            pltpu.VMEM((8, width + L), f32),
            pltpu.VMEM((STATE, width), f32),
            pltpu.VMEM((STATE, width), f32),
        ],
        compiler_params=pltpu.CompilerParams(
            dimension_semantics=("arbitrary",), vmem_limit_bytes=VMEM_LIMIT
        ),
        name="mixer_bwd",
    )(lengths, gate, rest, rest, gs, y, st, gsum, gdot, cp, sp, hp)


def pack_params(conv_inner, conv_inner_bias, conv_shared, conv_shared_bias, step_bias, log_decay,
                skip_gain, gate_gain):
    width = conv_inner.shape[1]
    heads = step_bias.shape[0]
    skip = jnp.repeat(skip_gain, HEAD)
    cp = jnp.concatenate(
        [conv_inner, conv_inner_bias[None], skip[None], gate_gain[None], jnp.zeros((1, width), f32)],
        axis=0,
    )
    sp = jnp.concatenate([conv_shared, conv_shared_bias[None], jnp.zeros((3, L), f32)], axis=0)
    hp = jnp.zeros((8, L), f32)
    hp = hp.at[0, :heads].set(step_bias).at[1, :heads].set(-jnp.exp(log_decay))
    return cp, sp, hp


def exchange_kernel(axis, x_ref, out_ref, slots, send_sem, recv_sem):
    me = lax.axis_index(axis)
    n = slots.shape[0]
    barrier = pltpu.get_barrier_semaphore()
    for k in range(1, n):
        peer = lax.rem(me + k, n)
        pl.semaphore_signal(barrier, inc=1, device_id={axis: peer})
    pl.semaphore_wait(barrier, n - 1)
    copies = []
    for k in range(1, n):
        peer = lax.rem(me + k, n)
        copy = pltpu.make_async_remote_copy(
            src_ref=x_ref,
            dst_ref=slots.at[k],
            send_sem=send_sem.at[k],
            recv_sem=recv_sem.at[k],
            device_id={axis: peer},
        )
        copy.start()
        copies.append(copy)
    for copy in copies:
        copy.wait()
    slots[0] = x_ref[...]
    total = slots[lax.rem(me, n)]
    for d in range(1, n):
        total = total + slots[lax.rem(me - d + n, n)]
    out_ref[...] = total


def sum_small(x, axis, collective_id):
    n = lax.axis_size(axis)
    return pl.pallas_call(
        functools.partial(exchange_kernel, axis),
        out_shape=jax.ShapeDtypeStruct(x.shape, f32),
        in_specs=[pl.BlockSpec(memory_space=pltpu.VMEM)],
        out_specs=pl.BlockSpec(memory_space=pltpu.VMEM),
        scratch_shapes=[
            pltpu.VMEM((n,) + x.shape, f32),
            pltpu.SemaphoreType.DMA((n,)),
            pltpu.SemaphoreType.DMA((n,)),
        ],
        compiler_params=pltpu.CompilerParams(collective_id=collective_id, has_side_effects=True),
        name="sum_small",
    )(x)


def after(x, *deps):
    deps = [d for d in deps if d is not None]
    return lax.optimization_barrier((x, *deps))[0]


SCALE = 16384.0


def encode(x, bound, kind):
    if bound is not None:
        x = x * (SCALE / bound)
    return x.astype(kind)


def decode(x, bound):
    x = x.astype(f32)
    return x if bound is None else x * (bound / SCALE)


class ScatterLine:

    def __init__(self, send, own, bound, kind):
        self.n = lax.axis_size("heads")
        self.chips = self.n // 2
        self.z = lax.axis_index("heads") >> 1
        self.own, self.kind, self.bound = own, kind, bound
        self.moving, self.out = [None, None], [None, None]
        self.message = encode(send, bound, kind)

    def swap(self):
        pairs = [(i, i ^ 1) for i in range(self.n)]
        self.got = lax.ppermute(self.message, "heads", pairs)

    def block(self, b):
        mine = lax.dynamic_index_in_dim(self.own, b, 0, keepdims=False)
        theirs = lax.dynamic_index_in_dim(self.got, b, 0, keepdims=False)
        return mine + decode(theirs, self.bound)

    def pack(self, r):
        last = self.chips - 1
        for way in range(2):
            b = last - r + self.z if way == 0 else r - last + self.z
            total = self.block(jnp.clip(b, 0, last))
            if r > 0:
                total = total + decode(self.moving[way], self.bound)
            self.out[way] = encode(total, self.bound, self.kind)

    def hold(self, *deps):
        self.moving = [after(m, *deps) for m in self.moving]

    def send(self, r):
        last = self.chips - 1
        out = lax.optimization_barrier(tuple(self.out))
        for way in range(2):
            chips = range(r + 1) if way == 0 else range(last - r, last + 1)
            hop = 2 if way == 0 else -2
            pairs = [(2 * k + c, 2 * k + c + hop) for k in chips for c in range(2)]
            self.moving[way] = lax.ppermute(out[way], "heads", pairs)
        self.moving = list(lax.optimization_barrier(tuple(self.moving)))

    def rest(self, r):
        for k in range(r, self.chips - 1):
            self.pack(k)
            self.send(k)

    def total(self):
        total = self.block(self.z)
        for way in range(2):
            if self.moving[way] is not None:
                total = total + decode(self.moving[way], self.bound)
        return total


class RowSum:

    def __init__(self, x, bound):
        self.n = lax.axis_size("rows")
        self.me = lax.axis_index("rows")
        self.bits = self.n.bit_length() - 1
        self.shape, self.bound = x.shape, bound
        piece = x.shape[0] // (2 * self.n)
        cut = x.reshape((2,) + (2,) * self.bits + (piece, x.shape[1]))
        self.cur = [cut[0], cut[1]]
        self.order = [[(k + part) % self.bits for k in range(self.bits)] for part in range(2)]
        self.left = [list(range(self.bits))[::-1] for _ in range(2)]

    def pairs(self, bit):
        return [(i, i ^ (1 << bit)) for i in range(self.n)]

    def reduce(self):
        for k in range(self.bits):
            for part in range(2):
                bit, left = self.order[part][k], self.left[part]
                mine = (self.me >> bit) & 1
                axis = left.index(bit)
                left.remove(bit)
                cur = self.cur[part]
                send = lax.dynamic_index_in_dim(cur, 1 - mine, axis, keepdims=False)
                keep = lax.dynamic_index_in_dim(cur, mine, axis, keepdims=False)
                got = lax.ppermute(encode(send, self.bound, jnp.float16), "rows", self.pairs(bit))
                self.cur[part] = keep + decode(got, self.bound)

    def spread(self):
        mine = jnp.stack([encode(cur, self.bound, jnp.float16) for cur in self.cur])
        every = lax.all_gather(mine, "rows", axis=1, tiled=True)
        return decode(every.reshape(self.shape), self.bound)


def per_device(
    hidden_in, lengths, norm_gain, in_gate_inner, in_step, in_shared, conv_inner, conv_inner_bias,
    conv_shared, conv_shared_bias, step_bias, log_decay, skip_gain, gate_gain, out_weight, cotangent,
):
    tokens, local = hidden_in.shape
    full = in_gate_inner.shape[0]
    width = in_gate_inner.shape[2]
    heads = step_bias.shape[0]
    chips = full // local // 2
    lines = tokens // L
    inner_total = width * (full // local)
    core = lax.axis_index("heads") & 1
    source = hidden_in.astype(f32)

    hidden_all = lax.all_gather(hidden_in, "heads", axis=1, tiled=True)
    shared_all = lax.all_gather(in_shared, "heads", axis=1, tiled=True)
    gain_all = lax.all_gather(norm_gain, "heads", axis=0, tiled=True)
    cot_all = lax.all_gather(cotangent, "heads", axis=1, tiled=True)
    wgi = in_gate_inner.reshape(full, 2 * width)
    step_pad = jnp.pad(in_step, ((0, 0), (0, L - heads)))
    wss = jnp.concatenate([shared_all.T, step_pad], axis=1)
    w_back = jnp.concatenate([wgi, step_pad], axis=1)

    def halves(w, axis):
        both = []
        for side in (1 - core, core):
            parts = [
                lax.dynamic_slice_in_dim(w, (2 * k + side) * local, local, axis) for k in range(chips)
            ]
            both.append(jnp.stack(parts))
        return both

    back_send, back_own = halves(w_back, 0)
    out_send, out_own = halves(out_weight, 1)
    w_size = jnp.sqrt(jnp.max(jnp.sum(jnp.square(w_back.astype(f32)), axis=1)))
    cp, sp, hp = pack_params(
        conv_inner, conv_inner_bias, conv_shared, conv_shared_bias, step_bias, log_decay,
        skip_gain, gate_gain,
    )

    hidden_all = after(hidden_all, back_send, back_own, out_send, out_own, w_size, cp, sp, hp)
    normed, inv_rows, gate, rest, gated, y, st, gsum_part = run_fwd(
        lengths, hidden_all, gain_all[None], wgi, wss, cp, sp, hp
    )
    inv_rms = inv_rows.reshape(tokens)
    gsum = sum_small(gsum_part.reshape(lines, L), "heads", 1)

    live = (jnp.arange(tokens, dtype=jnp.int32) < jnp.sum(lengths[0])).astype(bf16)
    gate_rms = lax.rsqrt(gsum.reshape(tokens) / inner_total + EPSILON)
    scaled = (gated * gate_rms[:, None] * gate_gain[None, :]).astype(bf16) * live[:, None]

    def project(w, v, axis):
        return lax.dot_general(w, v, (((axis,), (1,)), ((), ())), preferred_element_type=f32)

    mixed = ScatterLine(
        project(out_send, scaled, 1), project(out_own, scaled, 1), None, jnp.float16
    )
    mixed.swap()
    mixed.pack(0)
    cot_late = after(cot_all, *mixed.out)
    mixed.send(0)
    gs, gdot_part = run_mid(lengths, cot_late, out_weight, gated, cp)
    gdot = sum_small(gdot_part.reshape(lines, L), "heads", 2)
    mixed.hold(gdot)
    mixed.pack(1)
    gdot = after(gdot, *mixed.out)
    mixed.send(1)

    low, gsh_part, nd_part, size, pg, sg, hg = run_bwd(
        inner_total, lengths, gate, rest, gs, y, st, gsum.reshape(lines, 1, L),
        gdot.reshape(lines, 1, L), cp, sp, hp,
    )
    bound = jnp.sqrt(size.reshape(lines, L)) * (1.01 * w_size) + 1e-30
    mixed.hold(low)
    small = sum_small(
        jnp.concatenate([nd_part.reshape(lines, L), bound, sg], axis=0), "heads", 3
    )
    norm_dot, sg = small[:lines].reshape(tokens), small[2 * lines :]
    bound = small[lines : 2 * lines].reshape(tokens)
    low = after(low, bound)

    normal = ScatterLine(project(back_send, low, 2), project(back_own, low, 2), bound, jnp.float16)
    normal.swap()
    normal.pack(0)
    low_late = after(low, *normal.out)
    scaled_late = after(scaled, *normal.out)
    normal.send(0)
    mixed.hold(*normal.out)
    mixed.rest(2)
    output = (source + mixed.total().T).astype(bf16)

    grad_proj = lax.dot_general(
        normed, low_late, (((0,), (0,)), ((), ())), preferred_element_type=f32
    )
    top_proj = jnp.max(jnp.abs(grad_proj))
    grad_wout = lax.dot_general(
        scaled_late, cot_all, (((0,), (0,)), ((), ())), preferred_element_type=f32
    )
    top_wout = jnp.max(jnp.abs(grad_wout))
    tops = jnp.stack([top_proj, top_wout])
    tops = jnp.broadcast_to(jnp.repeat(tops * 1.01 + 1e-30, 8)[:, None], (16, L))
    wide = pg.reshape(8 * width // L, L)
    small = sum_small(jnp.concatenate([tops, sg, hg, wide], axis=0), "rows", 4)
    top_proj, top_wout, sg, hg = small[0, 0], small[8, 0], small[16:24], small[24:32]
    pg = small[32:].reshape(8, width)
    sum_proj, sum_wout = RowSum(grad_proj, top_proj), RowSum(grad_wout, top_wout)
    sum_proj.reduce()
    sum_wout.reduce()

    cut = gsh_part.T.reshape(chips, 2, L // (2 * chips), tokens)
    gsh_own = lax.dynamic_index_in_dim(cut, core, 1, keepdims=False)
    gsh_send = lax.dynamic_index_in_dim(cut, 1 - core, 1, keepdims=False)
    shared = ScatterLine(gsh_send, gsh_own, None, f32)
    shared.swap()
    shared.rest(0)
    low_shared = lax.all_gather(shared.total().astype(bf16), "heads", axis=0, tiled=True)
    shared_raw = rest[:, width : width + L]
    norm_dot = norm_dot + jnp.sum(low_shared.T.astype(f32) * shared_raw, axis=1)
    grad_proj, grad_step = unpack(sum_proj.spread(), width, heads)
    grad_wout = sum_wout.spread()
    normed_local = (source * inv_rms[:, None] * norm_gain[None, :]).astype(bf16)
    grad_shared_w = lax.dot_general(
        low_shared, normed_local, (((1,), (0,)), ((), ())), preferred_element_type=f32
    )
    grad_shared_w = lax.psum(grad_shared_w, "rows")

    normal.rest(1)
    grad_normed = normal.total() + lax.dot_general(
        in_shared, low_shared, (((0,), (0,)), ((), ())), preferred_element_type=f32
    )
    grad_normed = grad_normed.T
    grad_gain_norm = jnp.sum(grad_normed * source * inv_rms[:, None], axis=0)
    grad_source = (
        inv_rms[:, None] * norm_gain[None, :] * grad_normed
        - source * (inv_rms * inv_rms * norm_dot / full)[:, None]
    )
    grad_input = cotangent.astype(f32) + grad_source
    grad_gain_norm = sum_small(grad_gain_norm.reshape(local // L, L), "rows", 5).reshape(local)
    return (
        output,
        grad_input,
        grad_gain_norm,
        grad_proj,
        grad_step,
        grad_shared_w,
        pg[0:4],
        pg[4],
        sg[0:4],
        sg[4],
        hg[0, :heads],
        hg[1, :heads],
        pg[5].reshape(heads, HEAD).sum(axis=1),
        pg[6],
        grad_wout,
    )


def solution(mesh):
    return jax.shard_map(
        per_device,
        mesh=mesh,
        in_specs=(
            P("rows", "heads"), P("rows", None), P("heads"), P(None, None, "heads"),
            P(None, "heads"), P(None, "heads"), P(None, "heads"), P("heads"), P(), P(),
            P("heads"), P("heads"), P("heads"), P("heads"), P("heads", None), P("rows", "heads"),
        ),
        out_specs=(
            P("rows", "heads"), P("rows", "heads"), P("heads"), P(None, None, "heads"),
            P(None, "heads"), P(None, "heads"), P(None, "heads"), P("heads"), P(), P(),
            P("heads"), P("heads"), P("heads"), P("heads"), P("heads", None),
        ),
        check_vma=False,
    )
```

time: 2680 us -> 943 us (0.35)
  waiting for transfers between devices: 810 us -> 225 us
  matrix products: 620 us -> 104 us
  other arithmetic: 510 us -> 99.5 us
  local copies, waits for them, and re-layouts: 446 us -> 44 us
  Pallas kernels: 0 us -> 245 us
  blocking collectives: 235 us -> 116 us
  starting transfers between devices: 0.2 us -> 82.4 us
    dot_general x236 -> x8, matrix products: 620 us -> 104 us  [the longest x4 47.7 us: project(): lax.dot_general(w, v, (((axis,), (1,)), ((), ())), preferred_element_type...]
    reduce_scatter x2 -> x0, waiting for transfers between devices: 444 us -> none  [the longest x1 277 us: per_device(): lax.psum_scatter(lax.dot_general(w_block, scaled, (((0,), (1,)), ((), ())...]
    pallas_call x0 -> x9, Pallas kernels: none -> 245 us  [the longest x1 89.8 us: run_bwd(): pl.pallas_call(functools.partial(bwd_kernel, float(inner_total)), grid=(b...]
    psum x1, waiting for transfers between devices: 236 us -> 0.02 us  [per_device(): grad_shared_w = lax.psum(grad_shared_w, 'rows')]
    psum x6 -> x0, blocking collectives: 218 us -> none  [the longest x1 91.1 us: per_device(): lax.psum((grad_shared_part, grad_kernel_part, grad_bias_part), 'heads')]
    another operation x131 -> x9, other arithmetic: 131 us -> 7.98 us  [the longest x2 5.82 us: halves(): both.append(jnp.stack(parts))]
    mul x117 -> x3, other arithmetic: 132 us -> 11 us  [the longest x2 6.8 us: decode(): return x if bound is None else x * (bound / SCALE)]
    ppermute x0 -> x29, waiting for transfers between devices: none -> 112 us  [the longest x18 80.1 us: send(): self.moving[way] = lax.ppermute(out[way], 'heads', pairs)]
  transfers between devices with their start and end apart: 5 -> 33, of which waited for: 4 -> 10; matrix products, arithmetic and copies ran while one was open for 20% -> 23% of each run, Pallas kernels for 0% -> 15%
where the time goes in v1:
time: 943 us; the launch traced here: 934 us
  Pallas kernels  245 us (26%)
  waiting for transfers between devices  225 us (24%)
  blocking collectives  116 us (12%)
  matrix products  104 us (11%)
  other arithmetic  99.5 us (11%)
  starting transfers between devices  82.4 us (9%)
  local copies, waits for them, and re-layouts  44 us (5%)
  between operations  18.7 us (2%)
    pallas_call x1, Pallas kernels, run_bwd(): pl.pallas_call(functools.partial(bwd_kernel, float(inner_total)), grid=(b...  89.8 us
    all_gather x1, waiting for transfers between devices, per_device(): hidden_all = lax.all_gather(hidden_in, 'heads', axis=1, tiled=True)  87.3 us
    pallas_call x1, Pallas kernels, run_fwd(): pl.pallas_call(fwd_kernel, grid=(tokens // LB,), in_specs=[smem_spec(), r...  80.4 us
    ppermute x18, waiting for transfers between devices, send(): self.moving[way] = lax.ppermute(out[way], 'heads', pairs)  80.1 us
    ppermute x18, starting transfers between devices, send(): self.moving[way] = lax.ppermute(out[way], 'heads', pairs)  59.7 us
    all_gather x2, blocking collectives, spread(): every = lax.all_gather(mine, 'rows', axis=1, tiled=True)  58.2 us
    convert_element_type x14, other arithmetic, encode(): return x.astype(kind)  54.8 us
    dot_general x4, matrix products, project(): lax.dot_general(w, v, (((axis,), (1,)), ((), ())), preferred_element_type...  47.7 us
  transfers between devices with their start and end apart: 33, of which 10 were waited for; matrix products, arithmetic and copies ran while one was open for 23% of the time, Pallas kernels for 15%

profile of v1, /device:TPU:0, one launch (start us, length us, event | category | flops | bytes accessed | tf_op | source)
XLA Modules:
  0.0 934.0 jit_solution(17172343005396310940)
XLA Ops:
  22.7 14.4 %all-gather = f32[8,1,256]{2,1,0:T(1,128)} all-gather(f32[1,1,256]{2,1,0:T(1,128)S(1)} %bitcast.343), channel_id=1, replica_groups=mesh['rows'=4,'heads'=8] {'heads'}, dimensions={0}, use_global_device_ids=true | all-gather | bytes 9216 | tf_op jit(solution)/shard_map/all_gather | solution.py:760
  38.4 43.0 %all_gather.23 = bf16[128,2048]{0,1:T(8,128)(2,1)S(1)} all-gather(bf16[128,256]{0,1:T(8,128)(2,1)S(1)} %copy.94), channel_id=1, replica_groups=mesh['rows'=4,'heads'=8] {'heads'}, dimensions={1}, use_global_device_ids=true | all-gather | bytes 589824 | tf_op jit(solution)/shard_map/all_gather | solution.py:759
  82.5 87.3 %all-gather.7.cloned.1.call-done.h_ref = bf16[4096,2048]{1,0:T(8,128)(2,1)} async-done(((bf16[4096,256]{1,0:T(8,128)(2,1)}), bf16[4096,2048]{1,0:T(8,128)(2,1)}) %all-gather.7.cloned.1.call-update) | async-done | bytes 16777232 | tf_op jit(solution)/shard_map/all_gather | solution.py:758
  169.8 80.4 %mixer_fwd.1 = (bf16[4096,2048]{1,0:T(8,128)(2,1)}, f32[32,1,128]{2,1,0:T(1,128)}, f32[4096,512]{1,0:T(8,128)}, f32[4096,768]{1,0:T(8,128)}, f32[4096,512]{1,0:T...) custom-call(s32[1,4]{1,0:T(1,128)} %len_ref.5, ...), custom_call_target="tpu_custom_call" | custom-call | tf_op jit(solution)/shard_map/mixer_fwd/pallas_call | solution.py:442
  271.0 13.7 %collective-permute-start = (f16[4,256,4096]{2,1,0:T(8,128)(2,1)}, f16[4,256,4096]{2,1,0:T(8,128)(2,1)}, u32[]{:S(2)}, u32[]{:S(2)}) collective-permute-start(f16[4,256,4096]{2,1,0:T(8,128)(2,1)} %convolution_convert_fusion), channel_id=1, source_target_pairs={{0,1},{1,0},{2,3},{3,2},{4,5},{5,4},{6,7},{7,6},{8,9},{9,8},{10,11... | collective-permute-start | bytes 25165832 | tf_op jit(solution)/shard_map/ppermute | solution.py:667
  312.3 23.6 %all-gather.9.cloned.1.call-done.cot_ref = bf16[4096,2048]{1,0:T(8,128)(2,1)} async-done(((bf16[4096,256]{1,0:T(8,128)(2,1)}), bf16[4096,2048]{1,0:T(8,128)(2,1)}) %all-gather.9.cloned.1.call-update) | async-done | bytes 16777232 | tf_op jit(solution)/shard_map/all_gather | solution.py:761
  335.9 17.3 %mixer_mid.1 = (f32[4096,512]{1,0:T(8,128)}, f32[32,1,128]{2,1,0:T(1,128)}) custom-call(s32[1,4]{1,0:T(1,128)} %len_ref.5, bf16[4096,2048]{1,0:T(8,128)(2,1)} %all-gather.9.cloned.1.call-done.cot_ref, bf16[512,2048]{1,0:T(8,128)(2,1)} %w_ref.1, f32[4096,512]{1,0:T(8,128)} %get-tuple-element.106.gated_ref, f32[8,512]{1,0:T(8,128)} %concatenate.23.cp_ref), custom_call_target="tpu_custom_call" | custom-call | tf_op jit(solution)/shard_map/mixer_mid/pallas_call | solution.py:494
  353.2 15.1 %sum_small.6 = f32[32,128]{1,0:T(8,128)} custom-call(f32[32,128]{1,0:T(8,128)} %bitcast.340), custom_call_target="tpu_custom_call" | custom-call | tf_op jit(solution)/shard_map/sum_small/pallas_call | solution.py:621
  368.4 10.5 %fusion.42 = (f16[256,4096]{1,0:T(8,128)(2,1)}, f16[256,4096]{1,0:T(8,128)(2,1)}) fusion(f16[256,4096]{1,0:T(8,128)(2,1)} %collective-permute-done.2, f32[4,256,4096]{2,1,0:T(8,128)} %copy-done, s32[]{:T(128)S(6)} %min.47, f16[4,256,4096]{2,1,0:T(8,128)(2,1)} %collective-permute-done, f16[256,4096]{1,0:T(8,128)(2,1)} %collective-permute-done.1, s32[]{:T(128)S(6)} %min.44), kind=kLoop, calls=%fused_computation.69 | loop fusion | flops 10485760 | bytes 20971528 | tf_op jit(solution)/shard_map/convert_element_type | solution.py:647
  378.8 89.8 %mixer_bwd.1 = (bf16[4096,1152]{1,0:T(8,128)(2,1)}, f32[4096,128]{1,0:T(8,128)}, f32[32,1,128]{2,1,0:T(1,128)}, f32[32,1,128]{2,1,0:T(1,128)}, f32[8,512]{1,0:T(...) custom-call(s32[1,4]{1,0:T(1,128)} %len_ref.5, f32[4096,512]{1,0:T(8,128)} %get-tuple-element.119.gate_ref, ...), custom_call_target="tpu_custom_call" | custom-call | tf_op jit(solution)/shard_map/mixer_bwd/pallas_call | solution.py:527
  470.8 11.0 %sum_small.7 = f32[72,128]{1,0:T(8,128)} custom-call(f32[72,128]{1,0:T(8,128)} %pad_maximum_fusion.8.x_ref), custom_call_target="tpu_custom_call" | custom-call | tf_op jit(solution)/shard_map/sum_small/pallas_call | solution.py:621
  482.5 16.8 %multiply_convert_fusion = f16[4,256,4096]{2,1,0:T(8,128)(2,1)} fusion(bf16[4096,1152]{1,0:T(8,128)(2,1)} %get-tuple-element.165, f32[4096]{0:T(1024)S(1)} %get-tuple-element.258, bf16[1,256,1152]{2,1,0:T(8,128)(2,1)S(1)} %copy-done.24, bf16[1,256,1152]{2,1,0:T(8,128)(2,1)S(1)} %copy-done.23, bf16[1,256,1152]{2,1,0:T(8,128)(2,1)S(1)} %copy-done.22, ...), kind=kOutput, calls=%fused_computation.9 | convolution fusion | flops 9675603968 | bytes 20201472 | tf_op jit(solution)/shard_map/dot_general | solution.py:796
  502.9 11.6 %collective-permute-done.14 = f32[4,16,4096]{2,1,0:T(8,128)} collective-permute-done((f32[4,16,4096]{2,1,0:T(8,128)}, f32[4,16,4096]{2,1,0:T(8,128)}, u32[]{:S(2)}, u32[]{:S(2)}) %collective-permute-start.14) | collective-permute-done | bytes 1048608 | tf_op jit(solution)/shard_map/ppermute | solution.py:667
  560.9 17.7 %fusion.2 = f32[4,256,4096]{2,1,0:T(8,128)} fusion(bf16[4096,1152]{1,0:T(8,128)(2,1)} %get-tuple-element.165, bf16[1,256,1152]{2,1,0:T(8,128)(2,1)} %get-tuple-element.239, bf16[1,256,1152]{2,1,0:T(8,128)(2,1)} %get-tuple-element.238, bf16[1,256,1152]{2,1,0:T(8,128)(2,1)} %get-tuple-element.237, bf16[1,256,1152]{2,1,0:T(8,128)(2,1)} %get-tuple-element.236), kind=kOutput, calls=%fused_computation.12 | convolution fusion | flops 9667215360 | bytes 28573696 | tf_op jit(solution)/shard_map/dot_general | solution.py:796
  578.6 29.6 %collective-permute-done.3 = f16[256,4096]{1,0:T(8,128)(2,1)} collective-permute-done((f16[256,4096]{1,0:T(8,128)(2,1)}, f16[256,4096]{1,0:T(8,128)(2,1)}, u32[]{:S(2)}, u32[]{:S(2)}) %collective-permute-start.3) | collective-permute-done | bytes 2097184 | tf_op jit(solution)/shard_map/ppermute | solution.py:693
  622.8 30.0 %abs_reduce_fusion = (f32[]{:T(128)}, f32[2048,1152]{1,0:T(8,128)}) fusion(bf16[4096,2048]{1,0:T(8,128)(2,1)} %get-tuple-element.164, bf16[4096,1152]{1,0:T(8,128)(2,1)} %get-tuple-element.165), kind=kOutput, calls=%fused_computation.15 | convolution fusion | flops 19332071424 | bytes 35651588 | tf_op jit(solution)/shard_map/dot_general | solution.py:835
  652.9 11.1 %abs_reduce_fusion.1 = (f32[]{:T(128)}, f32[512,2048]{1,0:T(8,128)}) fusion(bf16[4096,512]{1,0:T(8,128)(2,1)S(1)} %copy-done.16, bf16[4096,2048]{1,0:T(8,128)(2,1)S(1)} %bitcast.310), kind=kOutput, calls=%fused_computation.80 | convolution fusion | flops 8592031744 | bytes 25165828 | tf_op jit(solution)/shard_map/dot_general | solution.py:839
  692.7 9.4 %collective-permute-start.8 = (f16[256,4096]{1,0:T(8,128)(2,1)S(1)}, f16[256,4096]{1,0:T(8,128)(2,1)}, u32[]{:S(2)}, u32[]{:S(2)}) collective-permute-start(f16[256,4096]{1,0:T(8,128)(2,1)S(1)} %copy-done.18), channel_id=1, source_target_pairs={{0,2},{1,3},{8,10},{9,11},{16,18},{17,19},{24,26},{25,27}} | collective-permute-start | bytes 6291464 | tf_op jit(solution)/shard_map/ppermute | solution.py:693
  702.1 10.6 %fusion.41 = (f16[256,4096]{1,0:T(8,128)(2,1)}, f16[256,4096]{1,0:T(8,128)(2,1)}) fusion(f16[256,4096]{1,0:T(8,128)(2,1)} %collective-permute-done.4, f32[4,256,4096]{2,1,0:T(8,128)} %copy-done, s32[]{:T(128)S(6)} %min.48, f16[4,256,4096]{2,1,0:T(8,128)(2,1)} %collective-permute-done, f16[256,4096]{1,0:T(8,128)(2,1)} %collective-permute-done.3, s32[]{:T(128)S(6)} %min.43), kind=kLoop, calls=%fused_computation.67 | loop fusion | flops 10485760 | bytes 20971528 | tf_op jit(solution)/shard_map/convert_element_type | solution.py:647
  740.6 21.5 %all-gather.12 = f16[2,256,2048]{2,1,0:T(8,128)(2,1)S(1)} all-gather(f16[2,64,2048]{2,1,0:T(8,128)(2,1)S(1)} %pad_maximum_fusion.7), channel_id=1, replica_groups=mesh['rows'=4,'heads'=8] {'rows'}, dimensions={1}, use_global_device_ids=true | all-gather | bytes 2621440 | tf_op jit(solution)/shard_map/all_gather | solution.py:740
  785.8 45.8 %collective-permute-done.10 = f16[256,4096]{1,0:T(8,128)(2,1)S(1)} collective-permute-done((f16[256,4096]{1,0:T(8,128)(2,1)S(1)}, f16[256,4096]{1,0:T(8,128)(2,1)S(1)}, u32[]{:S(2)}, u32[]{:S(2)}) %collective-permute-start.10) | collective-permute-done | bytes 2097184 | tf_op jit(solution)/shard_map/ppermute | solution.py:693
  844.5 36.7 %all-gather.13 = f16[2,1024,1152]{2,1,0:T(8,128)(2,1)S(1)} all-gather(f16[2,256,1152]{2,1,0:T(8,128)(2,1)S(1)} %pad_maximum_fusion.3), channel_id=1, replica_groups=mesh['rows'=4,'heads'=8] {'rows'}, dimensions={1}, use_global_device_ids=true | all-gather | bytes 5898240 | tf_op jit(solution)/shard_map/all_gather | solution.py:740
  885.5 10.2 %unpack.1 = (f32[2048,2,512]{2,1,0:T(2,128)}, f32[2048,8]{1,0:T(8,128)}) custom-call(f32[2048,1152]{1,0:T(8,128)} %bitcast.302), custom_call_target="tpu_custom_call" | custom-call | tf_op jit(solution)/shard_map/unpack/pallas_call | solution.py:399
  897.8 12.4 %fusion.12 = (f32[256]{0:T(256)}, f32[4096,256]{0,1:T(8,128)}, bf16[4096,256]{0,1:T(8,128)(2,1)}) fusion(bf16[4096,256]{0,1:T(8,128)(2,1)S(1)} %copy-done.6, f32[4096]{0:T(1024)S(1)} %bitcast.336, f32[4096]{0:T(1024)S(1)} %fusion.102, f32[256]{0:T(256)S(1)} %copy-done.40, bf16[4096,256]{0,1:T(8,128)(2,1)} %copy.96, ...), kind=kOutput, calls=%fused_computation.30 | convolution fusion | flops 297795328 | bytes 32622596 | tf_op jit(solution)/shard_map/dot_general | solution.py:871
  (282 shorter events, 246.0 us)
Async XLA Ops:
  7.2 162.7 %all-gather.7.cloned.1.call-start = ((), (), s32[]{:S(2)}) async-start(), calls=%async_computation | async-start | bytes 18874368 | tf_op jit(solution)/shard_map/all_gather | solution.py:758
  7.9 328.0 %all-gather.9.cloned.1.call-start = ((), (), s32[]{:S(2)}) async-start(), calls=%async_computation.1 | async-start | bytes 18874368 | tf_op jit(solution)/shard_map/all_gather | solution.py:761
  8.7 599.5 %all-gather.11.cloned.1.call-start = ((), (), s32[]{:S(2)}) async-start(), calls=%async_computation.2 | async-start | bytes 1179648 | tf_op jit(solution)/shard_map/all_gather | solution.py:859
  271.0 26.8 %collective-permute-start = (f16[4,256,4096]{2,1,0:T(8,128)(2,1)}, f16[4,256,4096]{2,1,0:T(8,128)(2,1)}, u32[]{:S(2)}, u32[]{:S(2)}) collective-permute-start(f16[4,256,4096]{2,1,0:T(8,128)(2,1)} %convolution_convert_fusion), channel_id=1, source_target_pairs={{0,1},{1,0},{2,3},{3,2},{4,5},{5,4},{6,7},{7,6},{8,9},{9,8},{10,11... | collective-permute-start | bytes 25165832 | tf_op jit(solution)/shard_map/ppermute | solution.py:667
  303.8 64.6 %collective-permute-start.1 = (f16[256,4096]{1,0:T(8,128)(2,1)}, f16[256,4096]{1,0:T(8,128)(2,1)}, u32[]{:S(2)}, u32[]{:S(2)}) collective-permute-start(f16[256,4096]{1,0:T(8,128)(2,1)} %get-tuple-element.108), channel_id=1, source_target_pairs={{0,2},{1,3},{8,10},{9,11},{16,18},{17,19},{24,26},{25,27}} | collective-permute-start | bytes 6291464 | tf_op jit(solution)/shard_map/ppermute | solution.py:693
  306.4 61.9 %collective-permute-start.2 = (f16[256,4096]{1,0:T(8,128)(2,1)S(1)}, f16[256,4096]{1,0:T(8,128)(2,1)}, u32[]{:S(2)}, u32[]{:S(2)}) collective-permute-start(f16[256,4096]{1,0:T(8,128)(2,1)S(1)} %get-tuple-element.109), channel_id=1, source_target_pairs={{6,4},{7,5},{14,12},{15,13},{22,20},{23,21},{30,28},{31,29}} | collective-permute-start | bytes 6291464 | tf_op jit(solution)/shard_map/ppermute | solution.py:693
  499.3 114.8 %collective-permute-start.5 = (f16[4,256,4096]{2,1,0:T(8,128)(2,1)}, f16[4,256,4096]{2,1,0:T(8,128)(2,1)}, u32[]{:S(2)}, u32[]{:S(2)}) collective-permute-start(f16[4,256,4096]{2,1,0:T(8,128)(2,1)} %multiply_convert_fusion), channel_id=1, source_target_pairs={{0,1},{1,0},{2,3},{3,2},{4,5},{5,4},{6,7},{7,6},{8,9},{9,8},{10,11... | collective-permute-start | bytes 25165832 | tf_op jit(solution)/shard_map/ppermute | solution.py:667
  543.5 15.5 %collective-permute-start.19 = (f32[16,4096]{1,0:T(8,128)}, f32[16,4096]{1,0:T(8,128)S(1)}, u32[]{:S(2)}, u32[]{:S(2)}) collective-permute-start(f32[16,4096]{1,0:T(8,128)} %get-tuple-element.160), channel_id=1, source_target_pairs={{0,2},{1,3},{2,4},{3,5},{4,6},{5,7},{8,10},{9,11},{10,12},{11,13},... | collective-permute-start | bytes 786440 | tf_op jit(solution)/shard_map/ppermute | solution.py:693
  550.6 57.6 %collective-permute-start.3 = (f16[256,4096]{1,0:T(8,128)(2,1)}, f16[256,4096]{1,0:T(8,128)(2,1)}, u32[]{:S(2)}, u32[]{:S(2)}) collective-permute-start(f16[256,4096]{1,0:T(8,128)(2,1)} %get-tuple-element.116), channel_id=1, source_target_pairs={{0,2},{1,3},{2,4},{3,5},{8,10},{9,11},{10,12},{11,13},{16,18},{17,... | collective-permute-start | bytes 6291464 | tf_op jit(solution)/shard_map/ppermute | solution.py:693
  557.0 51.2 %collective-permute-start.4 = (f16[256,4096]{1,0:T(8,128)(2,1)}, f16[256,4096]{1,0:T(8,128)(2,1)}, u32[]{:S(2)}, u32[]{:S(2)}) collective-permute-start(f16[256,4096]{1,0:T(8,128)(2,1)} %get-tuple-element.117), channel_id=1, source_target_pairs={{4,2},{5,3},{6,4},{7,5},{12,10},{13,11},{14,12},{15,13},{20,18},{2... | collective-permute-start | bytes 6291464 | tf_op jit(solution)/shard_map/ppermute | solution.py:693
  560.7 363.6 %all-reduce.4.cloned.1.call-start = ((), (), s32[]{:S(2)}) async-start(), calls=%async_computation.3 | async-start | bytes 262144 | tf_op jit(solution)/shard_map/psum | solution.py:868
  681.6 32.2 %collective-permute-start.25 = (f16[2,64,2048]{2,1,0:T(8,128)(2,1)}, f16[2,64,2048]{2,1,0:T(8,128)(2,1)}, u32[]{:S(2)}, u32[]{:S(2)}) collective-permute-start(f16[2,64,2048]{2,1,0:T(8,128)(2,1)} %fusion.85), channel_id=1, source_target_pairs={{0,8},{8,0},{16,24},{24,16},{1,9},{9,1},{17,25},{25,17},{2,10},{10... | collective-permute-start | bytes 1572872 | tf_op jit(solution)/shard_map/ppermute | solution.py:735
  683.9 33.1 %collective-permute-start.27 = (f16[2,64,2048]{2,1,0:T(8,128)(2,1)}, f16[2,64,2048]{2,1,0:T(8,128)(2,1)}, u32[]{:S(2)}, u32[]{:S(2)}) collective-permute-start(f16[2,64,2048]{2,1,0:T(8,128)(2,1)} %fusion.84), channel_id=1, source_target_pairs={{0,16},{8,24},{16,0},{24,8},{1,17},{9,25},{17,1},{25,9},{2,18},{10... | collective-permute-start | bytes 1572872 | tf_op jit(solution)/shard_map/ppermute | solution.py:735
  687.2 74.8 %collective-permute-start.21 = (f16[2,256,1152]{2,1,0:T(8,128)(2,1)}, f16[2,256,1152]{2,1,0:T(8,128)(2,1)}, u32[]{:S(2)}, u32[]{:S(2)}) collective-permute-start(f16[2,256,1152]{2,1,0:T(8,128)(2,1)} %fusion.58), channel_id=1, source_target_pairs={{0,8},{8,0},{16,24},{24,16},{1,9},{9,1},{17,25},{25,17},{2,10},{10... | collective-permute-start | bytes 3538952 | tf_op jit(solution)/shard_map/ppermute | solution.py:735
  690.5 84.6 %collective-permute-start.23 = (f16[2,256,1152]{2,1,0:T(8,128)(2,1)}, f16[2,256,1152]{2,1,0:T(8,128)(2,1)S(1)}, u32[]{:S(2)}, u32[]{:S(2)}) collective-permute-start(f16[2,256,1152]{2,1,0:T(8,128)(2,1)} %fusion.57), channel_id=1, source_target_pairs={{0,16},{8,24},{16,0},{24,8},{1,17},{9,25},{17,1},{25,9},{2,18},{10... | collective-permute-start | bytes 3538952 | tf_op jit(solution)/shard_map/ppermute | solution.py:735
  692.7 71.9 %collective-permute-start.8 = (f16[256,4096]{1,0:T(8,128)(2,1)S(1)}, f16[256,4096]{1,0:T(8,128)(2,1)}, u32[]{:S(2)}, u32[]{:S(2)}) collective-permute-start(f16[256,4096]{1,0:T(8,128)(2,1)S(1)} %copy-done.18), channel_id=1, source_target_pairs={{0,2},{1,3},{8,10},{9,11},{16,18},{17,19},{24,26},{25,27}} | collective-permute-start | bytes 6291464 | tf_op jit(solution)/shard_map/ppermute | solution.py:693
  713.7 50.9 %collective-permute-start.9 = (f16[256,4096]{1,0:T(8,128)(2,1)S(1)}, f16[256,4096]{1,0:T(8,128)(2,1)}, u32[]{:S(2)}, u32[]{:S(2)}) collective-permute-start(f16[256,4096]{1,0:T(8,128)(2,1)S(1)} %copy-done.17), channel_id=1, source_target_pairs={{6,4},{7,5},{14,12},{15,13},{22,20},{23,21},{30,28},{31,29}} | collective-permute-start | bytes 6291464 | tf_op jit(solution)/shard_map/ppermute | solution.py:693
  731.8 166.0 %collective-permute-start.6 = (f16[256,4096]{1,0:T(8,128)(2,1)}, f16[256,4096]{1,0:T(8,128)(2,1)}, u32[]{:S(2)}, u32[]{:S(2)}) collective-permute-start(f16[256,4096]{1,0:T(8,128)(2,1)} %get-tuple-element.134), channel_id=1, source_target_pairs={{0,2},{1,3},{2,4},{3,5},{4,6},{5,7},{8,10},{9,11},{10,12},{11,13},... | collective-permute-start | bytes 6291464 | tf_op jit(solution)/shard_map/ppermute | solution.py:693
  764.6 15.1 %collective-permute-start.22 = (f16[256,1152]{1,0:T(8,128)(2,1)}, f16[256,1152]{1,0:T(8,128)(2,1)}, u32[]{:S(2)}, u32[]{:S(2)}) collective-permute-start(f16[256,1152]{1,0:T(8,128)(2,1)} %fusion.72), channel_id=1, source_target_pairs={{0,16},{8,24},{16,0},{24,8},{1,17},{9,25},{17,1},{25,9},{2,18},{10... | collective-permute-start | bytes 1769480 | tf_op jit(solution)/shard_map/ppermute | solution.py:735
  772.4 59.2 %collective-permute-start.10 = (f16[256,4096]{1,0:T(8,128)(2,1)S(1)}, f16[256,4096]{1,0:T(8,128)(2,1)S(1)}, u32[]{:S(2)}, u32[]{:S(2)}) collective-permute-start(f16[256,4096]{1,0:T(8,128)(2,1)S(1)} %get-tuple-element.143), channel_id=1, source_target_pairs={{0,2},{1,3},{2,4},{3,5},{8,10},{9,11},{10,12},{11,13},{16,18},{17,... | collective-permute-start | bytes 6291464 | tf_op jit(solution)/shard_map/ppermute | solution.py:693
  774.1 57.5 %collective-permute-start.11 = (f16[256,4096]{1,0:T(8,128)(2,1)S(1)}, f16[256,4096]{1,0:T(8,128)(2,1)S(1)}, u32[]{:S(2)}, u32[]{:S(2)}) collective-permute-start(f16[256,4096]{1,0:T(8,128)(2,1)S(1)} %get-tuple-element.144), channel_id=1, source_target_pairs={{4,2},{5,3},{6,4},{7,5},{12,10},{13,11},{14,12},{15,13},{20,18},{2... | collective-permute-start | bytes 6291464 | tf_op jit(solution)/shard_map/ppermute | solution.py:693
  779.8 118.0 %collective-permute-start.7 = (f16[256,4096]{1,0:T(8,128)(2,1)}, f16[256,4096]{1,0:T(8,128)(2,1)}, u32[]{:S(2)}, u32[]{:S(2)}) collective-permute-start(f16[256,4096]{1,0:T(8,128)(2,1)} %get-tuple-element.135), channel_id=1, source_target_pairs={{2,0},{3,1},{4,2},{5,3},{6,4},{7,5},{10,8},{11,9},{12,10},{13,11},... | collective-permute-start | bytes 6291464 | tf_op jit(solution)/shard_map/ppermute | solution.py:693
  837.2 60.6 %collective-permute-start.12 = (f16[256,4096]{1,0:T(8,128)(2,1)}, f16[256,4096]{1,0:T(8,128)(2,1)}, u32[]{:S(2)}, u32[]{:S(2)}) collective-permute-start(f16[256,4096]{1,0:T(8,128)(2,1)} %get-tuple-element.147), channel_id=1, source_target_pairs={{0,2},{1,3},{2,4},{3,5},{4,6},{5,7},{8,10},{9,11},{10,12},{11,13},... | collective-permute-start | bytes 6291464 | tf_op jit(solution)/shard_map/ppermute | solution.py:693
  842.9 54.9 %collective-permute-start.13 = (f16[256,4096]{1,0:T(8,128)(2,1)}, f16[256,4096]{1,0:T(8,128)(2,1)}, u32[]{:S(2)}, u32[]{:S(2)}) collective-permute-start(f16[256,4096]{1,0:T(8,128)(2,1)} %get-tuple-element.148), channel_id=1, source_target_pairs={{2,0},{3,1},{4,2},{5,3},{6,4},{7,5},{10,8},{11,9},{12,10},{13,11},... | collective-permute-start | bytes 6291464 | tf_op jit(solution)/shard_map/ppermute | solution.py:693
  (69 other events, 1555.7 us)
Sparse Core Ops, SparseCore 0:
  9.6 160.2 all-gather.6
  171.4 164.4 all-gather.8
  560.8 27.5 all-gather.10
  611.3 45.5 all-reduce.3

commit v2 on v1

--- a/solution.py
+++ b/solution.py
@@ -387,29 +387,35 @@
     lax.fori_loop(0, NSUB, chunk, 0)
 
 
-def unpack_kernel(x_ref, gate_inner_ref, step_ref):
+def unpack_kernel(me_ref, x_ref, gate_inner_ref, step_ref):
     width = gate_inner_ref.shape[2]
-    gate_inner_ref[:, 0, :] = x_ref[:, :width]
-    gate_inner_ref[:, 1, :] = x_ref[:, width : 2 * width]
-    step_ref[...] = x_ref[:, 2 * width : 2 * width + step_ref.shape[1]]
-
-
-def unpack(x, width, heads):
-    rows = x.shape[0]
+    gate_inner_ref[:, 0, :] = x_ref[0, 0, :, :width]
+    gate_inner_ref[:, 1, :] = x_ref[0, 0, :, width : 2 * width]
+    step_ref[...] = x_ref[0, 0, :, 2 * width : 2 * width + step_ref.shape[1]]
+
+
+def place_kernel(me_ref, x_ref, out_ref):
+    out_ref[...] = x_ref[0, 0]
+
+
+def place(x, kernel, shapes):
+    _, n, piece, cols = x.shape
+
+    def spec(shape):
+        zeros = (0,) * (len(shape) - 1)
+        return pl.BlockSpec((piece,) + shape[1:], lambda p, k, me: (p * n + (me[0] ^ k),) + zeros)
+
     return pl.pallas_call(
-        unpack_kernel,
-        grid=(rows // 256,),
-        in_specs=[pl.BlockSpec((256, x.shape[1]), lambda i: (i, 0))],
-        out_specs=[
-            pl.BlockSpec((256, 2, width), lambda i: (i, 0, 0)),
-            pl.BlockSpec((256, heads), lambda i: (i, 0)),
-        ],
-        out_shape=[
-            jax.ShapeDtypeStruct((rows, 2, width), f32),
-            jax.ShapeDtypeStruct((rows, heads), f32),
-        ],
-        name="unpack",
-    )(x)
+        kernel,
+        grid_spec=pltpu.PrefetchScalarGridSpec(
+            num_scalar_prefetch=1,
+            grid=(2, n),
+            in_specs=[pl.BlockSpec((1, 1, piece, cols), lambda p, k, me: (p, k, 0, 0))],
+            out_specs=[spec(shape) for shape in shapes],
+        ),
+        out_shape=[jax.ShapeDtypeStruct(shape, f32) for shape in shapes],
+        name="place",
+    )(lax.axis_index("rows").astype(jnp.int32)[None], x)
 
 
 def rows_spec(cols, order):
@@ -712,33 +718,46 @@
         self.n = lax.axis_size("rows")
         self.me = lax.axis_index("rows")
         self.bits = self.n.bit_length() - 1
-        self.shape, self.bound = x.shape, bound
+        self.bound = bound
         piece = x.shape[0] // (2 * self.n)
         cut = x.reshape((2,) + (2,) * self.bits + (piece, x.shape[1]))
         self.cur = [cut[0], cut[1]]
         self.order = [[(k + part) % self.bits for k in range(self.bits)] for part in range(2)]
         self.left = [list(range(self.bits))[::-1] for _ in range(2)]
 
-    def pairs(self, bit):
-        return [(i, i ^ (1 << bit)) for i in range(self.n)]
-
-    def reduce(self):
-        for k in range(self.bits):
+    def move(self, x, bit):
+        return lax.ppermute(x, "rows", [(i, i ^ (1 << bit)) for i in range(self.n)])
+
+    def reduce(self, k):
+        for part in range(2):
+            bit, left = self.order[part][k], self.left[part]
+            mine = (self.me >> bit) & 1
+            axis = left.index(bit)
+            left.remove(bit)
+            cur = self.cur[part]
+            send = lax.dynamic_index_in_dim(cur, 1 - mine, axis, keepdims=False)
+            keep = lax.dynamic_index_in_dim(cur, mine, axis, keepdims=False)
+            got = self.move(encode(send, self.bound, jnp.float16), bit)
+            self.cur[part] = keep + decode(got, self.bound)
+
+    def hold(self, *deps):
+        self.cur = [after(cur, *deps) for cur in self.cur]
+
+    def spread(self):
+        pieces = [{0: encode(cur, self.bound, jnp.float16)} for cur in self.cur]
+        for k in reversed(range(self.bits)):
+            far = []
             for part in range(2):
-                bit, left = self.order[part][k], self.left[part]
-                mine = (self.me >> bit) & 1
-                axis = left.index(bit)
-                left.remove(bit)
-                cur = self.cur[part]
-                send = lax.dynamic_index_in_dim(cur, 1 - mine, axis, keepdims=False)
-                keep = lax.dynamic_index_in_dim(cur, mine, axis, keepdims=False)
-                got = lax.ppermute(encode(send, self.bound, jnp.float16), "rows", self.pairs(bit))
-                self.cur[part] = keep + decode(got, self.bound)
-
-    def spread(self):
-        mine = jnp.stack([encode(cur, self.bound, jnp.float16) for cur in self.cur])
-        every = lax.all_gather(mine, "rows", axis=1, tiled=True)
-        return decode(every.reshape(self.shape), self.bound)
+                bit = self.order[part][k]
+                for rel in list(pieces[part]):
+                    pieces[part][rel ^ (1 << bit)] = self.move(pieces[part][rel], bit)
+                    far.append((part, rel ^ (1 << bit)))
+            held = lax.optimization_barrier(tuple(pieces[part][rel] for part, rel in far))
+            for (part, rel), data in zip(far, held):
+                pieces[part][rel] = data
+        halves = [pieces[part][rel] for part in range(2) for rel in range(self.n)]
+        whole = decode(jnp.stack(halves), self.bound)
+        return whole.reshape((2, self.n) + whole.shape[1:])
 
 
 def per_device(
@@ -815,6 +834,9 @@
     )
     bound = jnp.sqrt(size.reshape(lines, L)) * (1.01 * w_size) + 1e-30
     mixed.hold(low)
+    mixed.pack(2)
+    nd_part = after(nd_part, *mixed.out)
+    mixed.send(2)
     small = sum_small(
         jnp.concatenate([nd_part.reshape(lines, L), bound, sg], axis=0), "heads", 3
     )
@@ -827,10 +849,8 @@
     normal.pack(0)
     low_late = after(low, *normal.out)
     scaled_late = after(scaled, *normal.out)
+    mixed.hold(*normal.out)
     normal.send(0)
-    mixed.hold(*normal.out)
-    mixed.rest(2)
-    output = (source + mixed.total().T).astype(bf16)
 
     grad_proj = lax.dot_general(
         normed, low_late, (((0,), (0,)), ((), ())), preferred_element_type=f32
@@ -844,11 +864,21 @@
     tops = jnp.broadcast_to(jnp.repeat(tops * 1.01 + 1e-30, 8)[:, None], (16, L))
     wide = pg.reshape(8 * width // L, L)
     small = sum_small(jnp.concatenate([tops, sg, hg, wide], axis=0), "rows", 4)
+
+    normal.hold(small)
+    normal.pack(1)
+    small = after(small, *normal.out)
+    gsh_part = after(gsh_part, *normal.out)
+    mixed.hold(*normal.out)
+    normal.send(1)
     top_proj, top_wout, sg, hg = small[0, 0], small[8, 0], small[16:24], small[24:32]
     pg = small[32:].reshape(8, width)
     sum_proj, sum_wout = RowSum(grad_proj, top_proj), RowSum(grad_wout, top_wout)
-    sum_proj.reduce()
-    sum_wout.reduce()
+    for k in range(sum_proj.bits):
+        sum_proj.reduce(k)
+        sum_wout.reduce(k)
+    mixed.rest(3)
+    output = (source + mixed.total().T).astype(bf16)
 
     cut = gsh_part.T.reshape(chips, 2, L // (2 * chips), tokens)
     gsh_own = lax.dynamic_index_in_dim(cut, core, 1, keepdims=False)
@@ -859,15 +889,22 @@
     low_shared = lax.all_gather(shared.total().astype(bf16), "heads", axis=0, tiled=True)
     shared_raw = rest[:, width : width + L]
     norm_dot = norm_dot + jnp.sum(low_shared.T.astype(f32) * shared_raw, axis=1)
-    grad_proj, grad_step = unpack(sum_proj.spread(), width, heads)
-    grad_wout = sum_wout.spread()
     normed_local = (source * inv_rms[:, None] * norm_gain[None, :]).astype(bf16)
     grad_shared_w = lax.dot_general(
         low_shared, normed_local, (((1,), (0,)), ((), ())), preferred_element_type=f32
     )
     grad_shared_w = lax.psum(grad_shared_w, "rows")
 
-    normal.rest(1)
+    normal.pack(2)
+    sum_proj.hold(*normal.out)
+    sum_wout.hold(*normal.out)
+    normal.send(2)
+    grad_proj, grad_step = place(
+        sum_proj.spread(), unpack_kernel, [(full, 2, width), (full, heads)]
+    )
+    (grad_wout,) = place(sum_wout.spread(), place_kernel, [grad_wout.shape])
+
+    normal.rest(3)
     grad_normed = normal.total() + lax.dot_general(
         in_shared, low_shared, (((0,), (0,)), ((), ())), preferred_element_type=f32
     )

time: 943 us -> 944 us (level)
  blocking collectives: 116 us -> 57.3 us
  starting transfers between devices: 82.4 us -> 120 us
  local copies, waits for them, and re-layouts: 44 us -> 63 us
    all_gather x2 -> x0, blocking collectives: 58.2 us -> none  [spread(): every = lax.all_gather(mine, 'rows', axis=1, tiled=True)]
    ppermute x8 -> x20, waiting for transfers between devices: 14.6 us -> 61.2 us  [move(): return lax.ppermute(x, 'rows', [(i, i ^ 1 << bit) for i in range(self.n)])]
    ppermute x18, waiting for transfers between devices: 80.1 us -> 36 us  [send(): self.moving[way] = lax.ppermute(out[way], 'heads', pairs)]
    ppermute x18, starting transfers between devices: 59.7 us -> 83.8 us  [send(): self.moving[way] = lax.ppermute(out[way], 'heads', pairs)]
    ppermute x8 -> x20, starting transfers between devices: 8.1 us -> 22 us  [move(): return lax.ppermute(x, 'rows', [(i, i ^ 1 << bit) for i in range(self.n)])]
    ppermute x3, waiting for transfers between devices: 17.8 us -> 6.13 us  [swap(): self.got = lax.ppermute(self.message, 'heads', pairs)]
    psum x1, waiting for transfers between devices: 0.02 us -> 10.2 us  [per_device(): grad_shared_w = lax.psum(grad_shared_w, 'rows')]
    slice x2, local copies, waits for them, and re-layouts: 3.25 us -> 12.7 us  [__init__(): self.cur = [cut[0], cut[1]]]
  transfers between devices with their start and end apart: 33 -> 45, of which waited for: 10 -> 20; matrix products, arithmetic and copies ran while one was open for 23% -> 21% of each run, Pallas kernels for 15% -> 26%
where the time goes in v2:
time: 944 us; the launch traced here: 938 us
  Pallas kernels  251 us (27%)
  waiting for transfers between devices  230 us (24%)
  starting transfers between devices  120 us (13%)
  matrix products  102 us (11%)
  other arithmetic  95.9 us (10%)
  local copies, waits for them, and re-layouts  63 us (7%)
  blocking collectives  57.3 us (6%)
  between operations  18.6 us (2%)
    pallas_call x1, Pallas kernels, run_bwd(): pl.pallas_call(functools.partial(bwd_kernel, float(inner_total)), grid=(b...  89.6 us
    all_gather x1, waiting for transfers between devices, per_device(): hidden_all = lax.all_gather(hidden_in, 'heads', axis=1, tiled=True)  87.3 us
    ppermute x18, starting transfers between devices, send(): self.moving[way] = lax.ppermute(out[way], 'heads', pairs)  83.8 us
    pallas_call x1, Pallas kernels, run_fwd(): pl.pallas_call(fwd_kernel, grid=(tokens // LB,), in_specs=[smem_spec(), r...  80.4 us
    ppermute x20, waiting for transfers between devices, move(): return lax.ppermute(x, 'rows', [(i, i ^ 1 << bit) for i in range(self.n)])  61.2 us
    convert_element_type x16, other arithmetic, encode(): return x.astype(kind)  58.2 us
    pallas_call x5, Pallas kernels, sum_small(): pl.pallas_call(functools.partial(exchange_kernel, axis), out_shape=jax.Sh...  47.1 us
    dot_general x4, matrix products, project(): lax.dot_general(w, v, (((axis,), (1,)), ((), ())), preferred_element_type...  46.4 us
  transfers between devices with their start and end apart: 45, of which 20 were waited for; matrix products, arithmetic and copies ran while one was open for 21% of the time, Pallas kernels for 26%

profile of v2, /device:TPU:0, one launch (start us, length us, event | category | flops | bytes accessed | tf_op | source)
XLA Modules:
  0.0 938.2 jit_solution(12156285444826981922)
XLA Ops:
  22.9 13.9 %all-gather = f32[8,1,256]{2,1,0:T(1,128)} all-gather(f32[1,1,256]{2,1,0:T(1,128)S(1)} %bitcast.342), channel_id=1, replica_groups=mesh['rows'=4,'heads'=8] {'heads'}, dimensions={0}, use_global_device_ids=true | all-gather | bytes 9216 | tf_op jit(solution)/shard_map/all_gather | solution.py:779
  38.2 43.4 %all_gather.17 = bf16[128,2048]{0,1:T(8,128)(2,1)S(1)} all-gather(bf16[128,256]{0,1:T(8,128)(2,1)S(1)} %copy-done.24), channel_id=1, replica_groups=mesh['rows'=4,'heads'=8] {'heads'}, dimensions={1}, use_global_device_ids=true | all-gather | bytes 589824 | tf_op jit(solution)/shard_map/all_gather | solution.py:778
  82.6 87.3 %all-gather.5.cloned.1.call-done.h_ref = bf16[4096,2048]{1,0:T(8,128)(2,1)} async-done(((bf16[4096,256]{1,0:T(8,128)(2,1)}), bf16[4096,2048]{1,0:T(8,128)(2,1)}) %all-gather.5.cloned.1.call-update) | async-done | bytes 16777232 | tf_op jit(solution)/shard_map/all_gather | solution.py:777
  169.9 80.4 %mixer_fwd.1 = (bf16[4096,2048]{1,0:T(8,128)(2,1)}, f32[32,1,128]{2,1,0:T(1,128)}, f32[4096,512]{1,0:T(8,128)}, f32[4096,768]{1,0:T(8,128)}, f32[4096,512]{1,0:T...) custom-call(s32[1,4]{1,0:T(1,128)} %len_ref.5, ...), custom_call_target="tpu_custom_call" | custom-call | tf_op jit(solution)/shard_map/mixer_fwd/pallas_call | solution.py:448
  250.3 8.9 sum_small.5
  270.9 13.7 %collective-permute-start = (f16[4,256,4096]{2,1,0:T(8,128)(2,1)}, f16[4,256,4096]{2,1,0:T(8,128)(2,1)}, u32[]{:S(2)}, u32[]{:S(2)}) collective-permute-start(f16[4,256,4096]{2,1,0:T(8,128)(2,1)} %convolution_convert_fusion), channel_id=1, source_target_pairs={{0,1},{1,0},{2,3},{3,2},{4,5},{5,4},{6,7},{7,6},{8,9},{9,8},{10,11... | collective-permute-start | bytes 25165832 | tf_op jit(solution)/shard_map/ppermute | solution.py:673
  308.5 27.5 %all-gather.7.cloned.1.call-done.cot_ref = bf16[4096,2048]{1,0:T(8,128)(2,1)} async-done(((bf16[4096,256]{1,0:T(8,128)(2,1)}), bf16[4096,2048]{1,0:T(8,128)(2,1)}) %all-gather.7.cloned.1.call-update) | async-done | bytes 16777232 | tf_op jit(solution)/shard_map/all_gather | solution.py:780
  336.0 17.3 %mixer_mid.1 = (f32[4096,512]{1,0:T(8,128)}, f32[32,1,128]{2,1,0:T(1,128)}) custom-call(s32[1,4]{1,0:T(1,128)} %len_ref.5, bf16[4096,2048]{1,0:T(8,128)(2,1)} %all-gather.7.cloned.1.call-done.cot_ref, bf16[512,2048]{1,0:T(8,128)(2,1)} %w_ref.1, f32[4096,512]{1,0:T(8,128)} %get-tuple-element.129.gated_ref, f32[8,512]{1,0:T(8,128)} %concatenate.23.cp_ref), custom_call_target="tpu_custom_call" | custom-call | tf_op jit(solution)/shard_map/mixer_mid/pallas_call | solution.py:500
  353.3 15.0 %sum_small.6 = f32[32,128]{1,0:T(8,128)} custom-call(f32[32,128]{1,0:T(8,128)} %bitcast.339), custom_call_target="tpu_custom_call" | custom-call | tf_op jit(solution)/shard_map/sum_small/pallas_call | solution.py:627
  368.4 9.6 %fusion.42 = (f16[256,4096]{1,0:T(8,128)(2,1)S(1)}, f16[256,4096]{1,0:T(8,128)(2,1)}) fusion(f16[256,4096]{1,0:T(8,128)(2,1)} %collective-permute-done.2, f32[4,256,4096]{2,1,0:T(8,128)} %copy-done.2, s32[]{:T(128)S(6)} %min.47, f16[4,256,4096]{2,1,0:T(8,128)(2,1)} %collective-permute-done, f16[256,4096]{1,0:T(8,128)(2,1)} %collective-permute-done.1, s32[]{:T(128)S(6)} %min.44), kind=kLoop, calls=%fused_computation.69 | loop fusion | flops 10485760 | bytes 20971528 | tf_op jit(solution)/shard_map/convert_element_type | solution.py:653
  387.6 89.6 %mixer_bwd.1 = (bf16[4096,1152]{1,0:T(8,128)(2,1)}, f32[4096,128]{1,0:T(8,128)}, f32[32,1,128]{2,1,0:T(1,128)}, f32[32,1,128]{2,1,0:T(1,128)}, f32[8,512]{1,0:T(...) custom-call(s32[1,4]{1,0:T(1,128)} %len_ref.5, f32[4096,512]{1,0:T(8,128)} %get-tuple-element.142.gate_ref, ...), custom_call_target="tpu_custom_call" | custom-call | tf_op jit(solution)/shard_map/mixer_bwd/pallas_call | solution.py:533
  478.0 10.6 %fusion.41 = (f16[256,4096]{1,0:T(8,128)(2,1)}, f16[256,4096]{1,0:T(8,128)(2,1)}) fusion(f16[256,4096]{1,0:T(8,128)(2,1)} %collective-permute-done.4, f32[4,256,4096]{2,1,0:T(8,128)} %copy-done.2, s32[]{:T(128)S(6)} %min.48, f16[4,256,4096]{2,1,0:T(8,128)(2,1)} %collective-permute-done, f16[256,4096]{1,0:T(8,128)(2,1)} %collective-permute-done.3, s32[]{:T(128)S(6)} %min.43), kind=kLoop, calls=%fused_computation.67 | loop fusion | flops 10485760 | bytes 20971528 | tf_op jit(solution)/shard_map/convert_element_type | solution.py:653
  489.2 10.2 %sum_small.7 = f32[72,128]{1,0:T(8,128)} custom-call(f32[72,128]{1,0:T(8,128)} %pad_maximum_fusion.6.x_ref), custom_call_target="tpu_custom_call" | custom-call | tf_op jit(solution)/shard_map/sum_small/pallas_call | solution.py:627
  500.1 16.4 %multiply_convert_fusion = f16[4,256,4096]{2,1,0:T(8,128)(2,1)} fusion(bf16[4096,1152]{1,0:T(8,128)(2,1)} %get-tuple-element.164, f32[4096]{0:T(1024)S(1)} %get-tuple-element.308, bf16[1,256,1152]{2,1,0:T(8,128)(2,1)} %get-tuple-element.285, bf16[1,256,1152]{2,1,0:T(8,128)(2,1)} %get-tuple-element.284, bf16[1,256,1152]{2,1,0:T(8,128)(2,1)} %get-tuple-element.283, ...), kind=kOutput, calls=%fused_computation.9 | convolution fusion | flops 9675603968 | bytes 20201472 | tf_op jit(solution)/shard_map/dot_general | solution.py:815
  532.1 16.8 %fusion.2 = f32[4,256,4096]{2,1,0:T(8,128)} fusion(bf16[4096,1152]{1,0:T(8,128)(2,1)} %get-tuple-element.164, bf16[1,256,1152]{2,1,0:T(8,128)(2,1)S(1)} %copy-done.21, bf16[1,256,1152]{2,1,0:T(8,128)(2,1)S(1)} %copy-done.20, bf16[1,256,1152]{2,1,0:T(8,128)(2,1)S(1)} %copy-done.19, bf16[1,256,1152]{2,1,0:T(8,128)(2,1)S(1)} %get-tuple-element.286), kind=kOutput, calls=%fused_computation.12 | convolution fusion | flops 9667215360 | bytes 28573696 | tf_op jit(solution)/shard_map/dot_general | solution.py:815
  549.0 17.5 %collective-permute-done.5 = f16[256,4096]{1,0:T(8,128)(2,1)} collective-permute-done((f16[256,4096]{1,0:T(8,128)(2,1)}, f16[256,4096]{1,0:T(8,128)(2,1)}, u32[]{:S(2)}, u32[]{:S(2)}) %collective-permute-start.5) | collective-permute-done | bytes 2097184 | tf_op jit(solution)/shard_map/ppermute | solution.py:699
  585.0 29.8 %abs_reduce_fusion = (f32[]{:T(128)}, f32[2048,1152]{1,0:T(8,128)}) fusion(bf16[4096,2048]{1,0:T(8,128)(2,1)} %get-tuple-element.163, bf16[4096,1152]{1,0:T(8,128)(2,1)} %get-tuple-element.164), kind=kOutput, calls=%fused_computation.15 | convolution fusion | flops 19332071424 | bytes 35651588 | tf_op jit(solution)/shard_map/dot_general | solution.py:855
  614.9 11.1 %abs_reduce_fusion.1 = (f32[]{:T(128)}, f32[512,2048]{1,0:T(8,128)}) fusion(bf16[4096,512]{1,0:T(8,128)(2,1)S(1)} %copy-done.14, bf16[4096,2048]{1,0:T(8,128)(2,1)S(1)} %bitcast.309), kind=kOutput, calls=%fused_computation.80 | convolution fusion | flops 8592031744 | bytes 25165828 | tf_op jit(solution)/shard_map/dot_general | solution.py:859
  684.2 25.9 %collective-permute-done.32 = f16[64,2048]{1,0:T(8,128)(2,1)S(1)} collective-permute-done((f16[64,2048]{1,0:T(8,128)(2,1)S(1)}, f16[64,2048]{1,0:T(8,128)(2,1)S(1)}, u32[]{:S(2)}, u32[]{:S(2)}) %collective-permute-start.32) | collective-permute-done | bytes 262176 | tf_op jit(solution)/shard_map/ppermute | solution.py:729
  737.7 43.0 %collective-permute-start.19 = (f32[16,4096]{1,0:T(8,128)S(1)}, f32[16,4096]{1,0:T(8,128)S(1)}, u32[]{:S(2)}, u32[]{:S(2)}) collective-permute-start(f32[16,4096]{1,0:T(8,128)S(1)} %get-tuple-element.194), channel_id=1, source_target_pairs={{0,2},{1,3},{2,4},{3,5},{4,6},{5,7},{8,10},{9,11},{10,12},{11,13},... | collective-permute-start | bytes 786440 | tf_op jit(solution)/shard_map/ppermute | solution.py:699
  789.8 9.3 fusion.19
  871.6 10.4 %place.2 = (f32[2048,2,512]{2,1,0:T(2,128)}, f32[2048,8]{1,0:T(8,128)}) custom-call(s32[1]{0:T(128)} %bitcast.84.me_ref, f32[2,4,256,1152]{3,2,1,0:T(8,128)} %bitcast.301), custom_call_target="tpu_custom_call" | custom-call | tf_op jit(solution)/shard_map/place/pallas_call | solution.py:408
  891.1 11.8 %fusion.12 = (f32[256]{0:T(256)}, f32[4096,256]{0,1:T(8,128)}, bf16[4096,256]{0,1:T(8,128)(2,1)}) fusion(bf16[4096,256]{0,1:T(8,128)(2,1)S(1)} %copy-done.4, f32[4096]{0:T(1024)S(1)} %bitcast.335, f32[4096]{0:T(1024)S(1)} %fusion.90, f32[256]{0:T(256)S(1)} %copy-done.38, bf16[4096,256]{0,1:T(8,128)(2,1)S(1)} %copy-done.5, ...), kind=kOutput, calls=%fused_computation.30 | convolution fusion | flops 297795328 | bytes 32622596 | tf_op jit(solution)/shard_map/dot_general | solution.py:908
  919.0 10.2 %all-reduce.4.cloned.1.call-done = f32[128,256]{1,0:T(8,128)} async-done(((f32[128,256]{1,0:T(8,128)}), f32[128,256]{1,0:T(8,128)}) %all-reduce.4.cloned.1.call-update) | async-done | bytes 131088 | tf_op jit(solution)/shard_map/psum | solution.py:896
  (312 shorter events, 289.8 us)
Async XLA Ops:
  7.2 162.7 %all-gather.5.cloned.1.call-start = ((), (), s32[]{:S(2)}) async-start(), calls=%async_computation | async-start | bytes 18874368 | tf_op jit(solution)/shard_map/all_gather | solution.py:777
  8.0 328.1 %all-gather.7.cloned.1.call-start = ((), (), s32[]{:S(2)}) async-start(), calls=%async_computation.1 | async-start | bytes 18874368 | tf_op jit(solution)/shard_map/all_gather | solution.py:780
  8.7 875.4 %all-gather.9.cloned.1.call-start = ((), (), s32[]{:S(2)}) async-start(), calls=%async_computation.2 | async-start | bytes 1179648 | tf_op jit(solution)/shard_map/all_gather | solution.py:889
  303.7 64.7 %collective-permute-start.1 = (f16[256,4096]{1,0:T(8,128)(2,1)}, f16[256,4096]{1,0:T(8,128)(2,1)}, u32[]{:S(2)}, u32[]{:S(2)}) collective-permute-start(f16[256,4096]{1,0:T(8,128)(2,1)} %get-tuple-element.131), channel_id=1, source_target_pairs={{0,2},{1,3},{8,10},{9,11},{16,18},{17,19},{24,26},{25,27}} | collective-permute-start | bytes 6291464 | tf_op jit(solution)/shard_map/ppermute | solution.py:699
  306.3 62.1 %collective-permute-start.2 = (f16[256,4096]{1,0:T(8,128)(2,1)S(1)}, f16[256,4096]{1,0:T(8,128)(2,1)}, u32[]{:S(2)}, u32[]{:S(2)}) collective-permute-start(f16[256,4096]{1,0:T(8,128)(2,1)S(1)} %get-tuple-element.132), channel_id=1, source_target_pairs={{6,4},{7,5},{14,12},{15,13},{22,20},{23,21},{30,28},{31,29}} | collective-permute-start | bytes 6291464 | tf_op jit(solution)/shard_map/ppermute | solution.py:699
  378.0 99.9 %collective-permute-start.3 = (f16[256,4096]{1,0:T(8,128)(2,1)}, f16[256,4096]{1,0:T(8,128)(2,1)}, u32[]{:S(2)}, u32[]{:S(2)}) collective-permute-start(f16[256,4096]{1,0:T(8,128)(2,1)} %get-tuple-element.139), channel_id=1, source_target_pairs={{0,2},{1,3},{2,4},{3,5},{8,10},{9,11},{10,12},{11,13},{16,18},{17,... | collective-permute-start | bytes 6291464 | tf_op jit(solution)/shard_map/ppermute | solution.py:699
  382.1 95.8 %collective-permute-start.4 = (f16[256,4096]{1,0:T(8,128)(2,1)S(1)}, f16[256,4096]{1,0:T(8,128)(2,1)}, u32[]{:S(2)}, u32[]{:S(2)}) collective-permute-start(f16[256,4096]{1,0:T(8,128)(2,1)S(1)} %get-tuple-element.140), channel_id=1, source_target_pairs={{4,2},{5,3},{6,4},{7,5},{12,10},{13,11},{14,12},{15,13},{20,18},{2... | collective-permute-start | bytes 6291464 | tf_op jit(solution)/shard_map/ppermute | solution.py:699
  516.6 55.4 %collective-permute-start.7 = (f16[4,256,4096]{2,1,0:T(8,128)(2,1)}, f16[4,256,4096]{2,1,0:T(8,128)(2,1)}, u32[]{:S(2)}, u32[]{:S(2)}) collective-permute-start(f16[4,256,4096]{2,1,0:T(8,128)(2,1)} %multiply_convert_fusion), channel_id=1, source_target_pairs={{0,1},{1,0},{2,3},{3,2},{4,5},{5,4},{6,7},{7,6},{8,9},{9,8},{10,11... | collective-permute-start | bytes 25165832 | tf_op jit(solution)/shard_map/ppermute | solution.py:673
  517.3 49.2 %collective-permute-start.5 = (f16[256,4096]{1,0:T(8,128)(2,1)}, f16[256,4096]{1,0:T(8,128)(2,1)}, u32[]{:S(2)}, u32[]{:S(2)}) collective-permute-start(f16[256,4096]{1,0:T(8,128)(2,1)} %get-tuple-element.152), channel_id=1, source_target_pairs={{0,2},{1,3},{2,4},{3,5},{4,6},{5,7},{8,10},{9,11},{10,12},{11,13},... | collective-permute-start | bytes 6291464 | tf_op jit(solution)/shard_map/ppermute | solution.py:699
  522.2 49.7 %collective-permute-start.6 = (f16[256,4096]{1,0:T(8,128)(2,1)}, f16[256,4096]{1,0:T(8,128)(2,1)}, u32[]{:S(2)}, u32[]{:S(2)}) collective-permute-start(f16[256,4096]{1,0:T(8,128)(2,1)} %get-tuple-element.153), channel_id=1, source_target_pairs={{2,0},{3,1},{4,2},{5,3},{6,4},{7,5},{10,8},{11,9},{12,10},{13,11},... | collective-permute-start | bytes 6291464 | tf_op jit(solution)/shard_map/ppermute | solution.py:699
  579.8 67.7 %collective-permute-start.8 = (f16[256,4096]{1,0:T(8,128)(2,1)}, f16[256,4096]{1,0:T(8,128)(2,1)}, u32[]{:S(2)}, u32[]{:S(2)}) collective-permute-start(f16[256,4096]{1,0:T(8,128)(2,1)} %get-tuple-element.160), channel_id=1, source_target_pairs={{0,2},{1,3},{8,10},{9,11},{16,18},{17,19},{24,26},{25,27}} | collective-permute-start | bytes 6291464 | tf_op jit(solution)/shard_map/ppermute | solution.py:699
  582.8 64.7 %collective-permute-start.9 = (f16[256,4096]{1,0:T(8,128)(2,1)S(1)}, f16[256,4096]{1,0:T(8,128)(2,1)}, u32[]{:S(2)}, u32[]{:S(2)}) collective-permute-start(f16[256,4096]{1,0:T(8,128)(2,1)S(1)} %get-tuple-element.161), channel_id=1, source_target_pairs={{6,4},{7,5},{14,12},{15,13},{22,20},{23,21},{30,28},{31,29}} | collective-permute-start | bytes 6291464 | tf_op jit(solution)/shard_map/ppermute | solution.py:699
  669.2 50.1 %collective-permute-start.14 = (f32[4,16,4096]{2,1,0:T(8,128)S(1)}, f32[4,16,4096]{2,1,0:T(8,128)S(1)}, u32[]{:S(2)}, u32[]{:S(2)}) collective-permute-start(f32[4,16,4096]{2,1,0:T(8,128)S(1)} %dynamic-slice_bitcast_fusion), channel_id=1, source_target_pairs={{0,1},{1,0},{2,3},{3,2},{4,5},{5,4},{6,7},{7,6},{8,9},{9,8},{10,11... | collective-permute-start | bytes 3145736 | tf_op jit(solution)/shard_map/ppermute | solution.py:673
  671.6 49.1 %collective-permute-start.21 = (f16[2,256,1152]{2,1,0:T(8,128)(2,1)S(1)}, f16[2,256,1152]{2,1,0:T(8,128)(2,1)S(1)}, u32[]{:S(2)}, u32[]{:S(2)}) collective-permute-start(f16[2,256,1152]{2,1,0:T(8,128)(2,1)S(1)} %fusion.58), channel_id=1, source_target_pairs={{0,8},{8,0},{16,24},{24,16},{1,9},{9,1},{17,25},{25,17},{2,10},{10... | collective-permute-start | bytes 3538952 | tf_op jit(solution)/shard_map/ppermute | solution.py:729
  672.2 60.0 %collective-permute-start.25 = (f16[2,256,1152]{2,1,0:T(8,128)(2,1)S(1)}, f16[2,256,1152]{2,1,0:T(8,128)(2,1)S(1)}, u32[]{:S(2)}, u32[]{:S(2)}) collective-permute-start(f16[2,256,1152]{2,1,0:T(8,128)(2,1)S(1)} %fusion.57), channel_id=1, source_target_pairs={{0,16},{8,24},{16,0},{24,8},{1,17},{9,25},{17,1},{25,9},{2,18},{10... | collective-permute-start | bytes 3538952 | tf_op jit(solution)/shard_map/ppermute | solution.py:729
  678.7 111.1 %collective-permute-start.10 = (f16[256,4096]{1,0:T(8,128)(2,1)}, f16[256,4096]{1,0:T(8,128)(2,1)}, u32[]{:S(2)}, u32[]{:S(2)}) collective-permute-start(f16[256,4096]{1,0:T(8,128)(2,1)} %get-tuple-element.176), channel_id=1, source_target_pairs={{0,2},{1,3},{2,4},{3,5},{8,10},{9,11},{10,12},{11,13},{16,18},{17,... | collective-permute-start | bytes 6291464 | tf_op jit(solution)/shard_map/ppermute | solution.py:699
  716.5 73.3 %collective-permute-start.11 = (f16[256,4096]{1,0:T(8,128)(2,1)}, f16[256,4096]{1,0:T(8,128)(2,1)}, u32[]{:S(2)}, u32[]{:S(2)}) collective-permute-start(f16[256,4096]{1,0:T(8,128)(2,1)} %get-tuple-element.177), channel_id=1, source_target_pairs={{4,2},{5,3},{6,4},{7,5},{12,10},{13,11},{14,12},{15,13},{20,18},{2... | collective-permute-start | bytes 6291464 | tf_op jit(solution)/shard_map/ppermute | solution.py:699
  726.3 54.4 %collective-permute-start.22 = (f16[256,1152]{1,0:T(8,128)(2,1)S(1)}, f16[256,1152]{1,0:T(8,128)(2,1)S(1)}, u32[]{:S(2)}, u32[]{:S(2)}) collective-permute-start(f16[256,1152]{1,0:T(8,128)(2,1)S(1)} %fusion.68), channel_id=1, source_target_pairs={{0,16},{8,24},{16,0},{24,8},{1,17},{9,25},{17,1},{25,9},{2,18},{10... | collective-permute-start | bytes 1769480 | tf_op jit(solution)/shard_map/ppermute | solution.py:729
  736.1 47.0 %collective-permute-start.26 = (f16[256,1152]{1,0:T(8,128)(2,1)S(1)}, f16[256,1152]{1,0:T(8,128)(2,1)S(1)}, u32[]{:S(2)}, u32[]{:S(2)}) collective-permute-start(f16[256,1152]{1,0:T(8,128)(2,1)S(1)} %fusion.69), channel_id=1, source_target_pairs={{0,8},{8,0},{16,24},{24,16},{1,9},{9,1},{17,25},{25,17},{2,10},{10... | collective-permute-start | bytes 1769480 | tf_op jit(solution)/shard_map/ppermute | solution.py:729
  737.7 46.8 %collective-permute-start.19 = (f32[16,4096]{1,0:T(8,128)S(1)}, f32[16,4096]{1,0:T(8,128)S(1)}, u32[]{:S(2)}, u32[]{:S(2)}) collective-permute-start(f32[16,4096]{1,0:T(8,128)S(1)} %get-tuple-element.194), channel_id=1, source_target_pairs={{0,2},{1,3},{2,4},{3,5},{4,6},{5,7},{8,10},{9,11},{10,12},{11,13},... | collective-permute-start | bytes 786440 | tf_op jit(solution)/shard_map/ppermute | solution.py:699
  789.7 139.6 %all-reduce.4.cloned.1.call-start = ((), (), s32[]{:S(2)}) async-start(), calls=%async_computation.3 | async-start | bytes 262144 | tf_op jit(solution)/shard_map/psum | solution.py:896
  804.3 47.5 %collective-permute-start.29 = (f16[256,1152]{1,0:T(8,128)(2,1)}, f16[256,1152]{1,0:T(8,128)(2,1)S(1)}, u32[]{:S(2)}, u32[]{:S(2)}) collective-permute-start(f16[256,1152]{1,0:T(8,128)(2,1)} %multiply_convert_fusion.3), channel_id=1, source_target_pairs={{0,16},{8,24},{16,0},{24,8},{1,17},{9,25},{17,1},{25,9},{2,18},{10... | collective-permute-start | bytes 1769480 | tf_op jit(solution)/shard_map/ppermute | solution.py:729
  829.0 62.0 %collective-permute-start.12 = (f16[256,4096]{1,0:T(8,128)(2,1)}, f16[256,4096]{1,0:T(8,128)(2,1)}, u32[]{:S(2)}, u32[]{:S(2)}) collective-permute-start(f16[256,4096]{1,0:T(8,128)(2,1)} %get-tuple-element.180), channel_id=1, source_target_pairs={{0,2},{1,3},{2,4},{3,5},{4,6},{5,7},{8,10},{9,11},{10,12},{11,13},... | collective-permute-start | bytes 6291464 | tf_op jit(solution)/shard_map/ppermute | solution.py:699
  851.8 39.3 %collective-permute-start.13 = (f16[256,4096]{1,0:T(8,128)(2,1)}, f16[256,4096]{1,0:T(8,128)(2,1)}, u32[]{:S(2)}, u32[]{:S(2)}) collective-permute-start(f16[256,4096]{1,0:T(8,128)(2,1)} %get-tuple-element.181), channel_id=1, source_target_pairs={{2,0},{3,1},{4,2},{5,3},{6,4},{7,5},{10,8},{11,9},{12,10},{13,11},... | collective-permute-start | bytes 6291464 | tf_op jit(solution)/shard_map/ppermute | solution.py:699
  (77 other events, 1180.7 us)
Sparse Core Ops, SparseCore 0:
  9.6 160.2 all-gather.4
  171.5 164.4 all-gather.6
  789.8 19.4 all-gather.8
  887.2 42.0 all-reduce.3

commit v3 on v2

--- a/solution.py
+++ b/solution.py
@@ -102,9 +102,10 @@
 
 
 def fwd_kernel(
-    len_ref, h_ref, gain_ref, wgi_ref, wss_ref, cp_ref, sp_ref, hp_ref,
-    normed_ref, inv_ref, gate_ref, rest_ref, gated_ref, y_ref, st_ref, gsum_ref,
-    vbuf, state,
+    first_block,
+    len_ref, h_ref, gain_ref, wgi_ref, wss_ref, cp_ref, sp_ref, hp_ref, v_in_ref, state_in_ref,
+    normed_ref, inv_ref, gate_ref, rest_ref, gated_ref, y_ref, st_ref, gsum_ref, v_out_ref,
+    state_out_ref, vbuf, state,
 ):
     blk = pl.program_id(0)
     width = gate_ref.shape[1]
@@ -113,8 +114,8 @@
 
     @pl.when(blk == 0)
     def _():
-        vbuf[0:8, :] = jnp.zeros((8, vbuf.shape[1]), f32)
-        state[...] = jnp.zeros(state.shape, f32)
+        vbuf[0:8, :] = v_in_ref[...]
+        state[...] = state_in_ref[...]
 
     piece = 256
 
@@ -148,7 +149,7 @@
     def chunk(s, carry):
         r0 = pl.multiple_of(s * L, L)
         rows = pl.ds(r0, L)
-        base = blk * LB + s * L
+        base = (blk + first_block) * LB + s * L
         step = rest_ref[rows, width + L :]
         tcol, trow, start_col, _, _, dt, _, cum, ecum, wend, cdec = chunk_columns(
             hp_ref, step, bounds, base
@@ -200,11 +201,16 @@
     lax.fori_loop(0, NSUB, chunk, 0)
     vbuf[0:8, :] = vbuf[LB : LB + 8, :]
 
-
-def mid_kernel(len_ref, cot_ref, w_ref, gated_ref, cp_ref, gs_ref, gdot_ref):
+    @pl.when(blk == pl.num_programs(0) - 1)
+    def _():
+        v_out_ref[...] = vbuf[0:8, :]
+        state_out_ref[...] = state[...]
+
+
+def mid_kernel(first_block, len_ref, cot_ref, w_ref, gated_ref, cp_ref, gs_ref, gdot_ref):
     blk = pl.program_id(0)
     live = bounds_of(len_ref)[3]
-    t = lax.broadcasted_iota(jnp.int32, gs_ref.shape, 0) + blk * LB
+    t = lax.broadcasted_iota(jnp.int32, gs_ref.shape, 0) + (blk + first_block) * LB
     gs = jnp.where(t < live, mm(cot_ref[...], w_ref[...], 1, 1), 0.0)
     gs_ref[...] = gs
     dots = jnp.sum(gs * cp_ref[6:7, :] * gated_ref[...], axis=1, keepdims=True)
@@ -213,10 +219,10 @@
 
 
 def bwd_kernel(
-    inner_total,
+    inner_total, first_block,
     len_ref, gate_ref, rest_ref, halo_ref, gs_ref, y_ref, st_ref, gsum_ref, gdot_ref,
-    cp_ref, sp_ref, hp_ref,
-    low_ref, gsh_ref, nd_ref, size_ref, pg_ref, sg_ref, hg_ref,
+    cp_ref, sp_ref, hp_ref, v_in_ref, q_in_ref, adj_in_ref, send_in_ref,
+    low_ref, gsh_ref, nd_ref, size_ref, pg_ref, sg_ref, hg_ref, q_out_ref, adj_out_ref,
     vbuf, qnext, adj, send,
 ):
     step_id = pl.program_id(0)
@@ -226,14 +232,21 @@
 
     @pl.when(step_id == 0)
     def _():
-        qnext[...] = jnp.zeros(qnext.shape, f32)
-        adj[...] = jnp.zeros(adj.shape, f32)
-        send[...] = jnp.zeros(send.shape, f32)
+        qnext[...] = q_in_ref[...]
+        adj[...] = adj_in_ref[...]
+        send[...] = send_in_ref[...]
         pg_ref[...] = jnp.zeros(pg_ref.shape, f32)
         sg_ref[...] = jnp.zeros(sg_ref.shape, f32)
         hg_ref[...] = jnp.zeros(hg_ref.shape, f32)
 
-    vbuf[0:8, :] = halo_ref[:, : width + L]
+    @pl.when(blk == 0)
+    def _():
+        vbuf[0:8, :] = v_in_ref[...]
+
+    @pl.when(blk > 0)
+    def _():
+        vbuf[0:8, :] = halo_ref[:, : width + L]
+
     vbuf[8:, :] = rest_ref[:, : width + L]
     bounds = bounds_of(len_ref)
     first = lax.broadcasted_iota(jnp.int32, (L, L), 1) < HEAD
@@ -244,7 +257,7 @@
         s = NSUB - 1 - i
         r0 = pl.multiple_of(s * L, L)
         rows = pl.ds(r0, L)
-        base = blk * LB + s * L
+        base = (blk + first_block) * LB + s * L
         step = rest_ref[rows, width + L :]
         tcol, trow, start_col, start_end, raw, dt, decay, cum, ecum, wend, cdec = chunk_columns(
             hp_ref, step, bounds, base
@@ -386,6 +399,11 @@
 
     lax.fori_loop(0, NSUB, chunk, 0)
 
+    @pl.when(blk == 0)
+    def _():
+        q_out_ref[...] = qnext[...]
+        adj_out_ref[...] = adj[...]
+
 
 def unpack_kernel(me_ref, x_ref, gate_inner_ref, step_ref):
     width = gate_inner_ref.shape[2]
@@ -437,7 +455,7 @@
 VMEM_LIMIT = 60 * 1024 * 1024
 
 
-def run_fwd(lengths, hidden, gain, wgi, wss, cp, sp, hp):
+def run_fwd(first_block, lengths, hidden, gain, wgi, wss, cp, sp, hp, v_in, state_in):
     tokens, full = hidden.shape
     width = wgi.shape[1] // 2
     lines = tokens // L
@@ -446,7 +464,7 @@
         return i
 
     return pl.pallas_call(
-        fwd_kernel,
+        functools.partial(fwd_kernel, first_block),
         grid=(tokens // LB,),
         in_specs=[
             smem_spec(),
@@ -457,6 +475,8 @@
             whole_spec(cp.shape),
             whole_spec(sp.shape),
             whole_spec(hp.shape),
+            whole_spec(v_in.shape),
+            whole_spec(state_in.shape),
         ],
         out_specs=[
             rows_spec(full, same),
@@ -467,6 +487,8 @@
             rows_spec(width, same),
             pl.BlockSpec((NSUB, STATE, width), lambda i: (i, 0, 0)),
             line_spec(same),
+            pl.BlockSpec(v_in.shape, lambda i: (0, 0)),
+            pl.BlockSpec(state_in.shape, lambda i: (0, 0)),
         ],
         out_shape=[
             jax.ShapeDtypeStruct((tokens, full), bf16),
@@ -477,6 +499,8 @@
             jax.ShapeDtypeStruct((tokens, width), f32),
             jax.ShapeDtypeStruct((lines, STATE, width), f32),
             jax.ShapeDtypeStruct((lines, 1, L), f32),
+            jax.ShapeDtypeStruct(v_in.shape, f32),
+            jax.ShapeDtypeStruct(state_in.shape, f32),
         ],
         scratch_shapes=[
             pltpu.VMEM((LB + 8, width + L), f32),
@@ -486,10 +510,10 @@
             dimension_semantics=("arbitrary",), vmem_limit_bytes=VMEM_LIMIT
         ),
         name="mixer_fwd",
-    )(lengths, hidden, gain, wgi, wss, cp, sp, hp)
-
-
-def run_mid(lengths, cot, w_out, gated, cp):
+    )(lengths, hidden, gain, wgi, wss, cp, sp, hp, v_in, state_in)
+
+
+def run_mid(first_block, lengths, cot, w_out, gated, cp):
     tokens, full = cot.shape
     width = gated.shape[1]
     lines = tokens // L
@@ -498,7 +522,7 @@
         return i
 
     return pl.pallas_call(
-        mid_kernel,
+        functools.partial(mid_kernel, first_block),
         grid=(tokens // LB,),
         in_specs=[
             smem_spec(),
@@ -519,7 +543,10 @@
     )(lengths, cot, w_out, gated, cp)
 
 
-def run_bwd(inner_total, lengths, gate, rest, gs, y, st, gsum, gdot, cp, sp, hp):
+def run_bwd(
+    inner_total, first_block, lengths, gate, rest, gs, y, st, gsum, gdot, cp, sp, hp, v_in, q_in,
+    adj_in, send_in,
+):
     tokens, width = gate.shape
     lines = tokens // L
     blocks = tokens // LB
@@ -531,7 +558,7 @@
         return (jnp.maximum(back(i) * (LB // 8) - 1, 0), 0)
 
     return pl.pallas_call(
-        functools.partial(bwd_kernel, float(inner_total)),
+        functools.partial(bwd_kernel, float(inner_total), first_block),
         grid=(blocks,),
         in_specs=[
             smem_spec(),
@@ -546,6 +573,10 @@
             whole_spec(cp.shape),
             whole_spec(sp.shape),
             whole_spec(hp.shape),
+            whole_spec(v_in.shape),
+            whole_spec(q_in.shape),
+            whole_spec(adj_in.shape),
+            whole_spec(send_in.shape),
         ],
         out_specs=[
             rows_spec(2 * width + L, back),
@@ -555,6 +586,8 @@
             pl.BlockSpec((8, width), lambda i: (0, 0)),
             pl.BlockSpec((8, L), lambda i: (0, 0)),
             pl.BlockSpec((8, L), lambda i: (0, 0)),
+            pl.BlockSpec(q_in.shape, lambda i: (0, 0)),
+            pl.BlockSpec(adj_in.shape, lambda i: (0, 0)),
         ],
         out_shape=[
             jax.ShapeDtypeStruct((tokens, 2 * width + L), bf16),
@@ -564,6 +597,8 @@
             jax.ShapeDtypeStruct((8, width), f32),
             jax.ShapeDtypeStruct((8, L), f32),
             jax.ShapeDtypeStruct((8, L), f32),
+            jax.ShapeDtypeStruct(q_in.shape, f32),
+            jax.ShapeDtypeStruct(adj_in.shape, f32),
         ],
         scratch_shapes=[
             pltpu.VMEM((LB + 8, width + L), f32),
@@ -575,7 +610,7 @@
             dimension_semantics=("arbitrary",), vmem_limit_bytes=VMEM_LIMIT
         ),
         name="mixer_bwd",
-    )(lengths, gate, rest, rest, gs, y, st, gsum, gdot, cp, sp, hp)
+    )(lengths, gate, rest, rest, gs, y, st, gsum, gdot, cp, sp, hp, v_in, q_in, adj_in, send_in)
 
 
 def pack_params(conv_inner, conv_inner_bias, conv_shared, conv_shared_bias, step_bias, log_decay,
@@ -774,10 +809,18 @@
     core = lax.axis_index("heads") & 1
     source = hidden_in.astype(f32)
 
-    hidden_all = lax.all_gather(hidden_in, "heads", axis=1, tiled=True)
+    part = tokens // 2
+    part_lines = lines // 2
+    part_blocks = part // LB
+
+    def gather(x):
+        return lax.all_gather(x, "heads", axis=1, tiled=True)
+
+    hidden_all = [gather(hidden_in[:part]), gather(hidden_in[part:])]
     shared_all = lax.all_gather(in_shared, "heads", axis=1, tiled=True)
     gain_all = lax.all_gather(norm_gain, "heads", axis=0, tiled=True)
-    cot_all = lax.all_gather(cotangent, "heads", axis=1, tiled=True)
+    cot_1 = gather(cotangent[part:])
+    cot_all = [gather(cotangent[:part]), cot_1]
     wgi = in_gate_inner.reshape(full, 2 * width)
     step_pad = jnp.pad(in_step, ((0, 0), (0, L - heads)))
     wss = jnp.concatenate([shared_all.T, step_pad], axis=1)
@@ -800,94 +843,143 @@
         skip_gain, gate_gain,
     )
 
-    hidden_all = after(hidden_all, back_send, back_own, out_send, out_own, w_size, cp, sp, hp)
-    normed, inv_rows, gate, rest, gated, y, st, gsum_part = run_fwd(
-        lengths, hidden_all, gain_all[None], wgi, wss, cp, sp, hp
+    hidden_all[0] = after(
+        hidden_all[0], back_send, back_own, out_send, out_own, w_size, cp, sp, hp
     )
-    inv_rms = inv_rows.reshape(tokens)
-    gsum = sum_small(gsum_part.reshape(lines, L), "heads", 1)
+    v_rows = jnp.zeros((8, width + L), f32)
+    state = jnp.zeros((STATE, width), f32)
+    v_starts, fwd = [], []
+    for i in range(2):
+        v_starts.append(v_rows)
+        *kept, v_rows, state = run_fwd(
+            i * part_blocks, lengths, hidden_all[i], gain_all[None], wgi, wss, cp, sp, hp, v_rows, state
+        )
+        fwd.append(kept)
+    normed, inv_rows, gate, rest, gated, y, st, gsum_part = zip(*fwd)
+    inv_rms = jnp.concatenate([rows.reshape(part) for rows in inv_rows])
+    gsum = sum_small(jnp.concatenate(gsum_part).reshape(lines, L), "heads", 1)
 
     live = (jnp.arange(tokens, dtype=jnp.int32) < jnp.sum(lengths[0])).astype(bf16)
     gate_rms = lax.rsqrt(gsum.reshape(tokens) / inner_total + EPSILON)
-    scaled = (gated * gate_rms[:, None] * gate_gain[None, :]).astype(bf16) * live[:, None]
+    scaled = []
+    for i in range(2):
+        span = slice(i * part, (i + 1) * part)
+        value = gated[i] * gate_rms[span, None] * gate_gain[None, :]
+        scaled.append(value.astype(bf16) * live[span, None])
 
     def project(w, v, axis):
         return lax.dot_general(w, v, (((axis,), (1,)), ((), ())), preferred_element_type=f32)
 
-    mixed = ScatterLine(
-        project(out_send, scaled, 1), project(out_own, scaled, 1), None, jnp.float16
+    mixed = [
+        ScatterLine(
+            project(out_send, scaled[i], 1), project(out_own, scaled[i], 1), None, jnp.float16
+        )
+        for i in range(2)
+    ]
+    ready = []
+    for line in mixed:
+        line.swap()
+        line.pack(0)
+        ready += line.out
+
+    q_rows = jnp.zeros((8, width + L), f32)
+    adj = jnp.zeros((STATE, width), f32)
+    sent = jnp.zeros((STATE, width), f32)
+    bwd, normal = [None, None], [None, None]
+    for i in (1, 0):
+        cot_late = after(cot_all[i], *ready)
+        if i == 1:
+            for line in mixed:
+                line.send(0)
+        else:
+            normal[1].send(0)
+        gs, gdot_part = run_mid(i * part_blocks, lengths, cot_late, out_weight, gated[i], cp)
+        gdot = sum_small(gdot_part.reshape(part_lines, L), "heads", 3 - i)
+        *kept, q_rows, adj = run_bwd(
+            inner_total, i * part_blocks, lengths, gate[i], rest[i], gs, y[i], st[i],
+            gsum[i * part_lines : (i + 1) * part_lines].reshape(part_lines, 1, L),
+            gdot.reshape(part_lines, 1, L), cp, sp, hp, v_starts[i], q_rows, adj, sent,
+        )
+        sent = st[i][0]
+        low, gsh, nd_part, size, pg, sg, hg = kept
+        ready = []
+        for line in mixed:
+            line.hold(low)
+            line.pack(2 - i)
+            ready += line.out
+        if i == 0:
+            normal[1].hold(low)
+            normal[1].pack(1)
+            ready += normal[1].out
+        bound = jnp.sqrt(size.reshape(part_lines, L)) * (1.01 * w_size) + 1e-30
+        nd_part = after(nd_part.reshape(part_lines, L), *ready)
+        for line in mixed:
+            line.send(2 - i)
+        if i == 0:
+            normal[1].send(1)
+        small = sum_small(jnp.concatenate([nd_part, bound], axis=0), "heads", 5 - i)
+        bound = small[part_lines:].reshape(part)
+        low_now = after(low, bound)
+        normal[i] = ScatterLine(
+            project(back_send, low_now, 2), project(back_own, low_now, 2), bound, jnp.float16
+        )
+        normal[i].swap()
+        normal[i].pack(0)
+        ready = list(normal[i].out)
+        bwd[i] = (low, gsh, small[:part_lines].reshape(part), pg, sg, hg)
+    low, gsh, norm_dot, pg, sg, hg = zip(*bwd)
+    pg, sg, hg = pg[0] + pg[1], sg[0] + sg[1], hg[0] + hg[1]
+    norm_dot = jnp.concatenate(norm_dot)
+
+    late = [after(v, *ready) for v in scaled + list(low)]
+    normal[0].send(0)
+    normal[1].hold(*ready)
+    normal[1].pack(2)
+    grad_wout = sum(
+        lax.dot_general(late[i], cot_all[i], (((0,), (0,)), ((), ())), preferred_element_type=f32)
+        for i in range(2)
     )
-    mixed.swap()
-    mixed.pack(0)
-    cot_late = after(cot_all, *mixed.out)
-    mixed.send(0)
-    gs, gdot_part = run_mid(lengths, cot_late, out_weight, gated, cp)
-    gdot = sum_small(gdot_part.reshape(lines, L), "heads", 2)
-    mixed.hold(gdot)
-    mixed.pack(1)
-    gdot = after(gdot, *mixed.out)
-    mixed.send(1)
-
-    low, gsh_part, nd_part, size, pg, sg, hg = run_bwd(
-        inner_total, lengths, gate, rest, gs, y, st, gsum.reshape(lines, 1, L),
-        gdot.reshape(lines, 1, L), cp, sp, hp,
-    )
-    bound = jnp.sqrt(size.reshape(lines, L)) * (1.01 * w_size) + 1e-30
-    mixed.hold(low)
-    mixed.pack(2)
-    nd_part = after(nd_part, *mixed.out)
-    mixed.send(2)
-    small = sum_small(
-        jnp.concatenate([nd_part.reshape(lines, L), bound, sg], axis=0), "heads", 3
-    )
-    norm_dot, sg = small[:lines].reshape(tokens), small[2 * lines :]
-    bound = small[lines : 2 * lines].reshape(tokens)
-    low = after(low, bound)
-
-    normal = ScatterLine(project(back_send, low, 2), project(back_own, low, 2), bound, jnp.float16)
-    normal.swap()
-    normal.pack(0)
-    low_late = after(low, *normal.out)
-    scaled_late = after(scaled, *normal.out)
-    mixed.hold(*normal.out)
-    normal.send(0)
-
-    grad_proj = lax.dot_general(
-        normed, low_late, (((0,), (0,)), ((), ())), preferred_element_type=f32
+    top_wout = jnp.max(jnp.abs(grad_wout))
+    normal[1].send(2)
+    grad_proj = sum(
+        lax.dot_general(normed[i], late[2 + i], (((0,), (0,)), ((), ())), preferred_element_type=f32)
+        for i in range(2)
     )
     top_proj = jnp.max(jnp.abs(grad_proj))
-    grad_wout = lax.dot_general(
-        scaled_late, cot_all, (((0,), (0,)), ((), ())), preferred_element_type=f32
-    )
-    top_wout = jnp.max(jnp.abs(grad_wout))
+    sg = sum_small(after(sg, *ready), "heads", 6)
     tops = jnp.stack([top_proj, top_wout])
     tops = jnp.broadcast_to(jnp.repeat(tops * 1.01 + 1e-30, 8)[:, None], (16, L))
     wide = pg.reshape(8 * width // L, L)
-    small = sum_small(jnp.concatenate([tops, sg, hg, wide], axis=0), "rows", 4)
-
-    normal.hold(small)
-    normal.pack(1)
-    small = after(small, *normal.out)
-    gsh_part = after(gsh_part, *normal.out)
-    mixed.hold(*normal.out)
-    normal.send(1)
+    small = sum_small(jnp.concatenate([tops, sg, hg, wide], axis=0), "rows", 7)
+
+    normal[0].hold(small)
+    normal[0].pack(1)
+    out = normal[0].out
+    small = after(small, *out)
+    gsh_all = after(jnp.concatenate(gsh), *out)
+    for line in mixed:
+        line.hold(*out)
+    normal[0].send(1)
     top_proj, top_wout, sg, hg = small[0, 0], small[8, 0], small[16:24], small[24:32]
     pg = small[32:].reshape(8, width)
     sum_proj, sum_wout = RowSum(grad_proj, top_proj), RowSum(grad_wout, top_wout)
     for k in range(sum_proj.bits):
         sum_proj.reduce(k)
         sum_wout.reduce(k)
-    mixed.rest(3)
-    output = (source + mixed.total().T).astype(bf16)
-
-    cut = gsh_part.T.reshape(chips, 2, L // (2 * chips), tokens)
+    mixed_out = []
+    for line in mixed:
+        line.rest(3)
+        mixed_out.append(line.total())
+    output = (source + jnp.concatenate(mixed_out, axis=1).T).astype(bf16)
+
+    cut = gsh_all.T.reshape(chips, 2, L // (2 * chips), tokens)
     gsh_own = lax.dynamic_index_in_dim(cut, core, 1, keepdims=False)
     gsh_send = lax.dynamic_index_in_dim(cut, 1 - core, 1, keepdims=False)
     shared = ScatterLine(gsh_send, gsh_own, None, f32)
     shared.swap()
     shared.rest(0)
     low_shared = lax.all_gather(shared.total().astype(bf16), "heads", axis=0, tiled=True)
-    shared_raw = rest[:, width : width + L]
+    shared_raw = jnp.concatenate([raw[:, width : width + L] for raw in rest])
     norm_dot = norm_dot + jnp.sum(low_shared.T.astype(f32) * shared_raw, axis=1)
     normed_local = (source * inv_rms[:, None] * norm_gain[None, :]).astype(bf16)
     grad_shared_w = lax.dot_general(
@@ -895,17 +987,20 @@
     )
     grad_shared_w = lax.psum(grad_shared_w, "rows")
 
-    normal.pack(2)
-    sum_proj.hold(*normal.out)
-    sum_wout.hold(*normal.out)
-    normal.send(2)
+    normal[0].pack(2)
+    sum_proj.hold(*normal[0].out)
+    sum_wout.hold(*normal[0].out)
+    normal[0].send(2)
     grad_proj, grad_step = place(
         sum_proj.spread(), unpack_kernel, [(full, 2, width), (full, heads)]
     )
     (grad_wout,) = place(sum_wout.spread(), place_kernel, [grad_wout.shape])
 
-    normal.rest(3)
-    grad_normed = normal.total() + lax.dot_general(
+    totals = []
+    for line in normal:
+        line.rest(3)
+        totals.append(line.total())
+    grad_normed = jnp.concatenate(totals, axis=1) + lax.dot_general(
         in_shared, low_shared, (((0,), (0,)), ((), ())), preferred_element_type=f32
     )
     grad_normed = grad_normed.T
@@ -915,7 +1010,7 @@
         - source * (inv_rms * inv_rms * norm_dot / full)[:, None]
     )
     grad_input = cotangent.astype(f32) + grad_source
-    grad_gain_norm = sum_small(grad_gain_norm.reshape(local // L, L), "rows", 5).reshape(local)
+    grad_gain_norm = sum_small(grad_gain_norm.reshape(local // L, L), "rows", 8).reshape(local)
     return (
         output,
         grad_input,

time: 944 us -> 1090 us (1.15)
  Pallas kernels: 251 us -> 358 us
  other arithmetic: 95.9 us -> 131 us
  local copies, waits for them, and re-layouts: 63 us -> 86.4 us
  blocking collectives: 57.3 us -> 37.4 us
  starting transfers between devices: 120 us -> 102 us
    pallas_call x5 -> x8, Pallas kernels: 47.1 us -> 139 us  [sum_small(): pl.pallas_call(functools.partial(exchange_kernel, axis), out_shape=jax.Sh...]
    all_gather x2 -> x4, waiting for transfers between devices: 115 us -> 65.7 us  [gather(): return lax.all_gather(x, 'heads', axis=1, tiled=True)]
    ppermute x18 -> x30, waiting for transfers between devices: 36 us -> 72.4 us  [send(): self.moving[way] = lax.ppermute(out[way], 'heads', pairs)]
    all_gather x1, blocking collectives: 43.4 us -> 23.1 us  [per_device(): shared_all = lax.all_gather(in_shared, 'heads', axis=1, tiled=True)]
    add x1 -> x9, other arithmetic: 0.73 us -> 20.1 us  [the longest x4 18.1 us: total(): total = total + decode(self.moving[way], self.bound)]
    ppermute x20, waiting for transfers between devices: 61.2 us -> 79.3 us  [move(): return lax.ppermute(x, 'rows', [(i, i ^ 1 << bit) for i in range(self.n)])]
    pallas_call x3 -> x6, Pallas kernels: 187 us -> 203 us  [the longest x2 95.7 us: run_bwd(): pl.pallas_call(functools.partial(bwd_kernel, float(inner_total), first_bl...]
    ppermute x18 -> x30, starting transfers between devices: 83.8 us -> 73.3 us  [send(): self.moving[way] = lax.ppermute(out[way], 'heads', pairs)]
  transfers between devices with their start and end apart: 45 -> 61, of which waited for: 20 -> 23; matrix products, arithmetic and copies ran while one was open for 21% -> 27% of each run, Pallas kernels for 26% -> 26%
where the time goes in v3:
time: 1090 us; the launch traced here: 1080 us
  Pallas kernels  358 us (33%)
  waiting for transfers between devices  239 us (22%)
  other arithmetic  131 us (12%)
  matrix products  108 us (10%)
  starting transfers between devices  102 us (9%)
  local copies, waits for them, and re-layouts  86.4 us (8%)
  blocking collectives  37.4 us (3%)
  between operations  19.3 us (2%)
    pallas_call x8, Pallas kernels, sum_small(): pl.pallas_call(functools.partial(exchange_kernel, axis), out_shape=jax.Sh...  139 us
    pallas_call x2, Pallas kernels, run_bwd(): pl.pallas_call(functools.partial(bwd_kernel, float(inner_total), first_bl...  95.7 us
    pallas_call x2, Pallas kernels, run_fwd(): pl.pallas_call(functools.partial(fwd_kernel, first_block), grid=(tokens /...  86.6 us
    ppermute x20, waiting for transfers between devices, move(): return lax.ppermute(x, 'rows', [(i, i ^ 1 << bit) for i in range(self.n)])  79.3 us
    ppermute x30, starting transfers between devices, send(): self.moving[way] = lax.ppermute(out[way], 'heads', pairs)  73.3 us
    ppermute x30, waiting for transfers between devices, send(): self.moving[way] = lax.ppermute(out[way], 'heads', pairs)  72.4 us
    convert_element_type x21, other arithmetic, encode(): return x.astype(kind)  66.8 us
    all_gather x4, waiting for transfers between devices, gather(): return lax.all_gather(x, 'heads', axis=1, tiled=True)  65.7 us
  transfers between devices with their start and end apart: 61, of which 23 were waited for; matrix products, arithmetic and copies ran while one was open for 27% of the time, Pallas kernels for 26%

profile of v3, /device:TPU:0, one launch (start us, length us, event | category | flops | bytes accessed | tf_op | source)
XLA Modules:
  0.0 1082.3 jit_solution(16026886326599128549)
XLA Ops:
  14.0 14.3 %all-gather = f32[8,1,256]{2,1,0:T(1,128)} all-gather(f32[1,1,256]{2,1,0:T(1,128)S(1)} %bitcast.457), channel_id=1, replica_groups=mesh['rows'=4,'heads'=8] {'heads'}, dimensions={0}, use_global_device_ids=true | all-gather | bytes 9216 | tf_op jit(solution)/shard_map/all_gather | solution.py:821
  34.1 23.1 %all_gather.23 = bf16[128,2048]{0,1:T(8,128)(2,1)S(1)} all-gather(bf16[128,256]{0,1:T(8,128)(2,1)S(1)} %copy.100), channel_id=1, replica_groups=mesh['rows'=4,'heads'=8] {'heads'}, dimensions={1}, use_global_device_ids=true | all-gather | bytes 589824 | tf_op jit(solution)/shard_map/all_gather | solution.py:820
  74.6 25.3 %all-gather.7.cloned.1.call-done.h_ref = bf16[2048,2048]{1,0:T(8,128)(2,1)} async-done(((bf16[2048,256]{1,0:T(8,128)(2,1)}), bf16[2048,2048]{1,0:T(8,128)(2,1)}) %all-gather.7.cloned.1.call-update) | async-done | bytes 8388624 | tf_op jit(solution)/shard_map/all_gather | solution.py:817
  101.1 43.2 %mixer_fwd.2 = (bf16[2048,2048]{1,0:T(8,128)(2,1)}, f32[16,1,128]{2,1,0:T(1,128)}, f32[2048,512]{1,0:T(8,128)}, f32[2048,768]{1,0:T(8,128)}, f32[2048,512]{1,0:T...) custom-call(s32[1,4]{1,0:T(1,128)} %len_ref.11, ...), custom_call_target="tpu_custom_call" | custom-call | tf_op jit(solution)/shard_map/mixer_fwd/pallas_call | solution.py:466
  144.4 40.4 %all-gather.9.cloned.1.call-done.h_ref = bf16[2048,2048]{1,0:T(8,128)(2,1)} async-done(((bf16[2048,256]{1,0:T(8,128)(2,1)}), bf16[2048,2048]{1,0:T(8,128)(2,1)}) %all-gather.9.cloned.1.call-update) | async-done | bytes 8388624 | tf_op jit(solution)/shard_map/all_gather | solution.py:817
  184.8 43.4 %mixer_fwd.3 = (bf16[2048,2048]{1,0:T(8,128)(2,1)}, f32[16,1,128]{2,1,0:T(1,128)}, f32[2048,512]{1,0:T(8,128)}, f32[2048,768]{1,0:T(8,128)}, f32[2048,512]{1,0:T...) custom-call(s32[1,4]{1,0:T(1,128)} %len_ref.11, ...), custom_call_target="tpu_custom_call" | custom-call | tf_op jit(solution)/shard_map/mixer_fwd/pallas_call | solution.py:466
  288.1 10.4 mixer_mid.2
  298.5 66.6 %sum_small.9 = f32[16,128]{1,0:T(8,128)} custom-call(f32[16,128]{1,0:T(8,128)} %bitcast.451), custom_call_target="tpu_custom_call" | custom-call | tf_op jit(solution)/shard_map/sum_small/pallas_call | solution.py:662
  365.1 48.0 %mixer_bwd.2 = (bf16[2048,1152]{1,0:T(8,128)(2,1)}, f32[2048,128]{1,0:T(8,128)}, f32[16,1,128]{2,1,0:T(1,128)}, f32[16,1,128]{2,1,0:T(1,128)}, f32[8,512]{1,0:T(...) custom-call(s32[1,4]{1,0:T(1,128)} %len_ref.11, ...), custom_call_target="tpu_custom_call" | custom-call | tf_op jit(solution)/shard_map/mixer_bwd/pallas_call | solution.py:560
  413.9 10.1 fusion.81
  471.2 21.9 %collective-permute-done.11 = f16[256,2048]{1,0:T(8,128)(2,1)S(1)} collective-permute-done((f16[256,2048]{1,0:T(8,128)(2,1)S(1)}, f16[256,2048]{1,0:T(8,128)(2,1)S(1)}, u32[]{:S(2)}, u32[]{:S(2)}) %collective-permute-start.11) | collective-permute-done | bytes 1048608 | tf_op jit(solution)/shard_map/ppermute | solution.py:734
  497.3 10.0 mixer_mid.3
  507.4 10.2 sum_small.11
  517.6 47.7 %mixer_bwd.3 = (bf16[2048,1152]{1,0:T(8,128)(2,1)}, f32[2048,128]{1,0:T(8,128)}, f32[16,1,128]{2,1,0:T(1,128)}, f32[16,1,128]{2,1,0:T(1,128)}, f32[8,512]{1,0:T(...) custom-call(s32[1,4]{1,0:T(1,128)} %len_ref.11, ...), custom_call_target="tpu_custom_call" | custom-call | tf_op jit(solution)/shard_map/mixer_bwd/pallas_call | solution.py:560
  581.4 10.4 collective-permute-done.13
  668.4 18.3 %collective-permute-done.24 = f16[256,2048]{1,0:T(8,128)(2,1)} collective-permute-done((f16[256,2048]{1,0:T(8,128)(2,1)}, f16[256,2048]{1,0:T(8,128)(2,1)}, u32[]{:S(2)}, u32[]{:S(2)}) %collective-permute-start.24) | collective-permute-done | bytes 1048608 | tf_op jit(solution)/shard_map/ppermute | solution.py:734
  700.2 25.0 %sum_small.13 = f32[8,128]{1,0:T(8,128)} custom-call(f32[8,128]{1,0:T(8,128)} %add.624.x_ref), custom_call_target="tpu_custom_call" | custom-call | tf_op jit(solution)/shard_map/sum_small/pallas_call | solution.py:662
  725.2 17.7 %fusion.142 = f32[2048,1152]{1,0:T(8,128)} fusion(bf16[2048,2048]{1,0:T(8,128)(2,1)} %get-tuple-element.252, bf16[2048,1152]{1,0:T(8,128)(2,1)} %get-tuple-element.253), kind=kOutput, calls=%fused_computation.287 | convolution fusion | flops 9663676416 | bytes 22544384 | tf_op jit(solution)/shard_map/dot_general | solution.py:945
  742.9 19.6 %abs_reduce_fusion = (f32[]{:T(128)}, f32[2048,1152]{1,0:T(8,128)}) fusion(f32[2048,1152]{1,0:T(8,128)} %fusion.142, bf16[2048,2048]{1,0:T(8,128)(2,1)} %get-tuple-element.254, bf16[2048,1152]{1,0:T(8,128)(2,1)} %get-tuple-element.255), kind=kOutput, calls=%fused_computation.10 | convolution fusion | flops 9670754304 | bytes 31981572 | tf_op jit(solution)/shard_map/dot_general | solution.py:945
  847.8 19.2 %collective-permute-done.45 = f16[2,64,2048]{2,1,0:T(8,128)(2,1)S(1)} collective-permute-done((f16[2,64,2048]{2,1,0:T(8,128)(2,1)S(1)}, f16[2,64,2048]{2,1,0:T(8,128)(2,1)S(1)}, u32[]{:S(2)}, u32[]{:S(2)}) %collective-permute-start.45) | collective-permute-done | bytes 524320 | tf_op jit(solution)/shard_map/ppermute | solution.py:764
  868.7 11.5 %collective-permute-done.49 = f16[2,64,2048]{2,1,0:T(8,128)(2,1)S(1)} collective-permute-done((f16[2,64,2048]{2,1,0:T(8,128)(2,1)S(1)}, f16[2,64,2048]{2,1,0:T(8,128)(2,1)S(1)}, u32[]{:S(2)}, u32[]{:S(2)}) %collective-permute-start.49) | collective-permute-done | bytes 524320 | tf_op jit(solution)/shard_map/ppermute | solution.py:764
  906.2 14.3 %collective-permute-done.39 = f16[2,256,1152]{2,1,0:T(8,128)(2,1)S(1)} collective-permute-done((f16[2,256,1152]{2,1,0:T(8,128)(2,1)S(1)}, f16[2,256,1152]{2,1,0:T(8,128)(2,1)S(1)}, u32[]{:S(2)}, u32[]{:S(2)}) %collective-permute-start.39) | collective-permute-done | bytes 1179680 | tf_op jit(solution)/shard_map/ppermute | solution.py:764
  1009.9 10.0 place.2
  1051.8 20.6 %all-reduce.4.cloned.1.call-done = f32[128,256]{1,0:T(8,128)} async-done(((f32[128,256]{1,0:T(8,128)}), f32[128,256]{1,0:T(8,128)}) %all-reduce.4.cloned.1.call-update) | async-done | bytes 131088 | tf_op jit(solution)/shard_map/psum | solution.py:988
  (450 shorter events, 481.8 us)
Async XLA Ops:
  7.2 92.7 %all-gather.7.cloned.1.call-start = ((), (), s32[]{:S(2)}) async-start(), calls=%async_computation | async-start | bytes 9437184 | tf_op jit(solution)/shard_map/all_gather | solution.py:817
  10.3 174.5 %all-gather.9.cloned.1.call-start = ((), (), s32[]{:S(2)}) async-start(), calls=%async_computation.1 | async-start | bytes 9437184 | tf_op jit(solution)/shard_map/all_gather | solution.py:817
  11.0 277.1 %all-gather.11.cloned.1.call-start = ((), (), s32[]{:S(2)}) async-start(), calls=%async_computation.2 | async-start | bytes 9437184 | tf_op jit(solution)/shard_map/all_gather | solution.py:817
  13.3 484.0 %all-gather.13.cloned.1.call-start = ((), (), s32[]{:S(2)}) async-start(), calls=%async_computation.3 | async-start | bytes 9437184 | tf_op jit(solution)/shard_map/all_gather | solution.py:817
  13.9 1008.2 %all-gather.15.cloned.1.call-start = ((), (), s32[]{:S(2)}) async-start(), calls=%async_computation.4 | async-start | bytes 1179648 | tf_op jit(solution)/shard_map/all_gather | solution.py:981
  272.2 141.7 %collective-permute-start.6 = (f16[256,2048]{1,0:T(8,128)(2,1)}, f16[256,2048]{1,0:T(8,128)(2,1)}, u32[]{:S(2)}, u32[]{:S(2)}) collective-permute-start(f16[256,2048]{1,0:T(8,128)(2,1)} %get-tuple-element.212), channel_id=1, source_target_pairs={{0,2},{1,3},{8,10},{9,11},{16,18},{17,19},{24,26},{25,27}} | collective-permute-start | bytes 3145736 | tf_op jit(solution)/shard_map/ppermute | solution.py:734
  274.4 139.5 %collective-permute-start.7 = (f16[256,2048]{1,0:T(8,128)(2,1)}, f16[256,2048]{1,0:T(8,128)(2,1)}, u32[]{:S(2)}, u32[]{:S(2)}) collective-permute-start(f16[256,2048]{1,0:T(8,128)(2,1)} %get-tuple-element.213), channel_id=1, source_target_pairs={{6,4},{7,5},{14,12},{15,13},{22,20},{23,21},{30,28},{31,29}} | collective-permute-start | bytes 3145736 | tf_op jit(solution)/shard_map/ppermute | solution.py:734
  279.9 134.0 %collective-permute-start.1 = (f16[256,2048]{1,0:T(8,128)(2,1)}, f16[256,2048]{1,0:T(8,128)(2,1)}, u32[]{:S(2)}, u32[]{:S(2)}) collective-permute-start(f16[256,2048]{1,0:T(8,128)(2,1)} %get-tuple-element.191), channel_id=1, source_target_pairs={{0,2},{1,3},{8,10},{9,11},{16,18},{17,19},{24,26},{25,27}} | collective-permute-start | bytes 3145736 | tf_op jit(solution)/shard_map/ppermute | solution.py:734
  282.2 131.8 %collective-permute-start.2 = (f16[256,2048]{1,0:T(8,128)(2,1)}, f16[256,2048]{1,0:T(8,128)(2,1)}, u32[]{:S(2)}, u32[]{:S(2)}) collective-permute-start(f16[256,2048]{1,0:T(8,128)(2,1)} %get-tuple-element.192), channel_id=1, source_target_pairs={{6,4},{7,5},{14,12},{15,13},{22,20},{23,21},{30,28},{31,29}} | collective-permute-start | bytes 3145736 | tf_op jit(solution)/shard_map/ppermute | solution.py:734
  442.8 50.3 %collective-permute-start.8 = (f16[4,256,2048]{2,1,0:T(8,128)(2,1)}, f16[4,256,2048]{2,1,0:T(8,128)(2,1)}, u32[]{:S(2)}, u32[]{:S(2)}) collective-permute-start(f16[4,256,2048]{2,1,0:T(8,128)(2,1)} %multiply_convert_fusion.1), channel_id=1, source_target_pairs={{0,1},{1,0},{2,3},{3,2},{4,5},{5,4},{6,7},{7,6},{8,9},{9,8},{10,11... | collective-permute-start | bytes 12582920 | tf_op jit(solution)/shard_map/ppermute | solution.py:708
  448.5 44.6 %collective-permute-start.11 = (f16[256,2048]{1,0:T(8,128)(2,1)S(1)}, f16[256,2048]{1,0:T(8,128)(2,1)S(1)}, u32[]{:S(2)}, u32[]{:S(2)}) collective-permute-start(f16[256,2048]{1,0:T(8,128)(2,1)S(1)} %copy-done.28), channel_id=1, source_target_pairs={{0,2},{1,3},{2,4},{3,5},{8,10},{9,11},{10,12},{11,13},{16,18},{17,... | collective-permute-start | bytes 3145736 | tf_op jit(solution)/shard_map/ppermute | solution.py:734
  452.0 41.1 %collective-permute-start.12 = (f16[256,2048]{1,0:T(8,128)(2,1)S(1)}, f16[256,2048]{1,0:T(8,128)(2,1)S(1)}, u32[]{:S(2)}, u32[]{:S(2)}) collective-permute-start(f16[256,2048]{1,0:T(8,128)(2,1)S(1)} %copy-done.27), channel_id=1, source_target_pairs={{4,2},{5,3},{6,4},{7,5},{12,10},{13,11},{14,12},{15,13},{20,18},{2... | collective-permute-start | bytes 3145736 | tf_op jit(solution)/shard_map/ppermute | solution.py:734
  615.3 71.4 %collective-permute-start.15 = (f16[4,256,2048]{2,1,0:T(8,128)(2,1)}, f16[4,256,2048]{2,1,0:T(8,128)(2,1)}, u32[]{:S(2)}, u32[]{:S(2)}) collective-permute-start(f16[4,256,2048]{2,1,0:T(8,128)(2,1)} %multiply_convert_fusion), channel_id=1, source_target_pairs={{0,1},{1,0},{2,3},{3,2},{4,5},{5,4},{6,7},{7,6},{8,9},{9,8},{10,11... | collective-permute-start | bytes 12582920 | tf_op jit(solution)/shard_map/ppermute | solution.py:708
  642.3 44.3 %collective-permute-start.24 = (f16[256,2048]{1,0:T(8,128)(2,1)}, f16[256,2048]{1,0:T(8,128)(2,1)}, u32[]{:S(2)}, u32[]{:S(2)}) collective-permute-start(f16[256,2048]{1,0:T(8,128)(2,1)} %get-tuple-element.287), channel_id=1, source_target_pairs={{0,2},{1,3},{2,4},{3,5},{8,10},{9,11},{10,12},{11,13},{16,18},{17,... | collective-permute-start | bytes 3145736 | tf_op jit(solution)/shard_map/ppermute | solution.py:734
  647.7 39.0 %collective-permute-start.25 = (f16[256,2048]{1,0:T(8,128)(2,1)}, f16[256,2048]{1,0:T(8,128)(2,1)}, u32[]{:S(2)}, u32[]{:S(2)}) collective-permute-start(f16[256,2048]{1,0:T(8,128)(2,1)} %get-tuple-element.288), channel_id=1, source_target_pairs={{4,2},{5,3},{6,4},{7,5},{12,10},{13,11},{14,12},{15,13},{20,18},{2... | collective-permute-start | bytes 3145736 | tf_op jit(solution)/shard_map/ppermute | solution.py:734
  690.2 114.2 %collective-permute-start.16 = (f16[256,2048]{1,0:T(8,128)(2,1)}, f16[256,2048]{1,0:T(8,128)(2,1)}, u32[]{:S(2)}, u32[]{:S(2)}) collective-permute-start(f16[256,2048]{1,0:T(8,128)(2,1)} %get-tuple-element.249), channel_id=1, source_target_pairs={{0,2},{1,3},{8,10},{9,11},{16,18},{17,19},{24,26},{25,27}} | collective-permute-start | bytes 3145736 | tf_op jit(solution)/shard_map/ppermute | solution.py:734
  698.5 105.9 %collective-permute-start.17 = (f16[256,2048]{1,0:T(8,128)(2,1)S(1)}, f16[256,2048]{1,0:T(8,128)(2,1)}, u32[]{:S(2)}, u32[]{:S(2)}) collective-permute-start(f16[256,2048]{1,0:T(8,128)(2,1)S(1)} %get-tuple-element.250), channel_id=1, source_target_pairs={{6,4},{7,5},{14,12},{15,13},{22,20},{23,21},{30,28},{31,29}} | collective-permute-start | bytes 3145736 | tf_op jit(solution)/shard_map/ppermute | solution.py:734
  815.6 86.7 %collective-permute-start.28 = (f32[4,16,4096]{2,1,0:T(8,128)}, f32[4,16,4096]{2,1,0:T(8,128)S(1)}, u32[]{:S(2)}, u32[]{:S(2)}) collective-permute-start(f32[4,16,4096]{2,1,0:T(8,128)} %dynamic-slice_bitcast_fusion), channel_id=1, source_target_pairs={{0,1},{1,0},{2,3},{3,2},{4,5},{5,4},{6,7},{7,6},{8,9},{9,8},{10,11... | collective-permute-start | bytes 3145736 | tf_op jit(solution)/shard_map/ppermute | solution.py:708
  818.3 76.6 %collective-permute-start.20 = (f16[256,2048]{1,0:T(8,128)(2,1)}, f16[256,2048]{1,0:T(8,128)(2,1)}, u32[]{:S(2)}, u32[]{:S(2)}) collective-permute-start(f16[256,2048]{1,0:T(8,128)(2,1)} %get-tuple-element.279), channel_id=1, source_target_pairs={{0,2},{1,3},{2,4},{3,5},{8,10},{9,11},{10,12},{11,13},{16,18},{17,... | collective-permute-start | bytes 3145736 | tf_op jit(solution)/shard_map/ppermute | solution.py:734
  822.8 72.1 %collective-permute-start.21 = (f16[256,2048]{1,0:T(8,128)(2,1)}, f16[256,2048]{1,0:T(8,128)(2,1)}, u32[]{:S(2)}, u32[]{:S(2)}) collective-permute-start(f16[256,2048]{1,0:T(8,128)(2,1)} %get-tuple-element.280), channel_id=1, source_target_pairs={{4,2},{5,3},{6,4},{7,5},{12,10},{13,11},{14,12},{15,13},{20,18},{2... | collective-permute-start | bytes 3145736 | tf_op jit(solution)/shard_map/ppermute | solution.py:734
  827.5 76.4 %collective-permute-start.35 = (f16[2,256,1152]{2,1,0:T(8,128)(2,1)}, f16[2,256,1152]{2,1,0:T(8,128)(2,1)}, u32[]{:S(2)}, u32[]{:S(2)}) collective-permute-start(f16[2,256,1152]{2,1,0:T(8,128)(2,1)} %fusion.96), channel_id=1, source_target_pairs={{0,8},{8,0},{16,24},{24,16},{1,9},{9,1},{17,25},{25,17},{2,10},{10... | collective-permute-start | bytes 3538952 | tf_op jit(solution)/shard_map/ppermute | solution.py:764
  927.9 44.9 %collective-permute-start.22 = (f16[256,2048]{1,0:T(8,128)(2,1)}, f16[256,2048]{1,0:T(8,128)(2,1)}, u32[]{:S(2)}, u32[]{:S(2)}) collective-permute-start(f16[256,2048]{1,0:T(8,128)(2,1)} %get-tuple-element.283), channel_id=1, source_target_pairs={{0,2},{1,3},{2,4},{3,5},{4,6},{5,7},{8,10},{9,11},{10,12},{11,13},... | collective-permute-start | bytes 3145736 | tf_op jit(solution)/shard_map/ppermute | solution.py:734
  935.2 39.6 %collective-permute-start.23 = (f16[256,2048]{1,0:T(8,128)(2,1)}, f16[256,2048]{1,0:T(8,128)(2,1)}, u32[]{:S(2)}, u32[]{:S(2)}) collective-permute-start(f16[256,2048]{1,0:T(8,128)(2,1)} %get-tuple-element.284), channel_id=1, source_target_pairs={{2,0},{3,1},{4,2},{5,3},{6,4},{7,5},{10,8},{11,9},{12,10},{13,11},... | collective-permute-start | bytes 3145736 | tf_op jit(solution)/shard_map/ppermute | solution.py:734
  974.5 97.8 %all-reduce.4.cloned.1.call-start = ((), (), s32[]{:S(2)}) async-start(), calls=%async_computation.5 | async-start | bytes 262144 | tf_op jit(solution)/shard_map/psum | solution.py:988
  (123 other events, 1896.2 us)
Sparse Core Ops, SparseCore 0:
  10.4 89.4 all-gather.6
  101.4 83.3 all-gather.8
  186.4 83.4 all-gather.10
  271.4 123.6 all-gather.12
  974.6 25.2 all-gather.14
  1028.4 43.9 all-reduce.3

commit v4 on v2

--- a/solution.py
+++ b/solution.py
@@ -71,6 +71,10 @@
 
 def pair_cols(a, q, first):
     return jnp.where(first, a[:, 2 * q : 2 * q + 1], a[:, 2 * q + 1 : 2 * q + 2])
+
+
+def sigmoid(v):
+    return 0.5 + 0.5 * jnp.tanh(0.5 * v)
 
 
 def softplus(v):
@@ -165,7 +169,7 @@
             return pre
 
         pre_s = conv(slice(width, width + L), sp_ref)
-        act = pre_s * lax.logistic(pre_s)
+        act = pre_s * sigmoid(pre_s)
         b_map = act[:, :STATE]
         c_map = act[:, STATE:]
         scores = jnp.where(mask, mm3(c_map, b_map, 1, 1), 0.0)
@@ -173,7 +177,7 @@
         for q in range(pairs):
             cols = slice(q * L, (q + 1) * L)
             pre = conv(cols, cp_ref.at[:, cols])
-            xin = pre * lax.logistic(pre)
+            xin = pre * sigmoid(pre)
             xp = xin * pair_cols(dt, q, first)
             xh, xl = split(xp)
             bdh, bdl = block_diag(xh, first), block_diag(xl, first)
@@ -191,7 +195,7 @@
             state[:, cols] = mm3(b_map, xw, 0, 0) + st * pair_cols(cdec, q, first[0:1, :])
             y_ref[rows, cols] = y
             gate = gate_ref[rows, cols]
-            gated = (y + cp_ref[5:6, cols] * xin) * (gate * lax.logistic(gate))
+            gated = (y + cp_ref[5:6, cols] * xin) * (gate * sigmoid(gate))
             gated_ref[rows, cols] = gated
             square = square + gated * gated
         gsum_ref[s] = to_row(jnp.sum(square, axis=1, keepdims=True))
@@ -281,7 +285,7 @@
             return grad
 
         seen_s, pre_s = conv(slice(width, width + L), sp_ref)
-        sig_s = lax.logistic(pre_s)
+        sig_s = sigmoid(pre_s)
         act = pre_s * sig_s
         b_map = act[:, :STATE]
         c_map = act[:, STATE:]
@@ -298,14 +302,14 @@
             taps = cp_ref.at[:, cols]
             skip = cp_ref[5:6, cols]
             seen, pre = conv(cols, taps)
-            sig = lax.logistic(pre)
+            sig = sigmoid(pre)
             xin = pre * sig
             dtx = pair_cols(dt, q, first)
             xp = xin * dtx
             y = y_ref[rows, cols]
             ho = y + skip * xin
             gate = gate_ref[rows, cols]
-            gsig = lax.logistic(gate)
+            gsig = sigmoid(gate)
             sl = gate * gsig
             gated = ho * sl
             gs = gs_ref[rows, cols]
@@ -372,7 +376,7 @@
         keep = jnp.where(mask_t, 1.0, 0.0).astype(bf16)
         d_decay = mm_exact_left(keep, reduced[:L, :]) + tail
         d_dt = reduced[L:, :] + d_decay * hp_ref[1:2, :]
-        d_raw = d_dt * lax.logistic(raw)
+        d_raw = d_dt * sigmoid(raw)
         hg_ref[0:1, :] += jnp.sum(d_raw, axis=0, keepdims=True)
         hg_ref[1:2, :] += jnp.sum(d_decay * decay, axis=0, keepdims=True)
         low_step = d_raw.astype(bf16)
@@ -660,13 +664,12 @@
 
 class ScatterLine:
 
-    def __init__(self, send, own, bound, kind):
+    def __init__(self, send, own):
         self.n = lax.axis_size("heads")
         self.chips = self.n // 2
         self.z = lax.axis_index("heads") >> 1
-        self.own, self.kind, self.bound = own, kind, bound
+        self.message, self.own, self.kind = send, own, own.dtype
         self.moving, self.out = [None, None], [None, None]
-        self.message = encode(send, bound, kind)
 
     def swap(self):
         pairs = [(i, i ^ 1) for i in range(self.n)]
@@ -675,7 +678,7 @@
     def block(self, b):
         mine = lax.dynamic_index_in_dim(self.own, b, 0, keepdims=False)
         theirs = lax.dynamic_index_in_dim(self.got, b, 0, keepdims=False)
-        return mine + decode(theirs, self.bound)
+        return mine.astype(f32) + theirs.astype(f32)
 
     def pack(self, r):
         last = self.chips - 1
@@ -683,8 +686,8 @@
             b = last - r + self.z if way == 0 else r - last + self.z
             total = self.block(jnp.clip(b, 0, last))
             if r > 0:
-                total = total + decode(self.moving[way], self.bound)
-            self.out[way] = encode(total, self.bound, self.kind)
+                total = total + self.moving[way].astype(f32)
+            self.out[way] = total.astype(self.kind)
 
     def hold(self, *deps):
         self.moving = [after(m, *deps) for m in self.moving]
@@ -708,7 +711,7 @@
         total = self.block(self.z)
         for way in range(2):
             if self.moving[way] is not None:
-                total = total + decode(self.moving[way], self.bound)
+                total = total + self.moving[way].astype(f32)
         return total
 
 
@@ -743,7 +746,7 @@
     def hold(self, *deps):
         self.cur = [after(cur, *deps) for cur in self.cur]
 
-    def spread(self):
+    def spread(self, *deps):
         pieces = [{0: encode(cur, self.bound, jnp.float16)} for cur in self.cur]
         for k in reversed(range(self.bits)):
             far = []
@@ -752,7 +755,9 @@
                 for rel in list(pieces[part]):
                     pieces[part][rel ^ (1 << bit)] = self.move(pieces[part][rel], bit)
                     far.append((part, rel ^ (1 << bit)))
-            held = lax.optimization_barrier(tuple(pieces[part][rel] for part, rel in far))
+            far_data = [pieces[part][rel] for part, rel in far]
+            held = lax.optimization_barrier((*far_data, *deps))
+            deps = ()
             for (part, rel), data in zip(far, held):
                 pieces[part][rel] = data
         halves = [pieces[part][rel] for part in range(2) for rel in range(self.n)]
@@ -772,7 +777,7 @@
     lines = tokens // L
     inner_total = width * (full // local)
     core = lax.axis_index("heads") & 1
-    source = hidden_in.astype(f32)
+    source_t, cot_t = lax.optimization_barrier((hidden_in.T, cotangent.T))
 
     hidden_all = lax.all_gather(hidden_in, "heads", axis=1, tiled=True)
     shared_all = lax.all_gather(in_shared, "heads", axis=1, tiled=True)
@@ -800,7 +805,8 @@
         skip_gain, gate_gain,
     )
 
-    hidden_all = after(hidden_all, back_send, back_own, out_send, out_own, w_size, cp, sp, hp)
+    hidden_all = after(hidden_all, back_send, back_own, out_send, out_own, w_size, cp, sp, hp, source_t, cot_t)
+    source_t = source_t.astype(f32)
     normed, inv_rows, gate, rest, gated, y, st, gsum_part = run_fwd(
         lengths, hidden_all, gain_all[None], wgi, wss, cp, sp, hp
     )
@@ -814,8 +820,9 @@
     def project(w, v, axis):
         return lax.dot_general(w, v, (((axis,), (1,)), ((), ())), preferred_element_type=f32)
 
+    half = jnp.float16
     mixed = ScatterLine(
-        project(out_send, scaled, 1), project(out_own, scaled, 1), None, jnp.float16
+        project(out_send, scaled, 1).astype(half), project(out_own, scaled, 1).astype(half)
     )
     mixed.swap()
     mixed.pack(0)
@@ -844,22 +851,38 @@
     bound = small[lines : 2 * lines].reshape(tokens)
     low = after(low, bound)
 
-    normal = ScatterLine(project(back_send, low, 2), project(back_own, low, 2), bound, jnp.float16)
+    normal = ScatterLine(
+        encode(project(back_send, low, 2), bound, half),
+        encode(project(back_own, low, 2), bound, half),
+    )
     normal.swap()
     normal.pack(0)
     low_late = after(low, *normal.out)
     scaled_late = after(scaled, *normal.out)
+    gsh_part = after(gsh_part, *normal.out)
     mixed.hold(*normal.out)
     normal.send(0)
 
+    cut = gsh_part.T.reshape(chips, 2, L // (2 * chips), tokens)
+    gsh_own = lax.dynamic_index_in_dim(cut, core, 1, keepdims=False)
+    gsh_send = lax.dynamic_index_in_dim(cut, 1 - core, 1, keepdims=False)
+    shared = ScatterLine(gsh_send, gsh_own)
+    shared.swap()
+    grad_wout = lax.dot_general(
+        scaled_late, cot_all, (((0,), (0,)), ((), ())), preferred_element_type=f32
+    )
+    top_wout = jnp.max(jnp.abs(grad_wout))
+    shared.pack(0)
+    low_late = after(low_late, *shared.out)
+    shared.send(0)
     grad_proj = lax.dot_general(
         normed, low_late, (((0,), (0,)), ((), ())), preferred_element_type=f32
     )
     top_proj = jnp.max(jnp.abs(grad_proj))
-    grad_wout = lax.dot_general(
-        scaled_late, cot_all, (((0,), (0,)), ((), ())), preferred_element_type=f32
-    )
-    top_wout = jnp.max(jnp.abs(grad_wout))
+    shared.hold(top_proj)
+    shared.pack(1)
+    top_proj = after(top_proj, *shared.out)
+    shared.send(1)
     tops = jnp.stack([top_proj, top_wout])
     tops = jnp.broadcast_to(jnp.repeat(tops * 1.01 + 1e-30, 8)[:, None], (16, L))
     wide = pg.reshape(8 * width // L, L)
@@ -868,7 +891,7 @@
     normal.hold(small)
     normal.pack(1)
     small = after(small, *normal.out)
-    gsh_part = after(gsh_part, *normal.out)
+    shared.hold(*normal.out)
     mixed.hold(*normal.out)
     normal.send(1)
     top_proj, top_wout, sg, hg = small[0, 0], small[8, 0], small[16:24], small[24:32]
@@ -877,44 +900,40 @@
     for k in range(sum_proj.bits):
         sum_proj.reduce(k)
         sum_wout.reduce(k)
+    shared.rest(2)
+    low_shared = lax.all_gather(shared.total().astype(bf16), "heads", axis=0, tiled=True)
     mixed.rest(3)
-    output = (source + mixed.total().T).astype(bf16)
-
-    cut = gsh_part.T.reshape(chips, 2, L // (2 * chips), tokens)
-    gsh_own = lax.dynamic_index_in_dim(cut, core, 1, keepdims=False)
-    gsh_send = lax.dynamic_index_in_dim(cut, 1 - core, 1, keepdims=False)
-    shared = ScatterLine(gsh_send, gsh_own, None, f32)
-    shared.swap()
-    shared.rest(0)
-    low_shared = lax.all_gather(shared.total().astype(bf16), "heads", axis=0, tiled=True)
-    shared_raw = rest[:, width : width + L]
-    norm_dot = norm_dot + jnp.sum(low_shared.T.astype(f32) * shared_raw, axis=1)
-    normed_local = (source * inv_rms[:, None] * norm_gain[None, :]).astype(bf16)
-    grad_shared_w = lax.dot_general(
-        low_shared, normed_local, (((1,), (0,)), ((), ())), preferred_element_type=f32
-    )
-    grad_shared_w = lax.psum(grad_shared_w, "rows")
+    output_t = (source_t + mixed.total()).astype(bf16)
 
     normal.pack(2)
-    sum_proj.hold(*normal.out)
-    sum_wout.hold(*normal.out)
+    out = normal.out
     normal.send(2)
     grad_proj, grad_step = place(
-        sum_proj.spread(), unpack_kernel, [(full, 2, width), (full, heads)]
-    )
-    (grad_wout,) = place(sum_wout.spread(), place_kernel, [grad_wout.shape])
+        sum_proj.spread(*out), unpack_kernel, [(full, 2, width), (full, heads)]
+    )
+    (grad_wout,) = place(sum_wout.spread(*out), place_kernel, [grad_wout.shape])
+
+    low_shared = after(low_shared, *out)
+    shared_raw = rest[:, width : width + L]
+    norm_dot = norm_dot + jnp.sum(low_shared.astype(f32) * shared_raw.T, axis=0)
+    normed_t = (source_t * inv_rms[None, :] * norm_gain[:, None]).astype(bf16)
+    grad_shared_w = lax.dot_general(
+        low_shared, normed_t, (((1,), (1,)), ((), ())), preferred_element_type=f32
+    )
+    grad_shared_w = sum_small(grad_shared_w.reshape(local, L), "rows", 6).reshape(L, local)
+    more = lax.dot_general(
+        in_shared, low_shared, (((0,), (0,)), ((), ())), preferred_element_type=f32
+    )
 
     normal.rest(3)
-    grad_normed = normal.total() + lax.dot_general(
-        in_shared, low_shared, (((0,), (0,)), ((), ())), preferred_element_type=f32
-    )
-    grad_normed = grad_normed.T
-    grad_gain_norm = jnp.sum(grad_normed * source * inv_rms[:, None], axis=0)
+    grad_normed = normal.total() * (bound / SCALE)[None, :] + more
+    grad_gain_norm = jnp.sum(grad_normed * source_t * inv_rms[None, :], axis=1)
     grad_source = (
-        inv_rms[:, None] * norm_gain[None, :] * grad_normed
-        - source * (inv_rms * inv_rms * norm_dot / full)[:, None]
-    )
-    grad_input = cotangent.astype(f32) + grad_source
+        inv_rms[None, :] * norm_gain[:, None] * grad_normed
+        - source_t * (inv_rms * inv_rms * norm_dot / full)[None, :]
+    )
+    grad_input = (cot_t.astype(f32) + grad_source).T
+    output = output_t.T
     grad_gain_norm = sum_small(grad_gain_norm.reshape(local // L, L), "rows", 5).reshape(local)
     return (
         output,

time: 944 us -> 907 us (0.961)
  starting transfers between devices: 120 us -> 82.1 us
  waiting for transfers between devices: 230 us -> 207 us
  Pallas kernels: 251 us -> 263 us
  local copies, waits for them, and re-layouts: 63 us -> 73.9 us
    convert_element_type x0 -> x6, other arithmetic: none -> 51.4 us  [pack(): self.out[way] = total.astype(self.kind)]
    convert_element_type x16 -> x10, other arithmetic: 58.2 us -> 9.91 us  [encode(): return x.astype(kind)]
    ppermute x18, starting transfers between devices: 83.8 us -> 45.4 us  [send(): self.moving[way] = lax.ppermute(out[way], 'heads', pairs)]
    pallas_call x5 -> x6, Pallas kernels: 47.1 us -> 59.7 us  [sum_small(): pl.pallas_call(functools.partial(exchange_kernel, axis), out_shape=jax.Sh...]
    ppermute x20, waiting for transfers between devices: 61.2 us -> 49.5 us  [move(): return lax.ppermute(x, 'rows', [(i, i ^ 1 << bit) for i in range(self.n)])]
    unnamed x128 -> x111, local copies, waits for them, and re-layouts: 36.4 us -> 47.6 us
    psum x1 -> x0, waiting for transfers between devices: 10.2 us -> none  [per_device(): grad_shared_w = lax.psum(grad_shared_w, 'rows')]
    all_gather x1, blocking collectives: 43.4 us -> 33.4 us  [per_device(): shared_all = lax.all_gather(in_shared, 'heads', axis=1, tiled=True)]
  transfers between devices with their start and end apart: 45 -> 44, of which waited for: 20 -> 14; matrix products, arithmetic and copies ran while one was open for 21% -> 22% of each run, Pallas kernels for 26% -> 27%
where the time goes in v4:
time: 907 us; the launch traced here: 900 us
  Pallas kernels  263 us (29%)
  waiting for transfers between devices  207 us (23%)
  other arithmetic  105 us (12%)
  matrix products  101 us (11%)
  starting transfers between devices  82.1 us (9%)
  local copies, waits for them, and re-layouts  73.9 us (8%)
  blocking collectives  48.5 us (5%)
  between operations  18.6 us (2%)
    pallas_call x1, Pallas kernels, run_bwd(): pl.pallas_call(functools.partial(bwd_kernel, float(inner_total)), grid=(b...  88.9 us
    all_gather x1, waiting for transfers between devices, per_device(): hidden_all = lax.all_gather(hidden_in, 'heads', axis=1, tiled=True)  87.4 us
    pallas_call x1, Pallas kernels, run_fwd(): pl.pallas_call(fwd_kernel, grid=(tokens // LB,), in_specs=[smem_spec(), r...  80.7 us
    pallas_call x6, Pallas kernels, sum_small(): pl.pallas_call(functools.partial(exchange_kernel, axis), out_shape=jax.Sh...  59.7 us
    convert_element_type x6, other arithmetic, pack(): self.out[way] = total.astype(self.kind)  51.4 us
    ppermute x20, waiting for transfers between devices, move(): return lax.ppermute(x, 'rows', [(i, i ^ 1 << bit) for i in range(self.n)])  49.5 us
    unnamed x111, local copies, waits for them, and re-layouts  47.6 us
    ppermute x18, starting transfers between devices, send(): self.moving[way] = lax.ppermute(out[way], 'heads', pairs)  45.4 us
  transfers between devices with their start and end apart: 44, of which 14 were waited for; matrix products, arithmetic and copies ran while one was open for 22% of the time, Pallas kernels for 27%

profile of v4, /device:TPU:0, one launch (start us, length us, event | category | flops | bytes accessed | tf_op | source)
XLA Modules:
  0.0 899.9 jit_solution(4707304460673199386)
XLA Ops:
  31.6 15.0 %all-gather = f32[8,1,256]{2,1,0:T(1,128)} all-gather(f32[1,1,256]{2,1,0:T(1,128)S(1)} %bitcast.368), channel_id=1, replica_groups=mesh['rows'=4,'heads'=8] {'heads'}, dimensions={0}, use_global_device_ids=true | all-gather | bytes 9216 | tf_op jit(solution)/shard_map/all_gather | solution.py:784
  48.0 33.4 %all_gather.17 = bf16[128,2048]{0,1:T(8,128)(2,1)S(1)} all-gather(bf16[128,256]{0,1:T(8,128)(2,1)S(1)} %copy.95), channel_id=1, replica_groups=mesh['rows'=4,'heads'=8] {'heads'}, dimensions={1}, use_global_device_ids=true | all-gather | bytes 589824 | tf_op jit(solution)/shard_map/all_gather | solution.py:783
  82.5 87.4 %all-gather.5.cloned.1.call-done.h_ref = bf16[4096,2048]{1,0:T(8,128)(2,1)} async-done(((bf16[4096,256]{1,0:T(8,128)(2,1)}), bf16[4096,2048]{1,0:T(8,128)(2,1)}) %all-gather.5.cloned.1.call-update) | async-done | bytes 16777232 | tf_op jit(solution)/shard_map/all_gather | solution.py:782
  169.9 80.7 %mixer_fwd.1 = (bf16[4096,2048]{1,0:T(8,128)(2,1)}, f32[32,1,128]{2,1,0:T(1,128)}, f32[4096,512]{1,0:T(8,128)}, f32[4096,768]{1,0:T(8,128)}, f32[4096,512]{1,0:T...) custom-call(s32[1,4]{1,0:T(1,128)} %len_ref.5, ...), custom_call_target="tpu_custom_call" | custom-call | tf_op jit(solution)/shard_map/mixer_fwd/pallas_call | solution.py:452
  250.6 8.9 sum_small.6
  271.4 13.4 %collective-permute-start = (f16[4,256,4096]{2,1,0:T(8,128)(2,1)}, f16[4,256,4096]{2,1,0:T(8,128)(2,1)}, u32[]{:S(2)}, u32[]{:S(2)}) collective-permute-start(f16[4,256,4096]{2,1,0:T(8,128)(2,1)} %convolution_convert_fusion), channel_id=1, source_target_pairs={{0,1},{1,0},{2,3},{3,2},{4,5},{5,4},{6,7},{7,6},{8,9},{9,8},{10,11... | collective-permute-start | bytes 25165832 | tf_op jit(solution)/shard_map/ppermute | solution.py:676
  308.7 26.2 %all-gather.7.cloned.1.call-done.cot_ref = bf16[4096,2048]{1,0:T(8,128)(2,1)} async-done(((bf16[4096,256]{1,0:T(8,128)(2,1)}), bf16[4096,2048]{1,0:T(8,128)(2,1)}) %all-gather.7.cloned.1.call-update) | async-done | bytes 16777232 | tf_op jit(solution)/shard_map/all_gather | solution.py:785
  334.9 17.3 %mixer_mid.1 = (f32[4096,512]{1,0:T(8,128)}, f32[32,1,128]{2,1,0:T(1,128)}) custom-call(s32[1,4]{1,0:T(1,128)} %len_ref.5, bf16[4096,2048]{1,0:T(8,128)(2,1)} %all-gather.7.cloned.1.call-done.cot_ref, bf16[512,2048]{1,0:T(8,128)(2,1)} %w_ref.1, f32[4096,512]{1,0:T(8,128)} %get-tuple-element.136.gated_ref, f32[8,512]{1,0:T(8,128)} %concatenate.23.cp_ref), custom_call_target="tpu_custom_call" | custom-call | tf_op jit(solution)/shard_map/mixer_mid/pallas_call | solution.py:504
  352.2 16.2 %sum_small.7 = f32[32,128]{1,0:T(8,128)} custom-call(f32[32,128]{1,0:T(8,128)} %bitcast.365), custom_call_target="tpu_custom_call" | custom-call | tf_op jit(solution)/shard_map/sum_small/pallas_call | solution.py:631
  369.7 9.2 %fusion.25 = (f16[256,4096]{1,0:T(8,128)(2,1)S(1)}, f16[256,4096]{1,0:T(8,128)(2,1)}) fusion(f16[256,4096]{1,0:T(8,128)(2,1)} %collective-permute-done.2, f16[4,256,4096]{2,1,0:T(8,128)(2,1)} %collective-permute-done, s32[]{:T(128)S(6)} %min.47, f16[4,256,4096]{2,1,0:T(8,128)(2,1)} %copy-done.2, f16[256,4096]{1,0:T(8,128)(2,1)} %copy-done.13, s32[]{:T(128)S(6)} %min.44), kind=kLoop, calls=%fused_computation.50 | loop fusion | flops 12582912 | bytes 16777224 | tf_op jit(solution)/shard_map/convert_element_type | solution.py:690
  388.6 88.9 %mixer_bwd.1 = (bf16[4096,1152]{1,0:T(8,128)(2,1)}, f32[4096,128]{1,0:T(8,128)}, f32[32,1,128]{2,1,0:T(1,128)}, f32[32,1,128]{2,1,0:T(1,128)}, f32[8,512]{1,0:T(...) custom-call(s32[1,4]{1,0:T(1,128)} %len_ref.5, f32[4096,512]{1,0:T(8,128)} %get-tuple-element.149.gate_ref, ...), custom_call_target="tpu_custom_call" | custom-call | tf_op jit(solution)/shard_map/mixer_bwd/pallas_call | solution.py:537
  478.2 10.2 %fusion.24 = (f16[256,4096]{1,0:T(8,128)(2,1)}, f16[256,4096]{1,0:T(8,128)(2,1)}) fusion(f16[256,4096]{1,0:T(8,128)(2,1)} %collective-permute-done.4, f16[4,256,4096]{2,1,0:T(8,128)(2,1)} %collective-permute-done, s32[]{:T(128)S(6)} %min.48, f16[4,256,4096]{2,1,0:T(8,128)(2,1)} %copy-done.2, f16[256,4096]{1,0:T(8,128)(2,1)} %collective-permute-done.3, ...), kind=kLoop, calls=%fused_computation.48 | loop fusion | flops 12582912 | bytes 16777224 | tf_op jit(solution)/shard_map/convert_element_type | solution.py:690
  489.0 10.2 %sum_small.8 = f32[72,128]{1,0:T(8,128)} custom-call(f32[72,128]{1,0:T(8,128)} %pad_maximum_fusion.6.x_ref), custom_call_target="tpu_custom_call" | custom-call | tf_op jit(solution)/shard_map/sum_small/pallas_call | solution.py:631
  500.0 16.4 %multiply_convert_fusion = f16[4,256,4096]{2,1,0:T(8,128)(2,1)} fusion(bf16[4096,1152]{1,0:T(8,128)(2,1)} %get-tuple-element.174, f32[4096]{0:T(1024)S(1)} %get-tuple-element.318, bf16[1,256,1152]{2,1,0:T(8,128)(2,1)} %get-tuple-element.296, bf16[1,256,1152]{2,1,0:T(8,128)(2,1)} %get-tuple-element.295, bf16[1,256,1152]{2,1,0:T(8,128)(2,1)} %get-tuple-element.294, ...), kind=kOutput, calls=%fused_computation.9 | convolution fusion | flops 9675603968 | bytes 20201472 | tf_op jit(solution)/shard_map/dot_general | solution.py:821
  523.2 14.1 %multiply_convert_fusion.1 = f16[4,256,4096]{2,1,0:T(8,128)(2,1)S(1)} fusion(bf16[4096,1152]{1,0:T(8,128)(2,1)} %get-tuple-element.174, f32[4096]{0:T(1024)S(1)} %get-tuple-element.318, bf16[1,256,1152]{2,1,0:T(8,128)(2,1)} %get-tuple-element.299, bf16[1,256,1152]{2,1,0:T(8,128)(2,1)} %get-tuple-element.298, bf16[1,256,1152]{2,1,0:T(8,128)(2,1)} %get-tuple-element.297, ...), kind=kOutput, calls=%fused_computation.10 | convolution fusion | flops 9675603968 | bytes 20201472 | tf_op jit(solution)/shard_map/dot_general | solution.py:821
  537.4 28.7 %collective-permute-done.5 = f16[256,4096]{1,0:T(8,128)(2,1)S(1)} collective-permute-done((f16[256,4096]{1,0:T(8,128)(2,1)}, f16[256,4096]{1,0:T(8,128)(2,1)S(1)}, u32[]{:S(2)}, u32[]{:S(2)}) %collective-permute-start.5) | collective-permute-done | bytes 2097184 | tf_op jit(solution)/shard_map/ppermute | solution.py:702
  584.9 13.7 %abs_reduce_fusion.1 = (f32[]{:T(128)}, f32[512,2048]{1,0:T(8,128)S(1)}) fusion(bf16[4096,512]{1,0:T(8,128)(2,1)} %copy-done.8, bf16[4096,2048]{1,0:T(8,128)(2,1)} %all-gather.7.cloned.1.call-done.cot_ref), kind=kOutput, calls=%fused_computation.60 | convolution fusion | flops 8592031744 | bytes 25165828 | tf_op jit(solution)/shard_map/dot_general | solution.py:871
  603.3 28.7 %abs_reduce_fusion = (f32[]{:T(128)}, f32[2048,1152]{1,0:T(8,128)S(1)}) fusion(bf16[4096,2048]{1,0:T(8,128)(2,1)} %get-tuple-element.170, bf16[4096,1152]{1,0:T(8,128)(2,1)} %get-tuple-element.174), kind=kOutput, calls=%fused_computation.16 | convolution fusion | flops 19332071424 | bytes 35651588 | tf_op jit(solution)/shard_map/dot_general | solution.py:878
  648.2 10.3 %fusion.22 = (f16[256,4096]{1,0:T(8,128)(2,1)}, f16[256,4096]{1,0:T(8,128)(2,1)}) fusion(f16[256,4096]{1,0:T(8,128)(2,1)} %collective-permute-done.9, f16[4,256,4096]{2,1,0:T(8,128)(2,1)} %collective-permute-done.7, s32[]{:T(128)S(6)} %min.47, f16[4,256,4096]{2,1,0:T(8,128)(2,1)} %copy-done.3, f16[256,4096]{1,0:T(8,128)(2,1)} %collective-permute-done.8, ...), kind=kLoop, calls=%fused_computation.44 | loop fusion | flops 12582912 | bytes 16777224 | tf_op jit(solution)/shard_map/convert_element_type | solution.py:690
  695.2 22.9 %collective-permute-done.31 = f16[2,64,2048]{2,1,0:T(8,128)(2,1)S(1)} collective-permute-done((f16[2,64,2048]{2,1,0:T(8,128)(2,1)}, f16[2,64,2048]{2,1,0:T(8,128)(2,1)S(1)}, u32[]{:S(2)}, u32[]{:S(2)}) %collective-permute-start.31) | collective-permute-done | bytes 524320 | tf_op jit(solution)/shard_map/ppermute | solution.py:732
  721.2 9.2 %collective-permute-done.35 = f16[2,64,2048]{2,1,0:T(8,128)(2,1)S(1)} collective-permute-done((f16[2,64,2048]{2,1,0:T(8,128)(2,1)}, f16[2,64,2048]{2,1,0:T(8,128)(2,1)S(1)}, u32[]{:S(2)}, u32[]{:S(2)}) %collective-permute-start.35) | collective-permute-done | bytes 524320 | tf_op jit(solution)/shard_map/ppermute | solution.py:732
  784.2 11.9 %sum_small.11 = f32[256,128]{1,0:T(8,128)} custom-call(f32[256,128]{1,0:T(8,128)} %reshape.319.x_ref), custom_call_target="tpu_custom_call" | custom-call | tf_op jit(solution)/shard_map/sum_small/pallas_call | solution.py:631
  848.2 10.1 %place.2 = (f32[2048,2,512]{2,1,0:T(2,128)}, f32[2048,8]{1,0:T(8,128)}) custom-call(s32[1]{0:T(128)} %bitcast.79.me_ref, f32[2,4,256,1152]{3,2,1,0:T(8,128)} %bitcast.320), custom_call_target="tpu_custom_call" | custom-call | tf_op jit(solution)/shard_map/place/pallas_call | solution.py:412
  864.9 11.3 %fusion.14 = (f32[256]{0:T(256)}, f32[4096,256]{0,1:T(8,128)}, bf16[4096,256]{0,1:T(8,128)(2,1)}) fusion(bf16[256,4096]{1,0:T(8,128)(2,1)S(1)} %bitcast.340, f32[4096]{0:T(1024)S(1)} %bitcast.361, f32[4096]{0:T(1024)S(1)} %fusion.83, f32[256]{0:T(256)S(1)} %copy-done.29, bf16[256,4096]{1,0:T(8,128)(2,1)} %bitcast.341, ...), kind=kOutput, calls=%fused_computation.32 | convolution fusion | flops 297795328 | bytes 28428292 | tf_op jit(solution)/shard_map/dot_general | solution.py:924
  (291 shorter events, 286.9 us)
Async XLA Ops:
  7.2 162.7 %all-gather.5.cloned.1.call-start = ((), (), s32[]{:S(2)}) async-start(), calls=%async_computation | async-start | bytes 18874368 | tf_op jit(solution)/shard_map/all_gather | solution.py:782
  7.9 327.0 %all-gather.7.cloned.1.call-start = ((), (), s32[]{:S(2)}) async-start(), calls=%async_computation.1 | async-start | bytes 18874368 | tf_op jit(solution)/shard_map/all_gather | solution.py:785
  8.7 765.8 %all-gather.9.cloned.1.call-start = ((), (), s32[]{:S(2)}) async-start(), calls=%async_computation.2 | async-start | bytes 1179648 | tf_op jit(solution)/shard_map/all_gather | solution.py:904
  304.9 63.5 %collective-permute-start.1 = (f16[256,4096]{1,0:T(8,128)(2,1)}, f16[256,4096]{1,0:T(8,128)(2,1)S(1)}, u32[]{:S(2)}, u32[]{:S(2)}) collective-permute-start(f16[256,4096]{1,0:T(8,128)(2,1)} %get-tuple-element.138), channel_id=1, source_target_pairs={{0,2},{1,3},{8,10},{9,11},{16,18},{17,19},{24,26},{25,27}} | collective-permute-start | bytes 6291464 | tf_op jit(solution)/shard_map/ppermute | solution.py:702
  306.3 63.4 %collective-permute-start.2 = (f16[256,4096]{1,0:T(8,128)(2,1)}, f16[256,4096]{1,0:T(8,128)(2,1)}, u32[]{:S(2)}, u32[]{:S(2)}) collective-permute-start(f16[256,4096]{1,0:T(8,128)(2,1)} %get-tuple-element.139), channel_id=1, source_target_pairs={{6,4},{7,5},{14,12},{15,13},{22,20},{23,21},{30,28},{31,29}} | collective-permute-start | bytes 6291464 | tf_op jit(solution)/shard_map/ppermute | solution.py:702
  378.9 99.3 %collective-permute-start.3 = (f16[256,4096]{1,0:T(8,128)(2,1)}, f16[256,4096]{1,0:T(8,128)(2,1)}, u32[]{:S(2)}, u32[]{:S(2)}) collective-permute-start(f16[256,4096]{1,0:T(8,128)(2,1)} %get-tuple-element.146), channel_id=1, source_target_pairs={{0,2},{1,3},{2,4},{3,5},{8,10},{9,11},{10,12},{11,13},{16,18},{17,... | collective-permute-start | bytes 6291464 | tf_op jit(solution)/shard_map/ppermute | solution.py:702
  383.0 95.2 %collective-permute-start.4 = (f16[256,4096]{1,0:T(8,128)(2,1)S(1)}, f16[256,4096]{1,0:T(8,128)(2,1)}, u32[]{:S(2)}, u32[]{:S(2)}) collective-permute-start(f16[256,4096]{1,0:T(8,128)(2,1)S(1)} %get-tuple-element.147), channel_id=1, source_target_pairs={{4,2},{5,3},{6,4},{7,5},{12,10},{13,11},{14,12},{15,13},{20,18},{2... | collective-permute-start | bytes 6291464 | tf_op jit(solution)/shard_map/ppermute | solution.py:702
  516.4 54.0 %collective-permute-start.7 = (f16[4,256,4096]{2,1,0:T(8,128)(2,1)}, f16[4,256,4096]{2,1,0:T(8,128)(2,1)}, u32[]{:S(2)}, u32[]{:S(2)}) collective-permute-start(f16[4,256,4096]{2,1,0:T(8,128)(2,1)} %multiply_convert_fusion), channel_id=1, source_target_pairs={{0,1},{1,0},{2,3},{3,2},{4,5},{5,4},{6,7},{7,6},{8,9},{9,8},{10,11... | collective-permute-start | bytes 25165832 | tf_op jit(solution)/shard_map/ppermute | solution.py:676
  517.0 49.1 %collective-permute-start.5 = (f16[256,4096]{1,0:T(8,128)(2,1)}, f16[256,4096]{1,0:T(8,128)(2,1)S(1)}, u32[]{:S(2)}, u32[]{:S(2)}) collective-permute-start(f16[256,4096]{1,0:T(8,128)(2,1)} %get-tuple-element.159), channel_id=1, source_target_pairs={{0,2},{1,3},{2,4},{3,5},{4,6},{5,7},{8,10},{9,11},{10,12},{11,13},... | collective-permute-start | bytes 6291464 | tf_op jit(solution)/shard_map/ppermute | solution.py:702
  520.6 49.8 %collective-permute-start.6 = (f16[256,4096]{1,0:T(8,128)(2,1)}, f16[256,4096]{1,0:T(8,128)(2,1)}, u32[]{:S(2)}, u32[]{:S(2)}) collective-permute-start(f16[256,4096]{1,0:T(8,128)(2,1)} %get-tuple-element.160), channel_id=1, source_target_pairs={{2,0},{3,1},{4,2},{5,3},{6,4},{7,5},{10,8},{11,9},{12,10},{13,11},... | collective-permute-start | bytes 6291464 | tf_op jit(solution)/shard_map/ppermute | solution.py:702
  578.7 69.5 %collective-permute-start.8 = (f16[256,4096]{1,0:T(8,128)(2,1)}, f16[256,4096]{1,0:T(8,128)(2,1)}, u32[]{:S(2)}, u32[]{:S(2)}) collective-permute-start(f16[256,4096]{1,0:T(8,128)(2,1)} %get-tuple-element.167), channel_id=1, source_target_pairs={{0,2},{1,3},{8,10},{9,11},{16,18},{17,19},{24,26},{25,27}} | collective-permute-start | bytes 6291464 | tf_op jit(solution)/shard_map/ppermute | solution.py:702
  583.0 65.2 %collective-permute-start.9 = (f16[256,4096]{1,0:T(8,128)(2,1)}, f16[256,4096]{1,0:T(8,128)(2,1)}, u32[]{:S(2)}, u32[]{:S(2)}) collective-permute-start(f16[256,4096]{1,0:T(8,128)(2,1)} %get-tuple-element.168), channel_id=1, source_target_pairs={{6,4},{7,5},{14,12},{15,13},{22,20},{23,21},{30,28},{31,29}} | collective-permute-start | bytes 6291464 | tf_op jit(solution)/shard_map/ppermute | solution.py:702
  601.1 35.3 %collective-permute-start.11 = (f32[16,4096]{1,0:T(8,128)S(1)}, f32[16,4096]{1,0:T(8,128)S(1)}, u32[]{:S(2)}, u32[]{:S(2)}) collective-permute-start(f32[16,4096]{1,0:T(8,128)S(1)} %get-tuple-element.175), channel_id=1, source_target_pairs={{0,2},{1,3},{8,10},{9,11},{16,18},{17,19},{24,26},{25,27}} | collective-permute-start | bytes 786440 | tf_op jit(solution)/shard_map/ppermute | solution.py:702
  602.4 34.0 %collective-permute-start.12 = (f32[16,4096]{1,0:T(8,128)S(1)}, f32[16,4096]{1,0:T(8,128)S(1)}, u32[]{:S(2)}, u32[]{:S(2)}) collective-permute-start(f32[16,4096]{1,0:T(8,128)S(1)} %get-tuple-element.176), channel_id=1, source_target_pairs={{6,4},{7,5},{14,12},{15,13},{22,20},{23,21},{30,28},{31,29}} | collective-permute-start | bytes 786440 | tf_op jit(solution)/shard_map/ppermute | solution.py:702
  671.5 91.7 %collective-permute-start.13 = (f16[256,4096]{1,0:T(8,128)(2,1)}, f16[256,4096]{1,0:T(8,128)(2,1)}, u32[]{:S(2)}, u32[]{:S(2)}) collective-permute-start(f16[256,4096]{1,0:T(8,128)(2,1)} %get-tuple-element.193), channel_id=1, source_target_pairs={{0,2},{1,3},{2,4},{3,5},{8,10},{9,11},{10,12},{11,13},{16,18},{17,... | collective-permute-start | bytes 6291464 | tf_op jit(solution)/shard_map/ppermute | solution.py:702
  678.0 87.3 %collective-permute-start.14 = (f16[256,4096]{1,0:T(8,128)(2,1)}, f16[256,4096]{1,0:T(8,128)(2,1)}, u32[]{:S(2)}, u32[]{:S(2)}) collective-permute-start(f16[256,4096]{1,0:T(8,128)(2,1)} %get-tuple-element.194), channel_id=1, source_target_pairs={{4,2},{5,3},{6,4},{7,5},{12,10},{13,11},{14,12},{15,13},{20,18},{2... | collective-permute-start | bytes 6291464 | tf_op jit(solution)/shard_map/ppermute | solution.py:702
  681.4 57.7 %collective-permute-start.21 = (f16[2,256,1152]{2,1,0:T(8,128)(2,1)}, f16[2,256,1152]{2,1,0:T(8,128)(2,1)}, u32[]{:S(2)}, u32[]{:S(2)}) collective-permute-start(f16[2,256,1152]{2,1,0:T(8,128)(2,1)} %fusion.43), channel_id=1, source_target_pairs={{0,8},{8,0},{16,24},{24,16},{1,9},{9,1},{17,25},{25,17},{2,10},{10... | collective-permute-start | bytes 3538952 | tf_op jit(solution)/shard_map/ppermute | solution.py:732
  691.4 50.0 %collective-permute-start.25 = (f16[2,256,1152]{2,1,0:T(8,128)(2,1)}, f16[2,256,1152]{2,1,0:T(8,128)(2,1)}, u32[]{:S(2)}, u32[]{:S(2)}) collective-permute-start(f16[2,256,1152]{2,1,0:T(8,128)(2,1)} %fusion.42), channel_id=1, source_target_pairs={{0,16},{8,24},{16,0},{24,8},{1,17},{9,25},{17,1},{25,9},{2,18},{10... | collective-permute-start | bytes 3538952 | tf_op jit(solution)/shard_map/ppermute | solution.py:732
  739.2 58.5 %collective-permute-start.33 = (f16[64,2048]{1,0:T(8,128)(2,1)}, f16[64,2048]{1,0:T(8,128)(2,1)}, u32[]{:S(2)}, u32[]{:S(2)}) collective-permute-start(f16[64,2048]{1,0:T(8,128)(2,1)} %get-tuple-element.273), channel_id=1, source_target_pairs={{0,8},{8,0},{16,24},{24,16},{1,9},{9,1},{17,25},{25,17},{2,10},{10... | collective-permute-start | bytes 786440 | tf_op jit(solution)/shard_map/ppermute | solution.py:732
  763.2 35.0 %collective-permute-start.39 = (f16[64,2048]{1,0:T(8,128)(2,1)S(1)}, f16[64,2048]{1,0:T(8,128)(2,1)}, u32[]{:S(2)}, u32[]{:S(2)}) collective-permute-start(f16[64,2048]{1,0:T(8,128)(2,1)S(1)} %fusion.70), channel_id=1, source_target_pairs={{0,16},{8,24},{16,0},{24,8},{1,17},{9,25},{17,1},{25,9},{2,18},{10... | collective-permute-start | bytes 786440 | tf_op jit(solution)/shard_map/ppermute | solution.py:732
  765.3 61.5 %collective-permute-start.23 = (f16[256,1152]{1,0:T(8,128)(2,1)}, f16[256,1152]{1,0:T(8,128)(2,1)}, u32[]{:S(2)}, u32[]{:S(2)}) collective-permute-start(f16[256,1152]{1,0:T(8,128)(2,1)} %get-tuple-element.275), channel_id=1, source_target_pairs={{0,8},{8,0},{16,24},{24,16},{1,9},{9,1},{17,25},{25,17},{2,10},{10... | collective-permute-start | bytes 1769480 | tf_op jit(solution)/shard_map/ppermute | solution.py:732
  799.6 28.9 %collective-permute-start.29 = (f16[256,1152]{1,0:T(8,128)(2,1)}, f16[256,1152]{1,0:T(8,128)(2,1)}, u32[]{:S(2)}, u32[]{:S(2)}) collective-permute-start(f16[256,1152]{1,0:T(8,128)(2,1)} %fusion.45), channel_id=1, source_target_pairs={{0,16},{8,24},{16,0},{24,8},{1,17},{9,25},{17,1},{25,9},{2,18},{10... | collective-permute-start | bytes 1769480 | tf_op jit(solution)/shard_map/ppermute | solution.py:732
  799.9 60.6 %collective-permute-start.15 = (f16[256,4096]{1,0:T(8,128)(2,1)}, f16[256,4096]{1,0:T(8,128)(2,1)}, u32[]{:S(2)}, u32[]{:S(2)}) collective-permute-start(f16[256,4096]{1,0:T(8,128)(2,1)} %get-tuple-element.197), channel_id=1, source_target_pairs={{0,2},{1,3},{2,4},{3,5},{4,6},{5,7},{8,10},{9,11},{10,12},{11,13},... | collective-permute-start | bytes 6291464 | tf_op jit(solution)/shard_map/ppermute | solution.py:702
  826.9 38.0 %collective-permute-start.16 = (f16[256,4096]{1,0:T(8,128)(2,1)}, f16[256,4096]{1,0:T(8,128)(2,1)}, u32[]{:S(2)}, u32[]{:S(2)}) collective-permute-start(f16[256,4096]{1,0:T(8,128)(2,1)} %get-tuple-element.198), channel_id=1, source_target_pairs={{2,0},{3,1},{4,2},{5,3},{6,4},{7,5},{10,8},{11,9},{12,10},{13,11},... | collective-permute-start | bytes 6291464 | tf_op jit(solution)/shard_map/ppermute | solution.py:702
  (67 other events, 1156.6 us)
Sparse Core Ops, SparseCore 0:
  9.6 160.2 all-gather.4
  171.5 163.3 all-gather.6
  695.3 26.7 all-gather.8

commit v5 on v4

--- a/solution.py
+++ b/solution.py
@@ -883,15 +883,17 @@
     shared.pack(1)
     top_proj = after(top_proj, *shared.out)
     shared.send(1)
+    shared.hold(top_proj)
+    shared.pack(2)
+    normal.hold(top_proj, *shared.out)
+    shared.send(2)
+    normal.pack(1)
+    top_proj = after(top_proj, *normal.out)
     tops = jnp.stack([top_proj, top_wout])
     tops = jnp.broadcast_to(jnp.repeat(tops * 1.01 + 1e-30, 8)[:, None], (16, L))
     wide = pg.reshape(8 * width // L, L)
     small = sum_small(jnp.concatenate([tops, sg, hg, wide], axis=0), "rows", 4)
 
-    normal.hold(small)
-    normal.pack(1)
-    small = after(small, *normal.out)
-    shared.hold(*normal.out)
     mixed.hold(*normal.out)
     normal.send(1)
     top_proj, top_wout, sg, hg = small[0, 0], small[8, 0], small[16:24], small[24:32]
@@ -900,7 +902,7 @@
     for k in range(sum_proj.bits):
         sum_proj.reduce(k)
         sum_wout.reduce(k)
-    shared.rest(2)
+    shared.rest(3)
     low_shared = lax.all_gather(shared.total().astype(bf16), "heads", axis=0, tiled=True)
     mixed.rest(3)
     output_t = (source_t + mixed.total()).astype(bf16)

time: 907 us -> 918 us (1.012)
  waiting for transfers between devices: 207 us -> 219 us
  transfers between devices with their start and end apart: 44 -> 44, of which waited for: 14 -> 16; matrix products, arithmetic and copies ran while one was open for 22% -> 22% of each run, Pallas kernels for 27% -> 27%
where the time goes in v5:
time: 918 us; the launch traced here: 911 us
  Pallas kernels  263 us (29%)
  waiting for transfers between devices  219 us (24%)
  other arithmetic  101 us (11%)
  matrix products  98.4 us (11%)
  starting transfers between devices  86.5 us (9%)
  local copies, waits for them, and re-layouts  75.9 us (8%)
  blocking collectives  48.5 us (5%)
  between operations  18.6 us (2%)
    pallas_call x1, Pallas kernels, run_bwd(): pl.pallas_call(functools.partial(bwd_kernel, float(inner_total)), grid=(b...  88.9 us
    all_gather x1, waiting for transfers between devices, per_device(): hidden_all = lax.all_gather(hidden_in, 'heads', axis=1, tiled=True)  87.4 us
    pallas_call x1, Pallas kernels, run_fwd(): pl.pallas_call(fwd_kernel, grid=(tokens // LB,), in_specs=[smem_spec(), r...  80.7 us
    pallas_call x6, Pallas kernels, sum_small(): pl.pallas_call(functools.partial(exchange_kernel, axis), out_shape=jax.Sh...  59.5 us
    ppermute x20, waiting for transfers between devices, move(): return lax.ppermute(x, 'rows', [(i, i ^ 1 << bit) for i in range(self.n)])  51.9 us
    convert_element_type x6, other arithmetic, pack(): self.out[way] = total.astype(self.kind)  51.2 us
    ppermute x18, starting transfers between devices, send(): self.moving[way] = lax.ppermute(out[way], 'heads', pairs)  49 us
    unnamed x111, local copies, waits for them, and re-layouts  47.5 us
  transfers between devices with their start and end apart: 44, of which 16 were waited for; matrix products, arithmetic and copies ran while one was open for 22% of the time, Pallas kernels for 27%

profile of v5, /device:TPU:0, one launch (start us, length us, event | category | flops | bytes accessed | tf_op | source)
XLA Modules:
  0.0 911.2 jit_solution(12857090808280978672)
XLA Ops:
  31.6 14.4 %all-gather = f32[8,1,256]{2,1,0:T(1,128)} all-gather(f32[1,1,256]{2,1,0:T(1,128)S(1)} %bitcast.366), channel_id=1, replica_groups=mesh['rows'=4,'heads'=8] {'heads'}, dimensions={0}, use_global_device_ids=true | all-gather | bytes 9216 | tf_op jit(solution)/shard_map/all_gather | solution.py:784
  47.4 34.1 %all_gather.17 = bf16[128,2048]{0,1:T(8,128)(2,1)S(1)} all-gather(bf16[128,256]{0,1:T(8,128)(2,1)S(1)} %copy.95), channel_id=1, replica_groups=mesh['rows'=4,'heads'=8] {'heads'}, dimensions={1}, use_global_device_ids=true | all-gather | bytes 589824 | tf_op jit(solution)/shard_map/all_gather | solution.py:783
  82.5 87.4 %all-gather.5.cloned.1.call-done.h_ref = bf16[4096,2048]{1,0:T(8,128)(2,1)} async-done(((bf16[4096,256]{1,0:T(8,128)(2,1)}), bf16[4096,2048]{1,0:T(8,128)(2,1)}) %all-gather.5.cloned.1.call-update) | async-done | bytes 16777232 | tf_op jit(solution)/shard_map/all_gather | solution.py:782
  169.9 80.7 %mixer_fwd.1 = (bf16[4096,2048]{1,0:T(8,128)(2,1)}, f32[32,1,128]{2,1,0:T(1,128)}, f32[4096,512]{1,0:T(8,128)}, f32[4096,768]{1,0:T(8,128)}, f32[4096,512]{1,0:T...) custom-call(s32[1,4]{1,0:T(1,128)} %len_ref.5, ...), custom_call_target="tpu_custom_call" | custom-call | tf_op jit(solution)/shard_map/mixer_fwd/pallas_call | solution.py:452
  271.2 13.4 %collective-permute-start = (f16[4,256,4096]{2,1,0:T(8,128)(2,1)}, f16[4,256,4096]{2,1,0:T(8,128)(2,1)}, u32[]{:S(2)}, u32[]{:S(2)}) collective-permute-start(f16[4,256,4096]{2,1,0:T(8,128)(2,1)} %convolution_convert_fusion), channel_id=1, source_target_pairs={{0,1},{1,0},{2,3},{3,2},{4,5},{5,4},{6,7},{7,6},{8,9},{9,8},{10,11... | collective-permute-start | bytes 25165832 | tf_op jit(solution)/shard_map/ppermute | solution.py:676
  308.6 26.4 %all-gather.7.cloned.1.call-done.cot_ref = bf16[4096,2048]{1,0:T(8,128)(2,1)} async-done(((bf16[4096,256]{1,0:T(8,128)(2,1)}), bf16[4096,2048]{1,0:T(8,128)(2,1)}) %all-gather.7.cloned.1.call-update) | async-done | bytes 16777232 | tf_op jit(solution)/shard_map/all_gather | solution.py:785
  335.0 17.3 %mixer_mid.1 = (f32[4096,512]{1,0:T(8,128)}, f32[32,1,128]{2,1,0:T(1,128)}) custom-call(s32[1,4]{1,0:T(1,128)} %len_ref.5, bf16[4096,2048]{1,0:T(8,128)(2,1)} %all-gather.7.cloned.1.call-done.cot_ref, bf16[512,2048]{1,0:T(8,128)(2,1)} %w_ref.1, f32[4096,512]{1,0:T(8,128)} %get-tuple-element.136.gated_ref, f32[8,512]{1,0:T(8,128)} %concatenate.23.cp_ref), custom_call_target="tpu_custom_call" | custom-call | tf_op jit(solution)/shard_map/mixer_mid/pallas_call | solution.py:504
  352.3 16.1 %sum_small.7 = f32[32,128]{1,0:T(8,128)} custom-call(f32[32,128]{1,0:T(8,128)} %bitcast.363), custom_call_target="tpu_custom_call" | custom-call | tf_op jit(solution)/shard_map/sum_small/pallas_call | solution.py:631
  369.7 9.2 %fusion.25 = (f16[256,4096]{1,0:T(8,128)(2,1)S(1)}, f16[256,4096]{1,0:T(8,128)(2,1)}) fusion(f16[256,4096]{1,0:T(8,128)(2,1)} %collective-permute-done.2, f16[4,256,4096]{2,1,0:T(8,128)(2,1)} %collective-permute-done, s32[]{:T(128)S(6)} %min.47, f16[4,256,4096]{2,1,0:T(8,128)(2,1)} %copy-done.2, f16[256,4096]{1,0:T(8,128)(2,1)} %copy-done.12, s32[]{:T(128)S(6)} %min.44), kind=kLoop, calls=%fused_computation.50 | loop fusion | flops 12582912 | bytes 16777224 | tf_op jit(solution)/shard_map/convert_element_type | solution.py:690
  388.5 88.9 %mixer_bwd.1 = (bf16[4096,1152]{1,0:T(8,128)(2,1)}, f32[4096,128]{1,0:T(8,128)}, f32[32,1,128]{2,1,0:T(1,128)}, f32[32,1,128]{2,1,0:T(1,128)}, f32[8,512]{1,0:T(...) custom-call(s32[1,4]{1,0:T(1,128)} %len_ref.5, f32[4096,512]{1,0:T(8,128)} %get-tuple-element.149.gate_ref, ...), custom_call_target="tpu_custom_call" | custom-call | tf_op jit(solution)/shard_map/mixer_bwd/pallas_call | solution.py:537
  478.3 10.2 %fusion.24 = (f16[256,4096]{1,0:T(8,128)(2,1)}, f16[256,4096]{1,0:T(8,128)(2,1)}) fusion(f16[256,4096]{1,0:T(8,128)(2,1)} %collective-permute-done.4, f16[4,256,4096]{2,1,0:T(8,128)(2,1)} %collective-permute-done, s32[]{:T(128)S(6)} %min.48, f16[4,256,4096]{2,1,0:T(8,128)(2,1)} %copy-done.2, f16[256,4096]{1,0:T(8,128)(2,1)} %collective-permute-done.3, ...), kind=kLoop, calls=%fused_computation.48 | loop fusion | flops 12582912 | bytes 16777224 | tf_op jit(solution)/shard_map/convert_element_type | solution.py:690
  489.0 10.2 %sum_small.8 = f32[72,128]{1,0:T(8,128)} custom-call(f32[72,128]{1,0:T(8,128)} %pad_maximum_fusion.6.x_ref), custom_call_target="tpu_custom_call" | custom-call | tf_op jit(solution)/shard_map/sum_small/pallas_call | solution.py:631
  500.0 16.4 %multiply_convert_fusion = f16[4,256,4096]{2,1,0:T(8,128)(2,1)} fusion(bf16[4096,1152]{1,0:T(8,128)(2,1)} %get-tuple-element.174, f32[4096]{0:T(1024)S(1)} %get-tuple-element.318, bf16[1,256,1152]{2,1,0:T(8,128)(2,1)} %get-tuple-element.296, bf16[1,256,1152]{2,1,0:T(8,128)(2,1)} %get-tuple-element.295, bf16[1,256,1152]{2,1,0:T(8,128)(2,1)} %get-tuple-element.294, ...), kind=kOutput, calls=%fused_computation.9 | convolution fusion | flops 9675603968 | bytes 20201472 | tf_op jit(solution)/shard_map/dot_general | solution.py:821
  523.3 14.1 %multiply_convert_fusion.1 = f16[4,256,4096]{2,1,0:T(8,128)(2,1)S(1)} fusion(bf16[4096,1152]{1,0:T(8,128)(2,1)} %get-tuple-element.174, f32[4096]{0:T(1024)S(1)} %get-tuple-element.318, bf16[1,256,1152]{2,1,0:T(8,128)(2,1)} %get-tuple-element.299, bf16[1,256,1152]{2,1,0:T(8,128)(2,1)} %get-tuple-element.298, bf16[1,256,1152]{2,1,0:T(8,128)(2,1)} %get-tuple-element.297, ...), kind=kOutput, calls=%fused_computation.10 | convolution fusion | flops 9675603968 | bytes 20201472 | tf_op jit(solution)/shard_map/dot_general | solution.py:821
  537.4 28.7 %collective-permute-done.5 = f16[256,4096]{1,0:T(8,128)(2,1)S(1)} collective-permute-done((f16[256,4096]{1,0:T(8,128)(2,1)}, f16[256,4096]{1,0:T(8,128)(2,1)S(1)}, u32[]{:S(2)}, u32[]{:S(2)}) %collective-permute-start.5) | collective-permute-done | bytes 2097184 | tf_op jit(solution)/shard_map/ppermute | solution.py:702
  585.2 13.7 %abs_reduce_fusion.1 = (f32[]{:T(128)}, f32[512,2048]{1,0:T(8,128)S(1)}) fusion(bf16[4096,512]{1,0:T(8,128)(2,1)} %copy-done.9, bf16[4096,2048]{1,0:T(8,128)(2,1)} %all-gather.7.cloned.1.call-done.cot_ref), kind=kOutput, calls=%fused_computation.60 | convolution fusion | flops 8592031744 | bytes 25165828 | tf_op jit(solution)/shard_map/dot_general | solution.py:871
  601.3 26.3 %abs_reduce_fusion = (f32[]{:T(128)}, f32[2048,1152]{1,0:T(8,128)S(1)}) fusion(bf16[4096,2048]{1,0:T(8,128)(2,1)} %get-tuple-element.170, bf16[4096,1152]{1,0:T(8,128)(2,1)S(1)} %bitcast.373), kind=kOutput, calls=%fused_computation.16 | convolution fusion | flops 19332071424 | bytes 35651588 | tf_op jit(solution)/shard_map/dot_general | solution.py:878
  643.3 9.3 %collective-permute-start.19 = (f32[16,4096]{1,0:T(8,128)S(1)}, f32[16,4096]{1,0:T(8,128)S(1)}, u32[]{:S(2)}, u32[]{:S(2)}) collective-permute-start(f32[16,4096]{1,0:T(8,128)S(1)} %get-tuple-element.204), channel_id=1, source_target_pairs={{0,2},{1,3},{2,4},{3,5},{4,6},{5,7},{8,10},{9,11},{10,12},{11,13},... | collective-permute-start | bytes 786440 | tf_op jit(solution)/shard_map/ppermute | solution.py:702
  661.7 10.2 %fusion.22 = (f16[256,4096]{1,0:T(8,128)(2,1)}, f16[256,4096]{1,0:T(8,128)(2,1)}) fusion(f16[256,4096]{1,0:T(8,128)(2,1)} %collective-permute-done.9, f16[4,256,4096]{2,1,0:T(8,128)(2,1)} %collective-permute-done.7, s32[]{:T(128)S(6)} %min.47, f16[4,256,4096]{2,1,0:T(8,128)(2,1)} %copy-done.3, f16[256,4096]{1,0:T(8,128)(2,1)} %collective-permute-done.8, ...), kind=kLoop, calls=%fused_computation.44 | loop fusion | flops 12582912 | bytes 16777224 | tf_op jit(solution)/shard_map/convert_element_type | solution.py:690
  706.2 25.4 %collective-permute-done.31 = f16[2,64,2048]{2,1,0:T(8,128)(2,1)S(1)} collective-permute-done((f16[2,64,2048]{2,1,0:T(8,128)(2,1)}, f16[2,64,2048]{2,1,0:T(8,128)(2,1)S(1)}, u32[]{:S(2)}, u32[]{:S(2)}) %collective-permute-start.31) | collective-permute-done | bytes 524320 | tf_op jit(solution)/shard_map/ppermute | solution.py:732
  734.7 9.0 collective-permute-done.35
  798.1 11.6 %sum_small.11 = f32[256,128]{1,0:T(8,128)} custom-call(f32[256,128]{1,0:T(8,128)} %reshape.319.x_ref), custom_call_target="tpu_custom_call" | custom-call | tf_op jit(solution)/shard_map/sum_small/pallas_call | solution.py:631
  860.8 10.1 %place.2 = (f32[2048,2,512]{2,1,0:T(2,128)}, f32[2048,8]{1,0:T(8,128)}) custom-call(s32[1]{0:T(128)} %bitcast.77.me_ref, f32[2,4,256,1152]{3,2,1,0:T(8,128)} %bitcast.320), custom_call_target="tpu_custom_call" | custom-call | tf_op jit(solution)/shard_map/place/pallas_call | solution.py:412
  875.9 11.2 %fusion.14 = (f32[256]{0:T(256)}, f32[4096,256]{0,1:T(8,128)}, bf16[4096,256]{0,1:T(8,128)(2,1)}) fusion(bf16[256,4096]{1,0:T(8,128)(2,1)S(1)} %bitcast.338, f32[4096]{0:T(1024)S(1)} %bitcast.359, f32[4096]{0:T(1024)S(1)} %fusion.83, f32[256]{0:T(256)S(1)} %copy-done.28, bf16[256,4096]{1,0:T(8,128)(2,1)} %bitcast.339, ...), kind=kOutput, calls=%fused_computation.32 | convolution fusion | flops 297795328 | bytes 28428292 | tf_op jit(solution)/shard_map/dot_general | solution.py:926
  (291 shorter events, 298.0 us)
Async XLA Ops:
  7.2 162.7 %all-gather.5.cloned.1.call-start = ((), (), s32[]{:S(2)}) async-start(), calls=%async_computation | async-start | bytes 18874368 | tf_op jit(solution)/shard_map/all_gather | solution.py:782
  7.9 327.1 %all-gather.7.cloned.1.call-start = ((), (), s32[]{:S(2)}) async-start(), calls=%async_computation.1 | async-start | bytes 18874368 | tf_op jit(solution)/shard_map/all_gather | solution.py:785
  8.7 779.1 %all-gather.9.cloned.1.call-start = ((), (), s32[]{:S(2)}) async-start(), calls=%async_computation.2 | async-start | bytes 1179648 | tf_op jit(solution)/shard_map/all_gather | solution.py:906
  304.7 63.7 %collective-permute-start.1 = (f16[256,4096]{1,0:T(8,128)(2,1)}, f16[256,4096]{1,0:T(8,128)(2,1)S(1)}, u32[]{:S(2)}, u32[]{:S(2)}) collective-permute-start(f16[256,4096]{1,0:T(8,128)(2,1)} %get-tuple-element.138), channel_id=1, source_target_pairs={{0,2},{1,3},{8,10},{9,11},{16,18},{17,19},{24,26},{25,27}} | collective-permute-start | bytes 6291464 | tf_op jit(solution)/shard_map/ppermute | solution.py:702
  306.1 63.5 %collective-permute-start.2 = (f16[256,4096]{1,0:T(8,128)(2,1)}, f16[256,4096]{1,0:T(8,128)(2,1)}, u32[]{:S(2)}, u32[]{:S(2)}) collective-permute-start(f16[256,4096]{1,0:T(8,128)(2,1)} %get-tuple-element.139), channel_id=1, source_target_pairs={{6,4},{7,5},{14,12},{15,13},{22,20},{23,21},{30,28},{31,29}} | collective-permute-start | bytes 6291464 | tf_op jit(solution)/shard_map/ppermute | solution.py:702
  378.9 99.3 %collective-permute-start.3 = (f16[256,4096]{1,0:T(8,128)(2,1)}, f16[256,4096]{1,0:T(8,128)(2,1)}, u32[]{:S(2)}, u32[]{:S(2)}) collective-permute-start(f16[256,4096]{1,0:T(8,128)(2,1)} %get-tuple-element.146), channel_id=1, source_target_pairs={{0,2},{1,3},{2,4},{3,5},{8,10},{9,11},{10,12},{11,13},{16,18},{17,... | collective-permute-start | bytes 6291464 | tf_op jit(solution)/shard_map/ppermute | solution.py:702
  383.0 95.3 %collective-permute-start.4 = (f16[256,4096]{1,0:T(8,128)(2,1)S(1)}, f16[256,4096]{1,0:T(8,128)(2,1)}, u32[]{:S(2)}, u32[]{:S(2)}) collective-permute-start(f16[256,4096]{1,0:T(8,128)(2,1)S(1)} %get-tuple-element.147), channel_id=1, source_target_pairs={{4,2},{5,3},{6,4},{7,5},{12,10},{13,11},{14,12},{15,13},{20,18},{2... | collective-permute-start | bytes 6291464 | tf_op jit(solution)/shard_map/ppermute | solution.py:702
  516.4 54.0 %collective-permute-start.7 = (f16[4,256,4096]{2,1,0:T(8,128)(2,1)}, f16[4,256,4096]{2,1,0:T(8,128)(2,1)}, u32[]{:S(2)}, u32[]{:S(2)}) collective-permute-start(f16[4,256,4096]{2,1,0:T(8,128)(2,1)} %multiply_convert_fusion), channel_id=1, source_target_pairs={{0,1},{1,0},{2,3},{3,2},{4,5},{5,4},{6,7},{7,6},{8,9},{9,8},{10,11... | collective-permute-start | bytes 25165832 | tf_op jit(solution)/shard_map/ppermute | solution.py:676
  517.0 49.1 %collective-permute-start.5 = (f16[256,4096]{1,0:T(8,128)(2,1)}, f16[256,4096]{1,0:T(8,128)(2,1)S(1)}, u32[]{:S(2)}, u32[]{:S(2)}) collective-permute-start(f16[256,4096]{1,0:T(8,128)(2,1)} %get-tuple-element.159), channel_id=1, source_target_pairs={{0,2},{1,3},{2,4},{3,5},{4,6},{5,7},{8,10},{9,11},{10,12},{11,13},... | collective-permute-start | bytes 6291464 | tf_op jit(solution)/shard_map/ppermute | solution.py:702
  520.6 49.8 %collective-permute-start.6 = (f16[256,4096]{1,0:T(8,128)(2,1)}, f16[256,4096]{1,0:T(8,128)(2,1)}, u32[]{:S(2)}, u32[]{:S(2)}) collective-permute-start(f16[256,4096]{1,0:T(8,128)(2,1)} %get-tuple-element.160), channel_id=1, source_target_pairs={{2,0},{3,1},{4,2},{5,3},{6,4},{7,5},{10,8},{11,9},{12,10},{13,11},... | collective-permute-start | bytes 6291464 | tf_op jit(solution)/shard_map/ppermute | solution.py:702
  578.8 82.9 %collective-permute-start.8 = (f16[256,4096]{1,0:T(8,128)(2,1)}, f16[256,4096]{1,0:T(8,128)(2,1)}, u32[]{:S(2)}, u32[]{:S(2)}) collective-permute-start(f16[256,4096]{1,0:T(8,128)(2,1)} %get-tuple-element.167), channel_id=1, source_target_pairs={{0,2},{1,3},{8,10},{9,11},{16,18},{17,19},{24,26},{25,27}} | collective-permute-start | bytes 6291464 | tf_op jit(solution)/shard_map/ppermute | solution.py:702
  583.3 78.4 %collective-permute-start.9 = (f16[256,4096]{1,0:T(8,128)(2,1)}, f16[256,4096]{1,0:T(8,128)(2,1)}, u32[]{:S(2)}, u32[]{:S(2)}) collective-permute-start(f16[256,4096]{1,0:T(8,128)(2,1)} %get-tuple-element.168), channel_id=1, source_target_pairs={{6,4},{7,5},{14,12},{15,13},{22,20},{23,21},{30,28},{31,29}} | collective-permute-start | bytes 6291464 | tf_op jit(solution)/shard_map/ppermute | solution.py:702
  599.0 34.3 %collective-permute-start.11 = (f32[16,4096]{1,0:T(8,128)S(1)}, f32[16,4096]{1,0:T(8,128)S(1)}, u32[]{:S(2)}, u32[]{:S(2)}) collective-permute-start(f32[16,4096]{1,0:T(8,128)S(1)} %get-tuple-element.175), channel_id=1, source_target_pairs={{0,2},{1,3},{8,10},{9,11},{16,18},{17,19},{24,26},{25,27}} | collective-permute-start | bytes 786440 | tf_op jit(solution)/shard_map/ppermute | solution.py:702
  600.4 33.0 %collective-permute-start.12 = (f32[16,4096]{1,0:T(8,128)S(1)}, f32[16,4096]{1,0:T(8,128)S(1)}, u32[]{:S(2)}, u32[]{:S(2)}) collective-permute-start(f32[16,4096]{1,0:T(8,128)S(1)} %get-tuple-element.176), channel_id=1, source_target_pairs={{6,4},{7,5},{14,12},{15,13},{22,20},{23,21},{30,28},{31,29}} | collective-permute-start | bytes 786440 | tf_op jit(solution)/shard_map/ppermute | solution.py:702
  687.1 90.2 %collective-permute-start.15 = (f16[256,4096]{1,0:T(8,128)(2,1)}, f16[256,4096]{1,0:T(8,128)(2,1)}, u32[]{:S(2)}, u32[]{:S(2)}) collective-permute-start(f16[256,4096]{1,0:T(8,128)(2,1)} %get-tuple-element.196), channel_id=1, source_target_pairs={{0,2},{1,3},{2,4},{3,5},{8,10},{9,11},{10,12},{11,13},{16,18},{17,... | collective-permute-start | bytes 6291464 | tf_op jit(solution)/shard_map/ppermute | solution.py:702
  690.4 88.2 %collective-permute-start.16 = (f16[256,4096]{1,0:T(8,128)(2,1)}, f16[256,4096]{1,0:T(8,128)(2,1)}, u32[]{:S(2)}, u32[]{:S(2)}) collective-permute-start(f16[256,4096]{1,0:T(8,128)(2,1)} %get-tuple-element.197), channel_id=1, source_target_pairs={{4,2},{5,3},{6,4},{7,5},{12,10},{13,11},{14,12},{15,13},{20,18},{2... | collective-permute-start | bytes 6291464 | tf_op jit(solution)/shard_map/ppermute | solution.py:702
  695.7 56.8 %collective-permute-start.21 = (f16[2,256,1152]{2,1,0:T(8,128)(2,1)}, f16[2,256,1152]{2,1,0:T(8,128)(2,1)}, u32[]{:S(2)}, u32[]{:S(2)}) collective-permute-start(f16[2,256,1152]{2,1,0:T(8,128)(2,1)} %fusion.43), channel_id=1, source_target_pairs={{0,8},{8,0},{16,24},{24,16},{1,9},{9,1},{17,25},{25,17},{2,10},{10... | collective-permute-start | bytes 3538952 | tf_op jit(solution)/shard_map/ppermute | solution.py:732
  699.3 32.3 %collective-permute-start.31 = (f16[2,64,2048]{2,1,0:T(8,128)(2,1)}, f16[2,64,2048]{2,1,0:T(8,128)(2,1)S(1)}, u32[]{:S(2)}, u32[]{:S(2)}) collective-permute-start(f16[2,64,2048]{2,1,0:T(8,128)(2,1)} %fusion.68), channel_id=1, source_target_pairs={{0,8},{8,0},{16,24},{24,16},{1,9},{9,1},{17,25},{25,17},{2,10},{10... | collective-permute-start | bytes 1572872 | tf_op jit(solution)/shard_map/ppermute | solution.py:732
  702.8 52.0 %collective-permute-start.25 = (f16[2,256,1152]{2,1,0:T(8,128)(2,1)}, f16[2,256,1152]{2,1,0:T(8,128)(2,1)}, u32[]{:S(2)}, u32[]{:S(2)}) collective-permute-start(f16[2,256,1152]{2,1,0:T(8,128)(2,1)} %fusion.42), channel_id=1, source_target_pairs={{0,16},{8,24},{16,0},{24,8},{1,17},{9,25},{17,1},{25,9},{2,18},{10... | collective-permute-start | bytes 3538952 | tf_op jit(solution)/shard_map/ppermute | solution.py:732
  752.5 58.9 %collective-permute-start.33 = (f16[64,2048]{1,0:T(8,128)(2,1)}, f16[64,2048]{1,0:T(8,128)(2,1)}, u32[]{:S(2)}, u32[]{:S(2)}) collective-permute-start(f16[64,2048]{1,0:T(8,128)(2,1)} %get-tuple-element.273), channel_id=1, source_target_pairs={{0,8},{8,0},{16,24},{24,16},{1,9},{9,1},{17,25},{25,17},{2,10},{10... | collective-permute-start | bytes 786440 | tf_op jit(solution)/shard_map/ppermute | solution.py:732
  777.3 34.8 %collective-permute-start.39 = (f16[64,2048]{1,0:T(8,128)(2,1)S(1)}, f16[64,2048]{1,0:T(8,128)(2,1)}, u32[]{:S(2)}, u32[]{:S(2)}) collective-permute-start(f16[64,2048]{1,0:T(8,128)(2,1)S(1)} %fusion.70), channel_id=1, source_target_pairs={{0,16},{8,24},{16,0},{24,8},{1,17},{9,25},{17,1},{25,9},{2,18},{10... | collective-permute-start | bytes 786440 | tf_op jit(solution)/shard_map/ppermute | solution.py:732
  778.7 62.1 %collective-permute-start.23 = (f16[256,1152]{1,0:T(8,128)(2,1)}, f16[256,1152]{1,0:T(8,128)(2,1)}, u32[]{:S(2)}, u32[]{:S(2)}) collective-permute-start(f16[256,1152]{1,0:T(8,128)(2,1)} %get-tuple-element.275), channel_id=1, source_target_pairs={{0,8},{8,0},{16,24},{24,16},{1,9},{9,1},{17,25},{25,17},{2,10},{10... | collective-permute-start | bytes 1769480 | tf_op jit(solution)/shard_map/ppermute | solution.py:732
  814.2 58.9 %collective-permute-start.17 = (f16[256,4096]{1,0:T(8,128)(2,1)}, f16[256,4096]{1,0:T(8,128)(2,1)}, u32[]{:S(2)}, u32[]{:S(2)}) collective-permute-start(f16[256,4096]{1,0:T(8,128)(2,1)} %get-tuple-element.200), channel_id=1, source_target_pairs={{0,2},{1,3},{2,4},{3,5},{4,6},{5,7},{8,10},{9,11},{10,12},{11,13},... | collective-permute-start | bytes 6291464 | tf_op jit(solution)/shard_map/ppermute | solution.py:702
  840.8 35.2 %collective-permute-start.18 = (f16[256,4096]{1,0:T(8,128)(2,1)}, f16[256,4096]{1,0:T(8,128)(2,1)}, u32[]{:S(2)}, u32[]{:S(2)}) collective-permute-start(f16[256,4096]{1,0:T(8,128)(2,1)} %get-tuple-element.201), channel_id=1, source_target_pairs={{2,0},{3,1},{4,2},{5,3},{6,4},{7,5},{10,8},{11,9},{12,10},{13,11},... | collective-permute-start | bytes 6291464 | tf_op jit(solution)/shard_map/ppermute | solution.py:702
  (67 other events, 1078.8 us)
Sparse Core Ops, SparseCore 0:
  9.6 160.2 all-gather.4
  171.5 163.4 all-gather.6
  661.8 20.3 all-gather.8

commit v6 on v5

--- a/solution.py
+++ b/solution.py
@@ -879,14 +879,7 @@
         normed, low_late, (((0,), (0,)), ((), ())), preferred_element_type=f32
     )
     top_proj = jnp.max(jnp.abs(grad_proj))
-    shared.hold(top_proj)
-    shared.pack(1)
-    top_proj = after(top_proj, *shared.out)
-    shared.send(1)
-    shared.hold(top_proj)
-    shared.pack(2)
-    normal.hold(top_proj, *shared.out)
-    shared.send(2)
+    normal.hold(top_proj)
     normal.pack(1)
     top_proj = after(top_proj, *normal.out)
     tops = jnp.stack([top_proj, top_wout])
@@ -895,27 +888,32 @@
     small = sum_small(jnp.concatenate([tops, sg, hg, wide], axis=0), "rows", 4)
 
     mixed.hold(*normal.out)
+    shared.hold(small)
     normal.send(1)
+    shared.pack(1)
+    shared.send(1)
     top_proj, top_wout, sg, hg = small[0, 0], small[8, 0], small[16:24], small[24:32]
     pg = small[32:].reshape(8, width)
     sum_proj, sum_wout = RowSum(grad_proj, top_proj), RowSum(grad_wout, top_wout)
     for k in range(sum_proj.bits):
         sum_proj.reduce(k)
         sum_wout.reduce(k)
-    shared.rest(3)
-    low_shared = lax.all_gather(shared.total().astype(bf16), "heads", axis=0, tiled=True)
     mixed.rest(3)
     output_t = (source_t + mixed.total()).astype(bf16)
 
     normal.pack(2)
-    out = normal.out
+    out = list(normal.out)
+    shared.hold(*out)
+    shared.pack(2)
+    shared.send(2)
     normal.send(2)
     grad_proj, grad_step = place(
         sum_proj.spread(*out), unpack_kernel, [(full, 2, width), (full, heads)]
     )
     (grad_wout,) = place(sum_wout.spread(*out), place_kernel, [grad_wout.shape])
 
-    low_shared = after(low_shared, *out)
+    shared.rest(3)
+    low_shared = lax.all_gather(shared.total().astype(bf16), "heads", axis=0, tiled=True)
     shared_raw = rest[:, width : width + L]
     norm_dot = norm_dot + jnp.sum(low_shared.astype(f32) * shared_raw.T, axis=0)
     normed_t = (source_t * inv_rms[None, :] * norm_gain[:, None]).astype(bf16)

time: 918 us -> 919 us (level)
    ppermute x20, waiting for transfers between devices: 51.9 us -> 65.3 us  [move(): return lax.ppermute(x, 'rows', [(i, i ^ 1 << bit) for i in range(self.n)])]
    ppermute x18, waiting for transfers between devices: 46.5 us -> 36.1 us  [send(): self.moving[way] = lax.ppermute(out[way], 'heads', pairs)]
    unnamed x111 -> x119, local copies, waits for them, and re-layouts: 47.5 us -> 44.4 us
  transfers between devices with their start and end apart: 44 -> 44, of which waited for: 16 -> 12; matrix products, arithmetic and copies ran while one was open for 22% -> 20% of each run, Pallas kernels for 27% -> 26%
where the time goes in v6:
time: 919 us; the launch traced here: 913 us
  Pallas kernels  260 us (28%)
  waiting for transfers between devices  222 us (24%)
  matrix products  102 us (11%)
  other arithmetic  97 us (11%)
  starting transfers between devices  88.9 us (10%)
  local copies, waits for them, and re-layouts  76.1 us (8%)
  blocking collectives  48.5 us (5%)
  between operations  18.7 us (2%)
    pallas_call x1, Pallas kernels, run_bwd(): pl.pallas_call(functools.partial(bwd_kernel, float(inner_total)), grid=(b...  88.9 us
    all_gather x1, waiting for transfers between devices, per_device(): hidden_all = lax.all_gather(hidden_in, 'heads', axis=1, tiled=True)  87.4 us
    pallas_call x1, Pallas kernels, run_fwd(): pl.pallas_call(fwd_kernel, grid=(tokens // LB,), in_specs=[smem_spec(), r...  80.7 us
    ppermute x20, waiting for transfers between devices, move(): return lax.ppermute(x, 'rows', [(i, i ^ 1 << bit) for i in range(self.n)])  65.3 us
    pallas_call x6, Pallas kernels, sum_small(): pl.pallas_call(functools.partial(exchange_kernel, axis), out_shape=jax.Sh...  56.7 us
    ppermute x18, starting transfers between devices, send(): self.moving[way] = lax.ppermute(out[way], 'heads', pairs)  51 us
    convert_element_type x6, other arithmetic, pack(): self.out[way] = total.astype(self.kind)  48.4 us
    dot_general x4, matrix products, project(): lax.dot_general(w, v, (((axis,), (1,)), ((), ())), preferred_element_type...  44.5 us
  transfers between devices with their start and end apart: 44, of which 12 were waited for; matrix products, arithmetic and copies ran while one was open for 20% of the time, Pallas kernels for 26%

profile of v6, /device:TPU:0, one launch (start us, length us, event | category | flops | bytes accessed | tf_op | source)
XLA Modules:
  0.0 912.9 jit_solution(5013254596126392351)
XLA Ops:
  31.6 15.0 %all-gather = f32[8,1,256]{2,1,0:T(1,128)} all-gather(f32[1,1,256]{2,1,0:T(1,128)S(1)} %bitcast.368), channel_id=1, replica_groups=mesh['rows'=4,'heads'=8] {'heads'}, dimensions={0}, use_global_device_ids=true | all-gather | bytes 9216 | tf_op jit(solution)/shard_map/all_gather | solution.py:784
  48.0 33.4 %all_gather.17 = bf16[128,2048]{0,1:T(8,128)(2,1)S(1)} all-gather(bf16[128,256]{0,1:T(8,128)(2,1)S(1)} %copy.95), channel_id=1, replica_groups=mesh['rows'=4,'heads'=8] {'heads'}, dimensions={1}, use_global_device_ids=true | all-gather | bytes 589824 | tf_op jit(solution)/shard_map/all_gather | solution.py:783
  82.5 87.4 %all-gather.5.cloned.1.call-done.h_ref = bf16[4096,2048]{1,0:T(8,128)(2,1)} async-done(((bf16[4096,256]{1,0:T(8,128)(2,1)}), bf16[4096,2048]{1,0:T(8,128)(2,1)}) %all-gather.5.cloned.1.call-update) | async-done | bytes 16777232 | tf_op jit(solution)/shard_map/all_gather | solution.py:782
  169.9 80.7 %mixer_fwd.1 = (bf16[4096,2048]{1,0:T(8,128)(2,1)}, f32[32,1,128]{2,1,0:T(1,128)}, f32[4096,512]{1,0:T(8,128)}, f32[4096,768]{1,0:T(8,128)}, f32[4096,512]{1,0:T...) custom-call(s32[1,4]{1,0:T(1,128)} %len_ref.5, ...), custom_call_target="tpu_custom_call" | custom-call | tf_op jit(solution)/shard_map/mixer_fwd/pallas_call | solution.py:452
  250.6 8.9 sum_small.6
  271.4 13.4 %collective-permute-start = (f16[4,256,4096]{2,1,0:T(8,128)(2,1)}, f16[4,256,4096]{2,1,0:T(8,128)(2,1)}, u32[]{:S(2)}, u32[]{:S(2)}) collective-permute-start(f16[4,256,4096]{2,1,0:T(8,128)(2,1)} %convolution_convert_fusion), channel_id=1, source_target_pairs={{0,1},{1,0},{2,3},{3,2},{4,5},{5,4},{6,7},{7,6},{8,9},{9,8},{10,11... | collective-permute-start | bytes 25165832 | tf_op jit(solution)/shard_map/ppermute | solution.py:676
  308.8 26.1 %all-gather.7.cloned.1.call-done.cot_ref = bf16[4096,2048]{1,0:T(8,128)(2,1)} async-done(((bf16[4096,256]{1,0:T(8,128)(2,1)}), bf16[4096,2048]{1,0:T(8,128)(2,1)}) %all-gather.7.cloned.1.call-update) | async-done | bytes 16777232 | tf_op jit(solution)/shard_map/all_gather | solution.py:785
  334.9 17.3 %mixer_mid.1 = (f32[4096,512]{1,0:T(8,128)}, f32[32,1,128]{2,1,0:T(1,128)}) custom-call(s32[1,4]{1,0:T(1,128)} %len_ref.5, bf16[4096,2048]{1,0:T(8,128)(2,1)} %all-gather.7.cloned.1.call-done.cot_ref, bf16[512,2048]{1,0:T(8,128)(2,1)} %w_ref.1, f32[4096,512]{1,0:T(8,128)} %get-tuple-element.134.gated_ref, f32[8,512]{1,0:T(8,128)} %concatenate.23.cp_ref), custom_call_target="tpu_custom_call" | custom-call | tf_op jit(solution)/shard_map/mixer_mid/pallas_call | solution.py:504
  352.2 16.2 %sum_small.7 = f32[32,128]{1,0:T(8,128)} custom-call(f32[32,128]{1,0:T(8,128)} %bitcast.365), custom_call_target="tpu_custom_call" | custom-call | tf_op jit(solution)/shard_map/sum_small/pallas_call | solution.py:631
  369.7 9.2 %fusion.25 = (f16[256,4096]{1,0:T(8,128)(2,1)S(1)}, f16[256,4096]{1,0:T(8,128)(2,1)}) fusion(f16[256,4096]{1,0:T(8,128)(2,1)} %collective-permute-done.2, f16[4,256,4096]{2,1,0:T(8,128)(2,1)} %collective-permute-done, s32[]{:T(128)S(6)} %min.47, f16[4,256,4096]{2,1,0:T(8,128)(2,1)} %copy-done.2, f16[256,4096]{1,0:T(8,128)(2,1)} %copy-done.15, s32[]{:T(128)S(6)} %min.44), kind=kLoop, calls=%fused_computation.50 | loop fusion | flops 12582912 | bytes 16777224 | tf_op jit(solution)/shard_map/convert_element_type | solution.py:690
  388.5 88.9 %mixer_bwd.1 = (bf16[4096,1152]{1,0:T(8,128)(2,1)}, f32[4096,128]{1,0:T(8,128)}, f32[32,1,128]{2,1,0:T(1,128)}, f32[32,1,128]{2,1,0:T(1,128)}, f32[8,512]{1,0:T(...) custom-call(s32[1,4]{1,0:T(1,128)} %len_ref.5, f32[4096,512]{1,0:T(8,128)} %get-tuple-element.147.gate_ref, ...), custom_call_target="tpu_custom_call" | custom-call | tf_op jit(solution)/shard_map/mixer_bwd/pallas_call | solution.py:537
  478.2 10.1 %fusion.24 = (f16[256,4096]{1,0:T(8,128)(2,1)}, f16[256,4096]{1,0:T(8,128)(2,1)}) fusion(f16[256,4096]{1,0:T(8,128)(2,1)} %collective-permute-done.4, f16[4,256,4096]{2,1,0:T(8,128)(2,1)} %collective-permute-done, s32[]{:T(128)S(6)} %min.48, f16[4,256,4096]{2,1,0:T(8,128)(2,1)} %copy-done.2, f16[256,4096]{1,0:T(8,128)(2,1)} %collective-permute-done.3, ...), kind=kLoop, calls=%fused_computation.48 | loop fusion | flops 12582912 | bytes 16777224 | tf_op jit(solution)/shard_map/convert_element_type | solution.py:690
  489.0 10.2 %sum_small.8 = f32[72,128]{1,0:T(8,128)} custom-call(f32[72,128]{1,0:T(8,128)} %pad_maximum_fusion.6.x_ref), custom_call_target="tpu_custom_call" | custom-call | tf_op jit(solution)/shard_map/sum_small/pallas_call | solution.py:631
  499.9 16.4 %multiply_convert_fusion = f16[4,256,4096]{2,1,0:T(8,128)(2,1)} fusion(bf16[4096,1152]{1,0:T(8,128)(2,1)} %get-tuple-element.172, f32[4096]{0:T(1024)S(1)} %get-tuple-element.314, bf16[1,256,1152]{2,1,0:T(8,128)(2,1)} %get-tuple-element.292, bf16[1,256,1152]{2,1,0:T(8,128)(2,1)} %get-tuple-element.291, bf16[1,256,1152]{2,1,0:T(8,128)(2,1)} %get-tuple-element.290, ...), kind=kOutput, calls=%fused_computation.9 | convolution fusion | flops 9675603968 | bytes 20201472 | tf_op jit(solution)/shard_map/dot_general | solution.py:821
  523.2 14.1 %multiply_convert_fusion.1 = f16[4,256,4096]{2,1,0:T(8,128)(2,1)S(1)} fusion(bf16[4096,1152]{1,0:T(8,128)(2,1)} %get-tuple-element.172, f32[4096]{0:T(1024)S(1)} %get-tuple-element.314, bf16[1,256,1152]{2,1,0:T(8,128)(2,1)} %get-tuple-element.295, bf16[1,256,1152]{2,1,0:T(8,128)(2,1)} %get-tuple-element.294, bf16[1,256,1152]{2,1,0:T(8,128)(2,1)} %get-tuple-element.293, ...), kind=kOutput, calls=%fused_computation.10 | convolution fusion | flops 9675603968 | bytes 20201472 | tf_op jit(solution)/shard_map/dot_general | solution.py:821
  537.4 28.7 %collective-permute-done.5 = f16[256,4096]{1,0:T(8,128)(2,1)S(1)} collective-permute-done((f16[256,4096]{1,0:T(8,128)(2,1)}, f16[256,4096]{1,0:T(8,128)(2,1)S(1)}, u32[]{:S(2)}, u32[]{:S(2)}) %collective-permute-start.5) | collective-permute-done | bytes 2097184 | tf_op jit(solution)/shard_map/ppermute | solution.py:702
  581.9 13.8 %abs_reduce_fusion.1 = (f32[]{:T(128)}, f32[512,2048]{1,0:T(8,128)S(1)}) fusion(bf16[4096,512]{1,0:T(8,128)(2,1)} %copy-done.10, bf16[4096,2048]{1,0:T(8,128)(2,1)} %all-gather.7.cloned.1.call-done.cot_ref), kind=kOutput, calls=%fused_computation.60 | convolution fusion | flops 8592031744 | bytes 25165828 | tf_op jit(solution)/shard_map/dot_general | solution.py:871
  601.3 29.9 %abs_reduce_fusion = (f32[]{:T(128)}, f32[2048,1152]{1,0:T(8,128)}) fusion(bf16[4096,2048]{1,0:T(8,128)(2,1)} %get-tuple-element.168, bf16[4096,1152]{1,0:T(8,128)(2,1)} %get-tuple-element.172), kind=kOutput, calls=%fused_computation.16 | convolution fusion | flops 19332071424 | bytes 35651588 | tf_op jit(solution)/shard_map/dot_general | solution.py:878
  667.9 15.9 %collective-permute-start.11 = (f16[256,4096]{1,0:T(8,128)(2,1)}, f16[256,4096]{1,0:T(8,128)(2,1)}, u32[]{:S(2)}, u32[]{:S(2)}) collective-permute-start(f16[256,4096]{1,0:T(8,128)(2,1)} %get-tuple-element.181), channel_id=1, source_target_pairs={{0,2},{1,3},{2,4},{3,5},{8,10},{9,11},{10,12},{11,13},{16,18},{17,... | collective-permute-start | bytes 6291464 | tf_op jit(solution)/shard_map/ppermute | solution.py:702
  704.0 31.8 %collective-permute-done.35 = f16[2,64,2048]{2,1,0:T(8,128)(2,1)S(1)} collective-permute-done((f16[2,64,2048]{2,1,0:T(8,128)(2,1)S(1)}, f16[2,64,2048]{2,1,0:T(8,128)(2,1)S(1)}, u32[]{:S(2)}, u32[]{:S(2)}) %collective-permute-start.35) | collective-permute-done | bytes 524320 | tf_op jit(solution)/shard_map/ppermute | solution.py:732
  755.6 10.0 %collective-permute-done.22 = f16[256,1152]{1,0:T(8,128)(2,1)S(1)} collective-permute-done((f16[256,1152]{1,0:T(8,128)(2,1)S(1)}, f16[256,1152]{1,0:T(8,128)(2,1)S(1)}, u32[]{:S(2)}, u32[]{:S(2)}) %collective-permute-start.22) | collective-permute-done | bytes 589856 | tf_op jit(solution)/shard_map/ppermute | solution.py:732
  793.0 10.0 %collective-permute-done.38 = f16[64,2048]{1,0:T(8,128)(2,1)} collective-permute-done((f16[64,2048]{1,0:T(8,128)(2,1)}, f16[64,2048]{1,0:T(8,128)(2,1)}, u32[]{:S(2)}, u32[]{:S(2)}) %collective-permute-start.38) | collective-permute-done | bytes 262176 | tf_op jit(solution)/shard_map/ppermute | solution.py:732
  848.3 10.1 %place.2 = (f32[2048,2,512]{2,1,0:T(2,128)}, f32[2048,8]{1,0:T(8,128)}) custom-call(s32[1]{0:T(128)} %bitcast.79.me_ref, f32[2,4,256,1152]{3,2,1,0:T(8,128)} %bitcast.320), custom_call_target="tpu_custom_call" | custom-call | tf_op jit(solution)/shard_map/place/pallas_call | solution.py:412
  877.9 11.3 %fusion.14 = (f32[256]{0:T(256)}, f32[4096,256]{0,1:T(8,128)}, bf16[4096,256]{0,1:T(8,128)(2,1)}) fusion(bf16[256,4096]{1,0:T(8,128)(2,1)S(1)} %bitcast.340, f32[4096]{0:T(1024)S(1)} %bitcast.361, f32[4096]{0:T(1024)S(1)} %fusion.83, f32[256]{0:T(256)S(1)} %copy-done.33, bf16[256,4096]{1,0:T(8,128)(2,1)} %bitcast.341, ...), kind=kOutput, calls=%fused_computation.32 | convolution fusion | flops 297795328 | bytes 28428292 | tf_op jit(solution)/shard_map/dot_general | solution.py:924
  (299 shorter events, 285.3 us)
Async XLA Ops:
  7.2 162.7 %all-gather.5.cloned.1.call-start = ((), (), s32[]{:S(2)}) async-start(), calls=%async_computation | async-start | bytes 18874368 | tf_op jit(solution)/shard_map/all_gather | solution.py:782
  7.9 327.0 %all-gather.7.cloned.1.call-start = ((), (), s32[]{:S(2)}) async-start(), calls=%async_computation.1 | async-start | bytes 18874368 | tf_op jit(solution)/shard_map/all_gather | solution.py:785
  8.7 851.9 %all-gather.9.cloned.1.call-start = ((), (), s32[]{:S(2)}) async-start(), calls=%async_computation.2 | async-start | bytes 1179648 | tf_op jit(solution)/shard_map/all_gather | solution.py:916
  304.9 63.5 %collective-permute-start.1 = (f16[256,4096]{1,0:T(8,128)(2,1)}, f16[256,4096]{1,0:T(8,128)(2,1)S(1)}, u32[]{:S(2)}, u32[]{:S(2)}) collective-permute-start(f16[256,4096]{1,0:T(8,128)(2,1)} %get-tuple-element.136), channel_id=1, source_target_pairs={{0,2},{1,3},{8,10},{9,11},{16,18},{17,19},{24,26},{25,27}} | collective-permute-start | bytes 6291464 | tf_op jit(solution)/shard_map/ppermute | solution.py:702
  306.3 63.4 %collective-permute-start.2 = (f16[256,4096]{1,0:T(8,128)(2,1)}, f16[256,4096]{1,0:T(8,128)(2,1)}, u32[]{:S(2)}, u32[]{:S(2)}) collective-permute-start(f16[256,4096]{1,0:T(8,128)(2,1)} %get-tuple-element.137), channel_id=1, source_target_pairs={{6,4},{7,5},{14,12},{15,13},{22,20},{23,21},{30,28},{31,29}} | collective-permute-start | bytes 6291464 | tf_op jit(solution)/shard_map/ppermute | solution.py:702
  378.9 99.3 %collective-permute-start.3 = (f16[256,4096]{1,0:T(8,128)(2,1)}, f16[256,4096]{1,0:T(8,128)(2,1)}, u32[]{:S(2)}, u32[]{:S(2)}) collective-permute-start(f16[256,4096]{1,0:T(8,128)(2,1)} %get-tuple-element.144), channel_id=1, source_target_pairs={{0,2},{1,3},{2,4},{3,5},{8,10},{9,11},{10,12},{11,13},{16,18},{17,... | collective-permute-start | bytes 6291464 | tf_op jit(solution)/shard_map/ppermute | solution.py:702
  383.0 95.2 %collective-permute-start.4 = (f16[256,4096]{1,0:T(8,128)(2,1)S(1)}, f16[256,4096]{1,0:T(8,128)(2,1)}, u32[]{:S(2)}, u32[]{:S(2)}) collective-permute-start(f16[256,4096]{1,0:T(8,128)(2,1)S(1)} %get-tuple-element.145), channel_id=1, source_target_pairs={{4,2},{5,3},{6,4},{7,5},{12,10},{13,11},{14,12},{15,13},{20,18},{2... | collective-permute-start | bytes 6291464 | tf_op jit(solution)/shard_map/ppermute | solution.py:702
  516.4 54.0 %collective-permute-start.7 = (f16[4,256,4096]{2,1,0:T(8,128)(2,1)}, f16[4,256,4096]{2,1,0:T(8,128)(2,1)}, u32[]{:S(2)}, u32[]{:S(2)}) collective-permute-start(f16[4,256,4096]{2,1,0:T(8,128)(2,1)} %multiply_convert_fusion), channel_id=1, source_target_pairs={{0,1},{1,0},{2,3},{3,2},{4,5},{5,4},{6,7},{7,6},{8,9},{9,8},{10,11... | collective-permute-start | bytes 25165832 | tf_op jit(solution)/shard_map/ppermute | solution.py:676
  517.0 49.1 %collective-permute-start.5 = (f16[256,4096]{1,0:T(8,128)(2,1)}, f16[256,4096]{1,0:T(8,128)(2,1)S(1)}, u32[]{:S(2)}, u32[]{:S(2)}) collective-permute-start(f16[256,4096]{1,0:T(8,128)(2,1)} %get-tuple-element.157), channel_id=1, source_target_pairs={{0,2},{1,3},{2,4},{3,5},{4,6},{5,7},{8,10},{9,11},{10,12},{11,13},... | collective-permute-start | bytes 6291464 | tf_op jit(solution)/shard_map/ppermute | solution.py:702
  520.6 49.8 %collective-permute-start.6 = (f16[256,4096]{1,0:T(8,128)(2,1)}, f16[256,4096]{1,0:T(8,128)(2,1)}, u32[]{:S(2)}, u32[]{:S(2)}) collective-permute-start(f16[256,4096]{1,0:T(8,128)(2,1)} %get-tuple-element.158), channel_id=1, source_target_pairs={{2,0},{3,1},{4,2},{5,3},{6,4},{7,5},{10,8},{11,9},{12,10},{13,11},... | collective-permute-start | bytes 6291464 | tf_op jit(solution)/shard_map/ppermute | solution.py:702
  578.7 60.6 %collective-permute-start.8 = (f16[256,4096]{1,0:T(8,128)(2,1)}, f16[256,4096]{1,0:T(8,128)(2,1)S(1)}, u32[]{:S(2)}, u32[]{:S(2)}) collective-permute-start(f16[256,4096]{1,0:T(8,128)(2,1)} %get-tuple-element.165), channel_id=1, source_target_pairs={{0,2},{1,3},{8,10},{9,11},{16,18},{17,19},{24,26},{25,27}} | collective-permute-start | bytes 6291464 | tf_op jit(solution)/shard_map/ppermute | solution.py:702
  595.7 43.7 %collective-permute-start.9 = (f16[256,4096]{1,0:T(8,128)(2,1)S(1)}, f16[256,4096]{1,0:T(8,128)(2,1)S(1)}, u32[]{:S(2)}, u32[]{:S(2)}) collective-permute-start(f16[256,4096]{1,0:T(8,128)(2,1)S(1)} %copy-done.14), channel_id=1, source_target_pairs={{6,4},{7,5},{14,12},{15,13},{22,20},{23,21},{30,28},{31,29}} | collective-permute-start | bytes 6291464 | tf_op jit(solution)/shard_map/ppermute | solution.py:702
  598.8 40.5 %collective-permute-start.15 = (f32[16,4096]{1,0:T(8,128)S(1)}, f32[16,4096]{1,0:T(8,128)S(1)}, u32[]{:S(2)}, u32[]{:S(2)}) collective-permute-start(f32[16,4096]{1,0:T(8,128)S(1)} %get-tuple-element.189), channel_id=1, source_target_pairs={{0,2},{1,3},{8,10},{9,11},{16,18},{17,19},{24,26},{25,27}} | collective-permute-start | bytes 786440 | tf_op jit(solution)/shard_map/ppermute | solution.py:702
  600.4 38.9 %collective-permute-start.16 = (f32[16,4096]{1,0:T(8,128)S(1)}, f32[16,4096]{1,0:T(8,128)S(1)}, u32[]{:S(2)}, u32[]{:S(2)}) collective-permute-start(f32[16,4096]{1,0:T(8,128)S(1)} %get-tuple-element.190), channel_id=1, source_target_pairs={{6,4},{7,5},{14,12},{15,13},{22,20},{23,21},{30,28},{31,29}} | collective-permute-start | bytes 786440 | tf_op jit(solution)/shard_map/ppermute | solution.py:702
  665.2 32.5 %collective-permute-start.17 = (f32[16,4096]{1,0:T(8,128)}, f32[16,4096]{1,0:T(8,128)S(1)}, u32[]{:S(2)}, u32[]{:S(2)}) collective-permute-start(f32[16,4096]{1,0:T(8,128)} %get-tuple-element.199), channel_id=1, source_target_pairs={{0,2},{1,3},{2,4},{3,5},{8,10},{9,11},{10,12},{11,13},{16,18},{17,... | collective-permute-start | bytes 786440 | tf_op jit(solution)/shard_map/ppermute | solution.py:702
  667.9 99.4 %collective-permute-start.11 = (f16[256,4096]{1,0:T(8,128)(2,1)}, f16[256,4096]{1,0:T(8,128)(2,1)}, u32[]{:S(2)}, u32[]{:S(2)}) collective-permute-start(f16[256,4096]{1,0:T(8,128)(2,1)} %get-tuple-element.181), channel_id=1, source_target_pairs={{0,2},{1,3},{2,4},{3,5},{8,10},{9,11},{10,12},{11,13},{16,18},{17,... | collective-permute-start | bytes 6291464 | tf_op jit(solution)/shard_map/ppermute | solution.py:702
  683.8 85.1 %collective-permute-start.12 = (f16[256,4096]{1,0:T(8,128)(2,1)}, f16[256,4096]{1,0:T(8,128)(2,1)}, u32[]{:S(2)}, u32[]{:S(2)}) collective-permute-start(f16[256,4096]{1,0:T(8,128)(2,1)} %get-tuple-element.182), channel_id=1, source_target_pairs={{4,2},{5,3},{6,4},{7,5},{12,10},{13,11},{14,12},{15,13},{20,18},{2... | collective-permute-start | bytes 6291464 | tf_op jit(solution)/shard_map/ppermute | solution.py:702
  697.7 54.8 %collective-permute-start.21 = (f16[2,256,1152]{2,1,0:T(8,128)(2,1)S(1)}, f16[2,256,1152]{2,1,0:T(8,128)(2,1)S(1)}, u32[]{:S(2)}, u32[]{:S(2)}) collective-permute-start(f16[2,256,1152]{2,1,0:T(8,128)(2,1)S(1)} %copy-done.16), channel_id=1, source_target_pairs={{0,8},{8,0},{16,24},{24,16},{1,9},{9,1},{17,25},{25,17},{2,10},{10... | collective-permute-start | bytes 3538952 | tf_op jit(solution)/shard_map/ppermute | solution.py:732
  698.4 56.2 %collective-permute-start.25 = (f16[2,256,1152]{2,1,0:T(8,128)(2,1)S(1)}, f16[2,256,1152]{2,1,0:T(8,128)(2,1)S(1)}, u32[]{:S(2)}, u32[]{:S(2)}) collective-permute-start(f16[2,256,1152]{2,1,0:T(8,128)(2,1)S(1)} %fusion.42), channel_id=1, source_target_pairs={{0,16},{8,24},{16,0},{24,8},{1,17},{9,25},{17,1},{25,9},{2,18},{10... | collective-permute-start | bytes 3538952 | tf_op jit(solution)/shard_map/ppermute | solution.py:732
  702.3 33.5 %collective-permute-start.35 = (f16[2,64,2048]{2,1,0:T(8,128)(2,1)S(1)}, f16[2,64,2048]{2,1,0:T(8,128)(2,1)S(1)}, u32[]{:S(2)}, u32[]{:S(2)}) collective-permute-start(f16[2,64,2048]{2,1,0:T(8,128)(2,1)S(1)} %fusion.67), channel_id=1, source_target_pairs={{0,16},{8,24},{16,0},{24,8},{1,17},{9,25},{17,1},{25,9},{2,18},{10... | collective-permute-start | bytes 1572872 | tf_op jit(solution)/shard_map/ppermute | solution.py:732
  751.0 40.8 %collective-permute-start.33 = (f16[64,2048]{1,0:T(8,128)(2,1)}, f16[64,2048]{1,0:T(8,128)(2,1)}, u32[]{:S(2)}, u32[]{:S(2)}) collective-permute-start(f16[64,2048]{1,0:T(8,128)(2,1)} %get-tuple-element.269), channel_id=1, source_target_pairs={{0,8},{8,0},{16,24},{24,16},{1,9},{9,1},{17,25},{25,17},{2,10},{10... | collective-permute-start | bytes 786440 | tf_op jit(solution)/shard_map/ppermute | solution.py:732
  784.4 47.0 %collective-permute-start.23 = (f16[256,1152]{1,0:T(8,128)(2,1)}, f16[256,1152]{1,0:T(8,128)(2,1)}, u32[]{:S(2)}, u32[]{:S(2)}) collective-permute-start(f16[256,1152]{1,0:T(8,128)(2,1)} %get-tuple-element.271), channel_id=1, source_target_pairs={{0,8},{8,0},{16,24},{24,16},{1,9},{9,1},{17,25},{25,17},{2,10},{10... | collective-permute-start | bytes 1769480 | tf_op jit(solution)/shard_map/ppermute | solution.py:732
  804.4 73.5 %collective-permute-start.13 = (f16[256,4096]{1,0:T(8,128)(2,1)}, f16[256,4096]{1,0:T(8,128)(2,1)}, u32[]{:S(2)}, u32[]{:S(2)}) collective-permute-start(f16[256,4096]{1,0:T(8,128)(2,1)} %get-tuple-element.185), channel_id=1, source_target_pairs={{0,2},{1,3},{2,4},{3,5},{4,6},{5,7},{8,10},{9,11},{10,12},{11,13},... | collective-permute-start | bytes 6291464 | tf_op jit(solution)/shard_map/ppermute | solution.py:702
  831.4 46.5 %collective-permute-start.14 = (f16[256,4096]{1,0:T(8,128)(2,1)}, f16[256,4096]{1,0:T(8,128)(2,1)}, u32[]{:S(2)}, u32[]{:S(2)}) collective-permute-start(f16[256,4096]{1,0:T(8,128)(2,1)} %get-tuple-element.186), channel_id=1, source_target_pairs={{2,0},{3,1},{4,2},{5,3},{6,4},{7,5},{10,8},{11,9},{12,10},{13,11},... | collective-permute-start | bytes 6291464 | tf_op jit(solution)/shard_map/ppermute | solution.py:702
  (71 other events, 1361.0 us)
Sparse Core Ops, SparseCore 0:
  9.6 160.2 all-gather.4
  171.5 163.3 all-gather.6
  791.9 21.1 all-gather.8
